TPU v7x, 16 devices: a whole 2x2x2 slice. The times are simulated.
16 devices in a mesh: dp: 2 (over z), tp: 8 (over y, x, core).
Axes of the slice: x: 2, y: 2, z: 2, core: 2. Of those that a mesh axis runs over, the one named last changes fastest.
Arguments:
- hidden: bfloat16 [8192, 960], P('dp')
- w_final: float32 [960], replicated
- emb_table: bfloat16 [49152, 960], P('tp')
- teacher: bfloat16 [8192, 49152], P('dp', 'tp')
- tok_mask: float32 [8192], P('dp')
Outputs:
- output 1: float32 [], replicated
- output 2: bfloat16 [8192, 960], P('dp')
- output 3: float32 [960], replicated
- output 4: float32 [49152, 960], P('tp')
All inputs are finite; a program needn't handle non-finite values.
Results may differ from a plain program's by a relative error of at most 0.00108574.
Values sent between devices are 32-bit elements.
A program may use at most 1 GiB of HBM per device.

v0:
```python
import functools

import jax
import jax.numpy as jnp
from jax import lax
from jax.experimental import pallas as pl
from jax.experimental.pallas import tpu as pltpu
from jax.sharding import PartitionSpec as P


SOFT_CAP = 30.0
NORM_EPS = 1e-6
INV_CAP = 1.0 / SOFT_CAP
EXP_SCALE = SOFT_CAP * 1.4426950408889634
TOK = 512
LINES = TOK // 128
RUN = 16
STOK = 256
COL = 512
BACK = 512
GCOL = 256
CHUNKS = (256, 256, 512, 1024, 2048, 1536, 256, 256)
VMEM_LIMIT = 62 * 1024 * 1024
MESH = pl.DeviceIdType.MESH
NT = (((1,), (1,)), ((), ()))
NN = (((1,), (0,)), ((), ()))


def stats_kernel(mask_ref, gain_ref, hid_hbm, tab_hbm, tea_hbm, x_hbm, xt_hbm, out_ref,
                 hid_buf, x_buf, xt_buf, tab_buf, tea_buf, rows_ref, z0_ref, z1_ref, acc_ref, sum_ref, gain_buf, flag_buf,
                 flags, order, hid_sem, tab_sem, tea_sem, flag_sem, out_sem):
    z_refs = (z0_ref, z1_ref)
    dim, tokens = hid_hbm.shape
    count = tab_hbm.shape[1] // COL
    slabs = tokens // TOK
    runs = tokens // RUN
    per = STOK // RUN

    def hid_copy(i):
        cols = pl.ds(i * TOK, TOK)
        return pltpu.make_async_copy(hid_hbm.at[:, cols], hid_buf.at[:, cols], hid_sem.at[i])

    def tab_copy(i):
        cols = pl.ds(i * COL, COL)
        return pltpu.make_async_copy(tab_hbm.at[:, cols], tab_buf.at[:, cols], tab_sem)

    for i in range(slabs):
        hid_copy(i).start()
    for i in range(count):
        tab_copy(i).start()

    flag = mask_ref[...]
    for shift in (1, 2, 4, 8):
        flag = jnp.maximum(flag, pltpu.roll(flag, 128 - shift, 1))
    flag_buf[...] = (flag > 0).astype(jnp.int32)
    flag_copy = pltpu.make_async_copy(flag_buf, flags, flag_sem)
    flag_copy.start()
    gain_buf[...] = jnp.broadcast_to(1.0 + gain_ref[...], (128, dim)).T
    sum_ref[...] = jnp.ones_like(sum_ref)
    flag_copy.wait()

    def mark(r, found):
        order[found] = r
        return found + flags[lax.div(r, 128 // RUN), lax.rem(r, 128 // RUN) * RUN]

    found = lax.fori_loop(0, runs, mark, 0)
    last = order[jnp.maximum(found - 1, 0)]
    last = jnp.where(found > 0, last, 0)

    def fill(k, _):
        order[found + k] = last
        return 0

    lax.fori_loop(0, 2 * per, fill, 0)
    blocks = lax.div(found + per - 1, per)

    def tea_start(b):
        slot = lax.rem(b, 2)

        def one(k, _):
            src = pl.ds(pl.multiple_of(order[b * per + k] * RUN, RUN), RUN)
            dst = pl.ds(pl.multiple_of(k * RUN, RUN), RUN)
            pltpu.make_async_copy(tea_hbm.at[src, :], tea_buf.at[slot, dst, :], tea_sem.at[slot]).start()
            return 0

        lax.fori_loop(0, per, one, 0)

    def tea_wait(b):
        slot = lax.rem(b, 2)
        pltpu.make_async_copy(tea_hbm.at[pl.ds(0, STOK), :], tea_buf.at[slot], tea_sem.at[slot]).wait()

    @pl.when(blocks > 0)
    def _():
        tea_start(0)

    def slab(i, _):
        pltpu.make_async_copy(hid_hbm.at[:, pl.ds(0, TOK)], hid_buf.at[:, pl.ds(0, TOK)], hid_sem.at[i]).wait()
        for b in range(LINES):
            lanes = pl.ds(pl.multiple_of(i * TOK + b * 128, 128), 128)
            hid = hid_buf[:, lanes].astype(jnp.float32)
            inv_rms = lax.rsqrt(jnp.mean(hid * hid, axis=0, keepdims=True) + NORM_EPS)
            xb = (hid * inv_rms * gain_buf[...]).astype(jnp.bfloat16)
            xt_buf[:, lanes] = xb
            x_buf[lanes, :] = xb.T
        return 0

    lax.fori_loop(0, slabs, slab, 0)
    x_out = pltpu.make_async_copy(x_buf, x_hbm, out_sem.at[0])
    xt_out = pltpu.make_async_copy(xt_buf, xt_hbm, out_sem.at[1])
    x_out.start()
    xt_out.start()
    pltpu.make_async_copy(tab_hbm, tab_buf, tab_sem).wait()

    def gather(b):
        slot = lax.rem(b, 2)
        for k in range(per):
            src = pl.ds(pl.multiple_of(order[b * per + k] * RUN, RUN), RUN)
            rows_ref[slot, k * RUN:(k + 1) * RUN, :] = x_buf[src, :]

    def logits(b, n, par):
        cols = slice(n * COL, (n + 1) * COL)
        z_refs[par][...] = lax.dot_general(rows_ref[lax.rem(b, 2)], tab_buf[:, cols], NN, preferred_element_type=jnp.float32)

    def collect(b, n, par):
        slot = lax.rem(b, 2)
        for r in range(0, STOK, 64):
            rows = slice(r, r + 64)
            acc_s = jnp.zeros((64, 128), jnp.float32) if n == 0 else acc_ref[0, rows, :]
            acc_t = jnp.zeros((64, 128), jnp.float32) if n == 0 else acc_ref[1, rows, :]
            for q in range(COL // 128):
                zq = z_refs[par][rows, q * 128:(q + 1) * 128]
                tq = tea_buf[slot, rows, n * COL + q * 128:n * COL + (q + 1) * 128].astype(jnp.float32)
                acc_s += jnp.exp2(jnp.tanh(zq * INV_CAP) * EXP_SCALE)
                acc_t += jnp.exp2(jnp.tanh(tq * INV_CAP) * EXP_SCALE)
            acc_ref[0, rows, :] = acc_s
            acc_ref[1, rows, :] = acc_t

    @pl.when(blocks > 0)
    def _():
        gather(0)
        logits(0, 0, 0)

    def block(b, _):
        @pl.when(b + 1 < blocks)
        def _():
            tea_start(b + 1)

        tea_wait(b)
        gather(b + 1)
        for n in range(count):
            if n + 1 < count:
                logits(b, n + 1, (n + 1) % 2)
            else:
                logits(b + 1, 0, 0)
            collect(b, n, n % 2)
        for k in range(per):
            dst = pl.ds(pl.multiple_of(order[b * per + k] * RUN, RUN), RUN)
            for s in range(2):
                sum_ref[s, dst, :] = acc_ref[s, k * RUN:(k + 1) * RUN, :]
        return 0

    lax.fori_loop(0, blocks, block, 0)

    def lines(i, _):
        for s in range(2):
            for b in range(8):
                rows = pl.ds(pl.multiple_of((i * 8 + b) * 128, 128), 128)
                out_ref[s * (tokens // 128) + i * 8 + b, :] = jnp.sum(sum_ref[s, rows, :].T, axis=0)
        return 0

    lax.fori_loop(0, tokens // 1024, lines, 0)
    x_out.wait()
    xt_out.wait()


def stats_call(mask_lines, gain_row, hid_t, tab_t, tea_rows):
    dim, tokens = hid_t.shape
    cols = tab_t.shape[1]
    assert (cols // COL) % 2 == 0
    hbm = pl.BlockSpec(memory_space=pl.ANY)
    vmem = pl.BlockSpec(memory_space=pltpu.VMEM)
    per = STOK // RUN
    return pl.pallas_call(
        stats_kernel,
        in_specs=[vmem, vmem, hbm, hbm, hbm],
        out_specs=[hbm, hbm, vmem],
        out_shape=[
            jax.ShapeDtypeStruct((tokens, dim), jnp.bfloat16),
            jax.ShapeDtypeStruct((dim, tokens), jnp.bfloat16),
            jax.ShapeDtypeStruct((tokens // 64, 128), jnp.float32),
        ],
        scratch_shapes=[
            pltpu.VMEM((dim, tokens), jnp.bfloat16),
            pltpu.VMEM((tokens, dim), jnp.bfloat16),
            pltpu.VMEM((dim, tokens), jnp.bfloat16),
            pltpu.VMEM((dim, cols), jnp.bfloat16),
            pltpu.VMEM((2, STOK, cols), jnp.bfloat16),
            pltpu.VMEM((2, STOK, dim), jnp.bfloat16),
            pltpu.VMEM((STOK, COL), jnp.float32),
            pltpu.VMEM((STOK, COL), jnp.float32),
            pltpu.VMEM((2, STOK, 128), jnp.float32),
            pltpu.VMEM((2, tokens, 128), jnp.float32),
            pltpu.VMEM((dim, 128), jnp.float32),
            pltpu.VMEM((tokens // 128, 128), jnp.int32),
            pltpu.SMEM((tokens // 128, 128), jnp.int32),
            pltpu.SMEM((tokens // RUN + 2 * per,), jnp.int32),
            pltpu.SemaphoreType.DMA((tokens // TOK,)),
            pltpu.SemaphoreType.DMA,
            pltpu.SemaphoreType.DMA((2,)),
            pltpu.SemaphoreType.DMA,
            pltpu.SemaphoreType.DMA((2,)),
        ],
        compiler_params=pltpu.CompilerParams(vmem_limit_bytes=VMEM_LIMIT),
        cost_estimate=pl.CostEstimate(flops=2 * tokens * cols * dim, bytes_accessed=2 * tokens * cols, transcendentals=0),
        name="stats",
    )(mask_lines, gain_row, hid_t, tab_t, tea_rows)


def exchange_kernel(tp, stats_ref, mask_ref, ab_ref, log_ref, slots, mask_slot, send_sem, recv_sem, msend_sem, mrecv_sem):
    dp_me = lax.axis_index("dp")
    me = lax.axis_index("tp")
    barrier = pltpu.get_barrier_semaphore()
    for d in range(1, tp):
        pl.semaphore_signal(barrier, inc=1, device_id=(dp_me, lax.rem(me + d, tp)), device_id_type=MESH)
    pl.semaphore_signal(barrier, inc=1, device_id=(1 - dp_me, me), device_id_type=MESH)
    pl.semaphore_wait(barrier, tp)

    copies = []
    for d in range(1, tp):
        copies.append(pltpu.make_async_remote_copy(
            src_ref=stats_ref, dst_ref=slots.at[me], send_sem=send_sem.at[d], recv_sem=recv_sem.at[d],
            device_id=(dp_me, lax.rem(me + d, tp)), device_id_type=MESH))
    copies.append(pltpu.make_async_remote_copy(
        src_ref=mask_ref, dst_ref=mask_slot, send_sem=msend_sem, recv_sem=mrecv_sem,
        device_id=(1 - dp_me, me), device_id_type=MESH))
    for copy in copies:
        copy.start()
    slots[me] = stats_ref[...]
    for copy in copies:
        copy.wait()
    total = slots[0]
    for k in range(1, tp):
        total += slots[k]
    mask = mask_ref[...]
    weight = mask / (jnp.sum(mask, keepdims=True) + jnp.sum(mask_slot[...], keepdims=True))
    half = mask.shape[0]
    ab_ref[:half, :] = weight / total[:half]
    ab_ref[half:, :] = weight / total[half:]
    logs = weight * (jnp.log(total[:half]) - jnp.log(total[half:]))
    log_ref[...] = jnp.sum(logs.reshape(-1, 8, 128), axis=0)


def exchange_call(stats, mask_lines, tp):
    whole = pl.BlockSpec(memory_space=pltpu.VMEM)
    return pl.pallas_call(
        functools.partial(exchange_kernel, tp),
        in_specs=[whole, whole],
        out_specs=[whole, whole],
        out_shape=[jax.ShapeDtypeStruct(stats.shape, jnp.float32), jax.ShapeDtypeStruct((8, 128), jnp.float32)],
        scratch_shapes=[
            pltpu.VMEM((tp,) + stats.shape, jnp.float32),
            pltpu.VMEM(mask_lines.shape, jnp.float32),
            pltpu.SemaphoreType.DMA((tp,)),
            pltpu.SemaphoreType.DMA((tp,)),
            pltpu.SemaphoreType.DMA,
            pltpu.SemaphoreType.DMA,
        ],
        compiler_params=pltpu.CompilerParams(collective_id=0, has_side_effects=True),
        name="exchange",
    )(stats, mask_lines)


def grad_kernel(first, ab_ref, x_ref, xt_ref, tab_ref, tea_ref, *refs):
    if first:
        table_ref, g_ref, kl_ref, z0_ref, z1_ref, coef_ref = refs
    else:
        kl_in_ref, table_ref, g_ref, kl_ref, z0_ref, z1_ref, coef_ref = refs
    z_refs = (z0_ref, z1_ref)
    col = z0_ref.shape[1]
    count = tab_ref.shape[1] // col
    block = pl.program_id(0)

    @pl.when(block == 0)
    def _():
        table_ref[...] = jnp.zeros_like(table_ref)
        kl_ref[...] = jnp.zeros_like(kl_ref) if first else kl_in_ref[...]

    for k in range(2):
        for b in range(LINES):
            line = ab_ref[pl.ds(k * (ab_ref.shape[0] // 2) + block * LINES + b, 1), :]
            coef_ref[k, b * 128:(b + 1) * 128, :] = jnp.broadcast_to(line, (128, 128)).T

    def columns(n):
        return pl.ds(pl.multiple_of(n * col, col), col)

    def logits(n, par):
        z_refs[par][...] = lax.dot_general(x_ref[...], tab_ref[:, columns(n)], NN, preferred_element_type=jnp.float32)

    def weigh(n, par):
        kl_acc = kl_ref[...]
        for r in range(0, TOK, 64):
            rows = slice(r, r + 64)
            a = coef_ref[0, rows, :]
            b = coef_ref[1, rows, :]
            for q in range(col // 128):
                lanes = pl.ds(pl.multiple_of(n * col + q * 128, 128), 128)
                zq = z_refs[par][rows, q * 128:(q + 1) * 128]
                tq = tea_ref[rows, lanes].astype(jnp.float32)
                ts = jnp.tanh(zq * INV_CAP)
                tt = jnp.tanh(tq * INV_CAP)
                pa = jnp.exp2(ts * EXP_SCALE) * a
                pb = jnp.exp2(tt * EXP_SCALE) * b
                kl = pb * (tt - ts)
                for w in range(0, 64, 8):
                    kl_acc += kl[w:w + 8]
                g_ref[rows, lanes] = ((pa - pb) * (1.0 - ts * ts)).astype(jnp.bfloat16)
        kl_ref[...] = kl_acc

    def product(n):
        table_ref[:, columns(n)] += lax.dot_general(xt_ref[...], g_ref[:, columns(n)], NN, preferred_element_type=jnp.float32)

    logits(0, 0)
    if count == 1:
        weigh(0, 0)
        product(0)
        return
    logits(1, 1)
    weigh(0, 0)

    def pair(p, _):
        for par in range(2):
            n = 2 * p + par
            logits(n, par)
            weigh(n - 1, 1 - par)
            product(n - 2)
        return 0

    if count == 4:
        pair(1, 0)
    elif count > 4:
        lax.fori_loop(1, count // 2, pair, 0)
    product(count - 2)
    weigh(count - 1, 1)
    product(count - 1)


def grad_call(ab, x_rows, x_t, tab_t, tea_rows, start, size, kl):
    tokens, dim = x_rows.shape
    first = kl is None
    col = min(GCOL, size)
    assert size == col or size % (2 * col) == 0
    in_specs = [
        pl.BlockSpec(ab.shape, lambda i: (0, 0)),
        pl.BlockSpec((TOK, dim), lambda i: (i, 0)),
        pl.BlockSpec((dim, TOK), lambda i: (0, i)),
        pl.BlockSpec((pl.Element(dim), pl.Element(size)), lambda i: (0, start), pipeline_mode=pl.Buffered(1)),
        pl.BlockSpec((pl.Element(TOK), pl.Element(size)), lambda i: (i * TOK, start)),
    ]
    operands = [ab, x_rows, x_t, tab_t, tea_rows]
    if not first:
        in_specs.append(pl.BlockSpec((8, 128), lambda i: (0, 0)))
        operands.append(kl)
    return pl.pallas_call(
        functools.partial(grad_kernel, first),
        grid=(tokens // TOK,),
        in_specs=in_specs,
        out_specs=[
            pl.BlockSpec((dim, size), lambda i: (0, 0)),
            pl.BlockSpec((TOK, size), lambda i: (i, 0)),
            pl.BlockSpec((8, 128), lambda i: (0, 0)),
        ],
        out_shape=[
            jax.ShapeDtypeStruct((dim, size), jnp.float32),
            jax.ShapeDtypeStruct((tokens, size), jnp.bfloat16),
            jax.ShapeDtypeStruct((8, 128), jnp.float32),
        ],
        scratch_shapes=[
            pltpu.VMEM((TOK, col), jnp.float32),
            pltpu.VMEM((TOK, col), jnp.float32),
            pltpu.VMEM((2, TOK, 128), jnp.float32),
        ],
        compiler_params=pltpu.CompilerParams(vmem_limit_bytes=VMEM_LIMIT),
        cost_estimate=pl.CostEstimate(flops=4 * tokens * size * dim, bytes_accessed=4 * tokens * size, transcendentals=0),
    )(*operands)


def back_kernel(half_ref, tab_ref, *refs):
    g_refs, dx_ref = refs[:-1], refs[-1]
    start = 0
    for g_ref in g_refs:
        size = g_ref.shape[1]
        step = min(BACK, size)
        for n in range(size // step):
            cols = slice(start + n * step, start + (n + 1) * step)
            dx = lax.dot_general(tab_ref[:, cols], g_ref[:, n * step:(n + 1) * step], NT, preferred_element_type=jnp.float32)
            if start + n == 0:
                dx_ref[...] = dx
            else:
                dx_ref[...] += dx
        start += size


def back_call(tab_t, grads, half):
    dim, cols = tab_t.shape
    tokens = grads[0].shape[0]
    rows = dim // 2
    return pl.pallas_call(
        back_kernel,
        grid_spec=pltpu.PrefetchScalarGridSpec(
            num_scalar_prefetch=1,
            grid=(tokens // TOK,),
            in_specs=[pl.BlockSpec((rows, cols), lambda i, h: (h[0], 0), pipeline_mode=pl.Buffered(1))]
            + [pl.BlockSpec((TOK, g.shape[1]), lambda i, h: (i, 0)) for g in grads],
            out_specs=pl.BlockSpec((rows, TOK), lambda i, h: (0, i)),
        ),
        out_shape=jax.ShapeDtypeStruct((rows, tokens), jnp.float32),
        compiler_params=pltpu.CompilerParams(vmem_limit_bytes=VMEM_LIMIT),
        cost_estimate=pl.CostEstimate(flops=tokens * cols * dim, bytes_accessed=2 * tokens * cols, transcendentals=0),
        name="back",
    )(half[None], tab_t, *grads)


def finish_kernel(off_ref, hid_ref, gain_ref, *refs):
    piece_refs, (out_ref, norm_ref, a_ref, gain_buf) = refs[:-4], refs[-4:]
    dim, toks = hid_ref.shape

    @pl.when(pl.program_id(0) == 0)
    def _():
        gain_buf[...] = jnp.broadcast_to(1.0 + gain_ref[...], (128, dim)).T

    hid = hid_ref[...].astype(jnp.float32)
    inv_rms = lax.rsqrt(jnp.mean(hid * hid, axis=0, keepdims=True) + NORM_EPS)
    norm_ref[...] = hid * inv_rms
    dot = jnp.zeros((1, toks), jnp.float32)
    for k, piece_ref in enumerate(piece_refs):
        rows = pl.ds(pl.multiple_of(off_ref[k], 8), piece_ref.shape[0])
        gain = gain_buf[rows, :]
        for b in range(toks // 128):
            a_ref[rows, b * 128:(b + 1) * 128] = piece_ref[:, b * 128:(b + 1) * 128] * gain
        dot += jnp.sum(a_ref[rows, :] * norm_ref[rows, :], axis=0, keepdims=True)
    out_ref[...] = (inv_rms * (a_ref[...] - norm_ref[...] * (dot / dim))).astype(jnp.bfloat16)


def finish_call(offsets, hid_t, gain_row, pieces):
    dim, tokens = hid_t.shape
    rows = pieces[0].shape[0]
    return pl.pallas_call(
        finish_kernel,
        grid_spec=pltpu.PrefetchScalarGridSpec(
            num_scalar_prefetch=1,
            grid=(tokens // TOK,),
            in_specs=[pl.BlockSpec((dim, TOK), lambda i, o: (0, i)), pl.BlockSpec((1, dim), lambda i, o: (0, 0))]
            + [pl.BlockSpec((rows, TOK), lambda i, o: (0, i))] * len(pieces),
            out_specs=pl.BlockSpec((dim, TOK), lambda i, o: (0, i)),
            scratch_shapes=[pltpu.VMEM((dim, TOK), jnp.float32), pltpu.VMEM((dim, TOK), jnp.float32), pltpu.VMEM((dim, 128), jnp.float32)],
        ),
        out_shape=jax.ShapeDtypeStruct((dim, tokens), jnp.bfloat16),
        compiler_params=pltpu.CompilerParams(vmem_limit_bytes=VMEM_LIMIT),
        cost_estimate=pl.CostEstimate(flops=10 * tokens * dim, bytes_accessed=8 * tokens * dim, transcendentals=0),
        name="finish",
    )(offsets, hid_t, gain_row, *pieces)


def add_kernel(own_ref, recv_ref, *refs):
    refs[-1][...] = own_ref[...] + recv_ref[...]


def add_call(own, recv, start, cols, out, after):
    dim, size = own.shape
    step = 128
    spec = pl.BlockSpec((dim, step), lambda i: (0, i))
    hold = pl.BlockSpec(memory_space=pl.ANY)
    in_specs = [spec, spec]
    operands = [own, recv]
    aliases = {}
    if out is not None:
        operands.append(out)
        aliases = {2: 0}
    operands += after
    in_specs += [hold] * (len(operands) - 2)
    return pl.pallas_call(
        add_kernel,
        grid=(size // step,),
        in_specs=in_specs,
        out_specs=pl.BlockSpec((dim, step), lambda i: (0, start // step + i)),
        out_shape=jax.ShapeDtypeStruct((dim, cols), jnp.float32),
        input_output_aliases=aliases,
        cost_estimate=pl.CostEstimate(flops=size * dim, bytes_accessed=12 * size * dim, transcendentals=0),
    )(*operands)


def exchange_partner(i, step):
    if step == 0:
        return i ^ 1
    return i ^ (2 if (i & 1) == (step - 1) else 4)


def place(bits, rows):
    return (bits[0] * (rows // 2) + bits[1] * (rows // 4) + bits[2] * (rows // 8)).astype(jnp.int32)


def solution(mesh):
    tp = mesh.shape["tp"]

    def local_step(hid_rows, w_final, tab_rows, tea_rows, mask_rows):
        tokens, dim = hid_rows.shape
        hid_t, tab_t = hid_rows.T, tab_rows.T
        mask_lines = mask_rows.reshape(tokens // 128, 128)
        x_rows, x_t, stats = stats_call(mask_lines, w_final.reshape(1, dim), hid_t, tab_t, tea_rows)
        ab, log_part = exchange_call(stats, mask_lines, tp)

        swap = [(0, 1), (1, 0)]
        kl = None
        start = 0
        parts, grads = [], []
        for c, size in enumerate(CHUNKS):
            table_c, g, kl = grad_call(ab, x_rows, x_t, tab_t, tea_rows, start, size, kl)
            grads.append(g)
            recv = lax.ppermute(table_c, "dp", swap)
            parts.append((start, table_c, recv))
            start += size

        me = lax.axis_index("tp")
        core, xb, yb = me & 1, (me >> 1) & 1, (me >> 2) & 1
        bits = (core, jnp.where(core == 0, xb, yb), jnp.where(core == 0, yb, xb))
        perms = [[(i, exchange_partner(i, s)) for i in range(tp)] for s in range(3)]
        away = back_call(tab_t, grads, 1 - core)
        recv = lax.ppermute(away, "tp", perms[0])
        keep = back_call(tab_t, grads, core)
        for s in (1, 2):
            half = keep.shape[0] // 2
            gone = (1 - bits[s]) * half
            away = lax.dynamic_slice_in_dim(keep, gone, half, 0) + lax.dynamic_slice_in_dim(recv, gone, half, 0)
            away = lax.ppermute(away, "tp", perms[s])
            kept = bits[s] * half
            keep = lax.dynamic_slice_in_dim(keep, kept, half, 0) + lax.dynamic_slice_in_dim(recv, kept, half, 0)
            recv = away
        own = keep + recv
        pieces = [own]
        for s in (2, 1, 0):
            pieces += [lax.ppermute(piece, "tp", perms[s]) for piece in pieces]
        c, u, v = bits
        spots = [(c, u, v), (c, u, 1 - v), (c, 1 - u, v), (c, 1 - u, 1 - v)]
        spots += [(1 - c, v, u), (1 - c, v, 1 - u), (1 - c, 1 - v, u), (1 - c, 1 - v, 1 - u)]
        offsets = jnp.stack([place(spot, dim) for spot in spots])

        hid_g = lax.optimization_barrier(hid_t)
        hid_f = hid_g.astype(jnp.float32)
        inv_rms = lax.rsqrt(jnp.mean(hid_f * hid_f, axis=0, keepdims=True) + NORM_EPS)
        hid_own = lax.dynamic_slice_in_dim(hid_g, offsets[0], dim // 8, 0).astype(jnp.float32)
        gain_part = jnp.sum(own * (hid_own * inv_rms), axis=1)
        loss_part = SOFT_CAP * jnp.sum(kl) + jnp.sum(log_part) / tp
        small = lax.dynamic_update_slice_in_dim(jnp.zeros((1024,), jnp.float32), gain_part, offsets[0], 0)
        small = small + jnp.where(jnp.arange(1024) == dim, loss_part, 0.0)
        small = lax.psum(small, ("dp", "tp"))
        grad_h = finish_call(offsets, hid_t, w_final.reshape(1, dim), pieces)

        out = None
        for n, (begin, own, recv) in enumerate(parts):
            last = n == len(parts) - 1
            out = add_call(own, recv, begin, tab_t.shape[1], out, [grad_h, small] if last else [])
        return small[dim], grad_h.T, small[:dim], out.T

    return jax.shard_map(local_step, mesh=mesh, in_specs=(P('dp', None), P(None), P('tp', None), P('dp', 'tp'), P('dp')), out_specs=(P(), P('dp', None), P(None), P('tp', None)), check_vma=False)
```

profile of v0, /device:TPU:0, one launch (start us, length us, event | category | flops | bytes accessed | tf_op | source)
XLA Modules:
  0.0 1059.8 jit_solution(9803791491683179246)
XLA Ops:
  0.6 65.5 %stats.1 = (bf16[4096,960]{1,0:T(8,128)(2,1)}, bf16[960,4096]{1,0:T(8,128)(2,1)}, f32[64,128]{1,0:T(8,128)}) custom-call(f32[32,128]{1,0:T(8,128)} %bitcast.36, f32[1,960]{1,0:T(1,128)} %bitcast.38, bf16[960,4096]{1,0:T(8,128)(2,1)} %bitcast.30, bf16[960,6144]{1,0:T(8,128)(2,1)} %bitcast.19, bf16[4096,6144]{1,0:T(8,128)(2,1)} %tea_ref.15), custom_call_target="tpu_custom_call" | custom-call | flops 48318382080 | bytes 50331648 | tf_op jit(solution)/shard_map/stats/pallas_call | solution.py:183
  66.1 9.8 exchange.1
  75.9 14.9 %shard_map.84 = (f32[960,256]{1,0:T(8,128)}, bf16[4096,256]{1,0:T(8,128)(2,1)}, f32[8,128]{1,0:T(8,128)}) custom-call(f32[64,128]{1,0:T(8,128)} %get-tuple-element.34.ab_ref, bf16[4096,960]{1,0:T(8,128)(2,1)} %get-tuple-element.35.x_ref, bf16[960,4096]{1,0:T(8,128)(2,1)} %get-tuple-element.36.xt_ref, bf16[960,6144]{1,0:T(8,128)(2,1)} %bitcast.20, ...), custom_call_target="tpu_custom_call" | custom-call | flops 4026531840 | bytes 4194304 | tf_op jit(solution)/shard_map/pallas_call | solution.py:363
  90.9 14.8 %shard_map.85 = (f32[960,256]{1,0:T(8,128)}, bf16[4096,256]{1,0:T(8,128)(2,1)}, f32[8,128]{1,0:T(8,128)}) custom-call(f32[64,128]{1,0:T(8,128)} %get-tuple-element.34.ab_ref, bf16[4096,960]{1,0:T(8,128)(2,1)} %get-tuple-element.35.x_ref, bf16[960,4096]{1,0:T(8,128)(2,1)} %get-tuple-element.36.xt_ref, bf16[960,6144]{1,0:T(8,128)(2,1)} %bitcast.21, ...), custom_call_target="tpu_custom_call" | custom-call | flops 4026531840 | bytes 4194304 | tf_op jit(solution)/shard_map/pallas_call | solution.py:363
  105.7 18.0 %shard_map.86 = (f32[960,512]{1,0:T(8,128)}, bf16[4096,512]{1,0:T(8,128)(2,1)}, f32[8,128]{1,0:T(8,128)}) custom-call(f32[64,128]{1,0:T(8,128)} %get-tuple-element.34.ab_ref, bf16[4096,960]{1,0:T(8,128)(2,1)} %get-tuple-element.35.x_ref, bf16[960,4096]{1,0:T(8,128)(2,1)} %get-tuple-element.36.xt_ref, bf16[960,6144]{1,0:T(8,128)(2,1)} %bitcast.22, ...), custom_call_target="tpu_custom_call" | custom-call | flops 8053063680 | bytes 8388608 | tf_op jit(solution)/shard_map/pallas_call | solution.py:363
  123.7 30.1 %shard_map.87 = (f32[960,1024]{1,0:T(8,128)}, bf16[4096,1024]{1,0:T(8,128)(2,1)}, f32[8,128]{1,0:T(8,128)}) custom-call(f32[64,128]{1,0:T(8,128)} %get-tuple-element.34.ab_ref, bf16[4096,960]{1,0:T(8,128)(2,1)} %get-tuple-element.35.x_ref, bf16[960,4096]{1,0:T(8,128)(2,1)} %get-tuple-element.36.xt_ref, bf16[960,6144]{1,0:T(8,128)(2,1)} %bitcast.23, ...), custom_call_target="tpu_custom_call" | custom-call | flops 16106127360 | bytes 16777216 | tf_op jit(solution)/shard_map/pallas_call | solution.py:363
  153.8 66.7 %shard_map.88 = (f32[960,2048]{1,0:T(8,128)}, bf16[4096,2048]{1,0:T(8,128)(2,1)}, f32[8,128]{1,0:T(8,128)}) custom-call(f32[64,128]{1,0:T(8,128)} %get-tuple-element.34.ab_ref, bf16[4096,960]{1,0:T(8,128)(2,1)} %get-tuple-element.35.x_ref, bf16[960,4096]{1,0:T(8,128)(2,1)} %get-tuple-element.36.xt_ref, bf16[960,6144]{1,0:T(8,128)(2,1)} %bitcast.24, ...), custom_call_target="tpu_custom_call" | custom-call | flops 32212254720 | bytes 33554432 | tf_op jit(solution)/shard_map/pallas_call | solution.py:363
  220.5 50.2 %shard_map.89 = (f32[960,1536]{1,0:T(8,128)}, bf16[4096,1536]{1,0:T(8,128)(2,1)}, f32[8,128]{1,0:T(8,128)}) custom-call(f32[64,128]{1,0:T(8,128)} %get-tuple-element.34.ab_ref, bf16[4096,960]{1,0:T(8,128)(2,1)} %get-tuple-element.35.x_ref, bf16[960,4096]{1,0:T(8,128)(2,1)} %get-tuple-element.36.xt_ref, bf16[960,6144]{1,0:T(8,128)(2,1)} %bitcast.25, ...), custom_call_target="tpu_custom_call" | custom-call | flops 24159191040 | bytes 25165824 | tf_op jit(solution)/shard_map/pallas_call | solution.py:363
  270.7 14.9 %shard_map.90 = (f32[960,256]{1,0:T(8,128)}, bf16[4096,256]{1,0:T(8,128)(2,1)}, f32[8,128]{1,0:T(8,128)}) custom-call(f32[64,128]{1,0:T(8,128)} %get-tuple-element.34.ab_ref, bf16[4096,960]{1,0:T(8,128)(2,1)} %get-tuple-element.35.x_ref, bf16[960,4096]{1,0:T(8,128)(2,1)} %get-tuple-element.36.xt_ref, bf16[960,6144]{1,0:T(8,128)(2,1)} %bitcast.26, ...), custom_call_target="tpu_custom_call" | custom-call | flops 4026531840 | bytes 4194304 | tf_op jit(solution)/shard_map/pallas_call | solution.py:363
  285.6 14.9 %shard_map.91 = (f32[960,256]{1,0:T(8,128)}, bf16[4096,256]{1,0:T(8,128)(2,1)}, f32[8,128]{1,0:T(8,128)}) custom-call(f32[64,128]{1,0:T(8,128)} %get-tuple-element.34.ab_ref, bf16[4096,960]{1,0:T(8,128)(2,1)} %get-tuple-element.35.x_ref, bf16[960,4096]{1,0:T(8,128)(2,1)} %get-tuple-element.36.xt_ref, bf16[960,6144]{1,0:T(8,128)(2,1)} %bitcast.27, ...), custom_call_target="tpu_custom_call" | custom-call | flops 4026531840 | bytes 4194304 | tf_op jit(solution)/shard_map/pallas_call | solution.py:363
  300.5 32.6 %back.3 = f32[480,4096]{1,0:T(8,128)} custom-call(s32[1]{0:T(128)} %bitcast.5.half_ref, bf16[960,6144]{1,0:T(8,128)(2,1)} %bitcast.28, bf16[4096,256]{1,0:T(8,128)(2,1)} %get-tuple-element.46.refs_0_, bf16[4096,256]{1,0:T(8,128)(2,1)} %get-tuple-element.47.refs_1_, bf16[4096,512]{1,0:T(8,128)(2,1)} %get-tuple-element.48.refs_2_, ...), custom_call_target="tpu_custom_call" | custom-call | flops 24159191040 | bytes 50331648 | tf_op jit(solution)/shard_map/back/pallas_call | solution.py:407
  333.2 32.6 %back.2 = f32[480,4096]{1,0:T(8,128)} custom-call(s32[1]{0:T(128)} %bitcast.4.half_ref, bf16[960,6144]{1,0:T(8,128)(2,1)} %bitcast.29, bf16[4096,256]{1,0:T(8,128)(2,1)} %get-tuple-element.46.refs_0_, bf16[4096,256]{1,0:T(8,128)(2,1)} %get-tuple-element.47.refs_1_, bf16[4096,512]{1,0:T(8,128)(2,1)} %get-tuple-element.48.refs_2_, ...), custom_call_target="tpu_custom_call" | custom-call | flops 24159191040 | bytes 50331648 | tf_op jit(solution)/shard_map/back/pallas_call | solution.py:407
  365.9 10.7 %dynamic-slice_add_fusion.1 = (f32[240,4096]{1,0:T(8,128)}, f32[240,4096]{1,0:T(8,128)}) fusion(f32[480,4096]{1,0:T(8,128)} %collective-permute-done, s32[]{:T(128)S(6)} %select_n.40, f32[480,4096]{1,0:T(8,128)} %back.2, s32[]{:T(128)S(6)} %select_n.42), kind=kLoop, calls=%fused_computation.2 | loop fusion | flops 1966080 | bytes 23592968 | tf_op jit(solution)/shard_map/add | solution.py:536
  376.6 1.5 collective-permute-start.1
  378.1 44.5 %collective-permute-done.1 = f32[240,4096]{1,0:T(8,128)} collective-permute-done((f32[240,4096]{1,0:T(8,128)}, f32[240,4096]{1,0:T(8,128)}, u32[]{:S(2)}, u32[]{:S(2)}) %collective-permute-start.1) | collective-permute-done | bytes 3932192 | tf_op jit(solution)/shard_map/ppermute | solution.py:534
  422.6 3.6 dynamic-slice_add_fusion.2
  426.3 1.5 collective-permute-start.2
  427.8 2.0 collective-permute-start.12
  429.8 2.0 collective-permute-start.16
  431.8 19.3 %collective-permute-done.2 = f32[120,4096]{1,0:T(8,128)S(1)} collective-permute-done((f32[120,4096]{1,0:T(8,128)}, f32[120,4096]{1,0:T(8,128)S(1)}, u32[]{:S(2)}, u32[]{:S(2)}) %collective-permute-start.2) | collective-permute-done | bytes 1966112 | tf_op jit(solution)/shard_map/ppermute | solution.py:534
  451.1 0.2 collective-permute-start.17
  451.3 5.6 multiply_reduce_fusion
  457.1 3.1 multiply_reduce_fusion.1
  460.2 287.4 %collective-permute-done.11.recv_ref = f32[960,256]{1,0:T(8,128)} collective-permute-done((f32[960,256]{1,0:T(8,128)}, f32[960,256]{1,0:T(8,128)}, u32[]{:S(2)}, u32[]{:S(2)}) %collective-permute-start.11) | collective-permute-done | bytes 983072 | tf_op jit(solution)/shard_map/ppermute | solution.py:519
  747.6 21.0 %collective-permute-done.16.recv_ref = f32[960,256]{1,0:T(8,128)} collective-permute-done((f32[960,256]{1,0:T(8,128)}, f32[960,256]{1,0:T(8,128)}, u32[]{:S(2)}, u32[]{:S(2)}) %collective-permute-start.16) | collective-permute-done | bytes 983072 | tf_op jit(solution)/shard_map/ppermute | solution.py:519
  768.7 20.9 %collective-permute-done.17.recv_ref = f32[960,256]{1,0:T(8,128)S(1)} collective-permute-done((f32[960,256]{1,0:T(8,128)}, f32[960,256]{1,0:T(8,128)S(1)}, u32[]{:S(2)}, u32[]{:S(2)}) %collective-permute-start.17) | collective-permute-done | bytes 983072 | tf_op jit(solution)/shard_map/ppermute | solution.py:519
  789.6 0.6 collective-permute-start.3
  790.2 124.1 %collective-permute-done.15.recv_ref = f32[960,512]{1,0:T(8,128)S(1)} collective-permute-done((f32[960,512]{1,0:T(8,128)S(1)}, f32[960,512]{1,0:T(8,128)S(1)}, u32[]{:S(2)}, u32[]{:S(2)}) %collective-permute-start.15) | collective-permute-done | bytes 1966112 | tf_op jit(solution)/shard_map/ppermute | solution.py:519
  914.3 0.6 collective-permute-start.4
  914.8 1.5 collective-permute-start.5
  916.3 0.5 collective-permute-start.7
  916.8 22.2 %collective-permute-done.4.refs_2_ = f32[120,4096]{1,0:T(8,128)} collective-permute-done((f32[120,4096]{1,0:T(8,128)S(1)}, f32[120,4096]{1,0:T(8,128)}, u32[]{:S(2)}, u32[]{:S(2)}) %collective-permute-start.4) | collective-permute-done | bytes 1966112 | tf_op jit(solution)/shard_map/ppermute | solution.py:541
  939.0 21.1 %collective-permute-done.5.refs_3_ = f32[120,4096]{1,0:T(8,128)} collective-permute-done((f32[120,4096]{1,0:T(8,128)}, f32[120,4096]{1,0:T(8,128)}, u32[]{:S(2)}, u32[]{:S(2)}) %collective-permute-start.5) | collective-permute-done | bytes 1966112 | tf_op jit(solution)/shard_map/ppermute | solution.py:541
  960.1 0.3 collective-permute-start.10
  960.4 0.6 reduce_sum.36
  961.0 0.6 reduce_sum.37
  962.9 2.3 shard_map.92.refs_0_
  965.2 2.3 shard_map.93.refs_0_
  967.6 4.1 shard_map.94.refs_0_
  971.7 7.4 shard_map.95.refs_0_
  979.1 14.2 %shard_map.96.refs_0_ = f32[960,6144]{1,0:T(8,128)} custom-call(f32[960,2048]{1,0:T(8,128)} %get-tuple-element.57.own_ref, f32[960,2048]{1,0:T(8,128)} %collective-permute-done.13.recv_ref, f32[960,6144]{1,0:T(8,128)} %shard_map.95.refs_0_), custom_call_target="tpu_custom_call", output_to_operand_aliasing={{}: (2, {})} | custom-call | flops 1966080 | bytes 23592960 | tf_op jit(solution)/shard_map/pallas_call | solution.py:481
  993.3 10.8 %shard_map.97.refs_0_ = f32[960,6144]{1,0:T(8,128)} custom-call(f32[960,1536]{1,0:T(8,128)} %get-tuple-element.56.own_ref, f32[960,1536]{1,0:T(8,128)} %collective-permute-done.12.recv_ref, f32[960,6144]{1,0:T(8,128)} %shard_map.96.refs_0_), custom_call_target="tpu_custom_call", output_to_operand_aliasing={{}: (2, {})} | custom-call | flops 1474560 | bytes 17694720 | tf_op jit(solution)/shard_map/pallas_call | solution.py:481
  1004.0 0.6 stack.35.off_ref
  1004.6 2.3 shard_map.98.refs_0_
  1007.1 32.1 %psum.7.refs_2_ = f32[1024]{0:T(1024)S(1)} all-reduce(f32[1024]{0:T(1024)S(1)} %add_dynamic-update-slice_fusion), channel_id=1, replica_groups=mesh['dp'=2,'tp'=8] {'dp','tp'}, use_global_device_ids=true, to_apply=%region_4.5 | all-reduce | flops 1024 | bytes 8192 | tf_op jit(solution)/shard_map/psum | solution.py:555
  1039.2 0.6 slice.6
  1039.8 17.7 %finish.1.refs_1_ = bf16[960,4096]{1,0:T(8,128)(2,1)} custom-call(s32[8]{0:T(128)} %stack.35.off_ref, bf16[960,4096]{1,0:T(8,128)(2,1)} %bitcast.33, f32[1,960]{1,0:T(1,128)} %bitcast.39, f32[120,4096]{1,0:T(8,128)} %copy-done.1, f32[120,4096]{1,0:T(8,128)} %collective-permute-done.3.refs_1_, f32[120,4096]{1,0:T(8,128)} %collective-permute-done.4.refs_2_, ...), custom_call_target="tpu_custom_call" | custom-call | flops 39321600 | bytes 31457280 | tf_op jit(solution)/shard_map/finish/pallas_call | solution.py:447
  1057.5 2.3 shard_map.99
  (45 shorter events, 0.6 us)
Async XLA Ops:
  333.1 32.8 %collective-permute-start = (f32[480,4096]{1,0:T(8,128)}, f32[480,4096]{1,0:T(8,128)}, u32[]{:S(2)}, u32[]{:S(2)}) collective-permute-start(f32[480,4096]{1,0:T(8,128)} %back.3), channel_id=1, source_target_pairs={{0,1},{1,0},{2,3},{3,2},{4,5},{5,4},{6,7},{7,6},{8,9},{9,8},{10,11... | collective-permute-start | bytes 23592968 | tf_op jit(solution)/shard_map/ppermute | solution.py:528
  376.6 46.0 %collective-permute-start.1 = (f32[240,4096]{1,0:T(8,128)}, f32[240,4096]{1,0:T(8,128)}, u32[]{:S(2)}, u32[]{:S(2)}) collective-permute-start(f32[240,4096]{1,0:T(8,128)} %get-tuple-element.65), channel_id=1, source_target_pairs={{0,2},{1,5},{2,0},{3,7},{4,6},{5,1},{6,4},{7,3},{8,10},{9,13},{10,... | collective-permute-start | bytes 11796488 | tf_op jit(solution)/shard_map/ppermute | solution.py:534
  426.3 24.8 %collective-permute-start.2 = (f32[120,4096]{1,0:T(8,128)}, f32[120,4096]{1,0:T(8,128)S(1)}, u32[]{:S(2)}, u32[]{:S(2)}) collective-permute-start(f32[120,4096]{1,0:T(8,128)} %dynamic-slice_add_fusion.2), channel_id=1, source_target_pairs={{0,4},{1,3},{2,6},{3,1},{4,0},{5,7},{6,2},{7,5},{8,12},{9,11},{10,... | collective-permute-start | bytes 5898248 | tf_op jit(solution)/shard_map/ppermute | solution.py:534
  427.7 532.3 %collective-permute-start.13 = (f32[960,2048]{1,0:T(8,128)}, f32[960,2048]{1,0:T(8,128)}, u32[]{:S(2)}, u32[]{:S(2)}) collective-permute-start(f32[960,2048]{1,0:T(8,128)} %get-tuple-element.57.own_ref), channel_id=1, source_target_pairs={{0,8},{8,0},{1,9},{9,1},{2,10},{10,2},{3,11},{11,3},{4,12},{12,4},... | collective-permute-start | bytes 23592968 | tf_op jit(solution)/shard_map/ppermute | solution.py:519
  427.8 488.5 %collective-permute-start.12 = (f32[960,1536]{1,0:T(8,128)}, f32[960,1536]{1,0:T(8,128)}, u32[]{:S(2)}, u32[]{:S(2)}) collective-permute-start(f32[960,1536]{1,0:T(8,128)} %get-tuple-element.56.own_ref), channel_id=1, source_target_pairs={{0,8},{8,0},{1,9},{9,1},{2,10},{10,2},{3,11},{11,3},{4,12},{12,4},... | collective-permute-start | bytes 17694728 | tf_op jit(solution)/shard_map/ppermute | solution.py:519
  429.8 317.8 %collective-permute-start.11 = (f32[960,256]{1,0:T(8,128)}, f32[960,256]{1,0:T(8,128)}, u32[]{:S(2)}, u32[]{:S(2)}) collective-permute-start(f32[960,256]{1,0:T(8,128)} %get-tuple-element.55.own_ref), channel_id=1, source_target_pairs={{0,8},{8,0},{1,9},{9,1},{2,10},{10,2},{3,11},{11,3},{4,12},{12,4},... | collective-permute-start | bytes 2949128 | tf_op jit(solution)/shard_map/ppermute | solution.py:519
  429.8 338.9 %collective-permute-start.16 = (f32[960,256]{1,0:T(8,128)}, f32[960,256]{1,0:T(8,128)}, u32[]{:S(2)}, u32[]{:S(2)}) collective-permute-start(f32[960,256]{1,0:T(8,128)} %get-tuple-element.60.own_ref), channel_id=1, source_target_pairs={{0,8},{8,0},{1,9},{9,1},{2,10},{10,2},{3,11},{11,3},{4,12},{12,4},... | collective-permute-start | bytes 2949128 | tf_op jit(solution)/shard_map/ppermute | solution.py:519
  451.1 5.9 copy-start.6
  451.1 5.9 copy-start
  451.1 338.5 %collective-permute-start.17 = (f32[960,256]{1,0:T(8,128)}, f32[960,256]{1,0:T(8,128)S(1)}, u32[]{:S(2)}, u32[]{:S(2)}) collective-permute-start(f32[960,256]{1,0:T(8,128)} %get-tuple-element.61.own_ref), channel_id=1, source_target_pairs={{0,8},{8,0},{1,9},{9,1},{2,10},{10,2},{3,11},{11,3},{4,12},{12,4},... | collective-permute-start | bytes 2949128 | tf_op jit(solution)/shard_map/ppermute | solution.py:519
  457.0 290.6 %copy-start.2 = (f32[960,1024]{1,0:T(8,128)S(1)}, f32[960,1024]{1,0:T(8,128)}, u32[]{:S(2)}) copy-start(f32[960,1024]{1,0:T(8,128)} %get-tuple-element.58.own_ref) | copy-start | bytes 11796484
  457.0 311.6 %copy-start.4 = (f32[960,512]{1,0:T(8,128)S(1)}, f32[960,512]{1,0:T(8,128)}, u32[]{:S(2)}) copy-start(f32[960,512]{1,0:T(8,128)} %get-tuple-element.59.own_ref) | copy-start | bytes 5898244
  457.0 503.0 %copy-start.7 = (f32[960,256]{1,0:T(8,128)S(1)}, f32[960,256]{1,0:T(8,128)}, u32[]{:S(2)}) copy-start(f32[960,256]{1,0:T(8,128)} %get-tuple-element.54.own_ref) | copy-start | bytes 2949124
  457.1 503.4 %copy-start.11 = (f32[8,128]{1,0:T(8,128)S(1)}, f32[8,128]{1,0:T(8,128)}, u32[]{:S(2)}) copy-start(f32[8,128]{1,0:T(8,128)} %get-tuple-element.44) | copy-start | bytes 12292
  457.1 503.9 %copy-start.10 = (f32[8,128]{1,0:T(8,128)S(1)}, f32[8,128]{1,0:T(8,128)}, u32[]{:S(2)}) copy-start(f32[8,128]{1,0:T(8,128)} %get-tuple-element.45) | copy-start | bytes 12292
  460.2 505.0 %copy-start.1 = (f32[120,4096]{1,0:T(8,128)}, f32[120,4096]{1,0:T(8,128)S(1)}, u32[]{:S(2)}) copy-start(f32[120,4096]{1,0:T(8,128)S(1)} %get-tuple-element.63.refs_0_) | copy-start | bytes 5898244
  747.6 168.7 %collective-permute-start.14 = (f32[960,1024]{1,0:T(8,128)S(1)}, f32[960,1024]{1,0:T(8,128)S(1)}, u32[]{:S(2)}, u32[]{:S(2)}) collective-permute-start(f32[960,1024]{1,0:T(8,128)S(1)} %copy-done.2), channel_id=1, source_target_pairs={{0,8},{8,0},{1,9},{9,1},{2,10},{10,2},{3,11},{11,3},{4,12},{12,4},... | collective-permute-start | bytes 11796488 | tf_op jit(solution)/shard_map/ppermute | solution.py:519
  768.7 145.6 %collective-permute-start.15 = (f32[960,512]{1,0:T(8,128)S(1)}, f32[960,512]{1,0:T(8,128)S(1)}, u32[]{:S(2)}, u32[]{:S(2)}) collective-permute-start(f32[960,512]{1,0:T(8,128)S(1)} %copy-done.4), channel_id=1, source_target_pairs={{0,8},{8,0},{1,9},{9,1},{2,10},{10,2},{3,11},{11,3},{4,12},{12,4},... | collective-permute-start | bytes 5898248 | tf_op jit(solution)/shard_map/ppermute | solution.py:519
  789.6 170.4 %copy-start.8 = (f32[960,256]{1,0:T(8,128)}, f32[960,256]{1,0:T(8,128)S(1)}, u32[]{:S(2)}) copy-start(f32[960,256]{1,0:T(8,128)S(1)} %collective-permute-done.17.recv_ref) | copy-start | bytes 2949124
  789.6 125.2 %collective-permute-start.3 = (f32[120,4096]{1,0:T(8,128)S(1)}, f32[120,4096]{1,0:T(8,128)}, u32[]{:S(2)}, u32[]{:S(2)}) collective-permute-start(f32[120,4096]{1,0:T(8,128)S(1)} %get-tuple-element.63.refs_0_), channel_id=1, source_target_pairs={{0,4},{1,3},{2,6},{3,1},{4,0},{5,7},{6,2},{7,5},{8,12},{9,11},{10,... | collective-permute-start | bytes 5898248 | tf_op jit(solution)/shard_map/ppermute | solution.py:541
  914.3 24.7 %copy-start.5 = (f32[960,512]{1,0:T(8,128)}, f32[960,512]{1,0:T(8,128)S(1)}, u32[]{:S(2)}) copy-start(f32[960,512]{1,0:T(8,128)S(1)} %collective-permute-done.15.recv_ref) | copy-start | bytes 5898244
  914.3 24.7 %collective-permute-start.4 = (f32[120,4096]{1,0:T(8,128)S(1)}, f32[120,4096]{1,0:T(8,128)}, u32[]{:S(2)}, u32[]{:S(2)}) collective-permute-start(f32[120,4096]{1,0:T(8,128)S(1)} %get-tuple-element.63.refs_0_), channel_id=1, source_target_pairs={{0,2},{1,5},{2,0},{3,7},{4,6},{5,1},{6,4},{7,3},{8,10},{9,13},{10,... | collective-permute-start | bytes 5898248 | tf_op jit(solution)/shard_map/ppermute | solution.py:541
  914.8 45.2 %collective-permute-start.5 = (f32[120,4096]{1,0:T(8,128)}, f32[120,4096]{1,0:T(8,128)}, u32[]{:S(2)}, u32[]{:S(2)}) collective-permute-start(f32[120,4096]{1,0:T(8,128)} %collective-permute-done.3.refs_1_), channel_id=1, source_target_pairs={{0,2},{1,5},{2,0},{3,7},{4,6},{5,1},{6,4},{7,3},{8,10},{9,13},{10,... | collective-permute-start | bytes 5898248 | tf_op jit(solution)/shard_map/ppermute | solution.py:541
  916.3 22.7 %copy-start.3 = (f32[960,1024]{1,0:T(8,128)}, f32[960,1024]{1,0:T(8,128)S(1)}, u32[]{:S(2)}) copy-start(f32[960,1024]{1,0:T(8,128)S(1)} %collective-permute-done.14.recv_ref) | copy-start | bytes 11796484
  916.3 123.5 %collective-permute-start.6 = (f32[120,4096]{1,0:T(8,128)S(1)}, f32[120,4096]{1,0:T(8,128)}, u32[]{:S(2)}, u32[]{:S(2)}) collective-permute-start(f32[120,4096]{1,0:T(8,128)S(1)} %get-tuple-element.63.refs_0_), channel_id=1, source_target_pairs={{0,1},{1,0},{2,3},{3,2},{4,5},{5,4},{6,7},{7,6},{8,9},{9,8},{10,11... | collective-permute-start | bytes 5898248 | tf_op jit(solution)/shard_map/ppermute | solution.py:541
  916.3 123.5 %collective-permute-start.7 = (f32[120,4096]{1,0:T(8,128)}, f32[120,4096]{1,0:T(8,128)}, u32[]{:S(2)}, u32[]{:S(2)}) collective-permute-start(f32[120,4096]{1,0:T(8,128)} %collective-permute-done.3.refs_1_), channel_id=1, source_target_pairs={{0,1},{1,0},{2,3},{3,2},{4,5},{5,4},{6,7},{7,6},{8,9},{9,8},{10,11... | collective-permute-start | bytes 5898248 | tf_op jit(solution)/shard_map/ppermute | solution.py:541
  939.0 100.8 %collective-permute-start.8 = (f32[120,4096]{1,0:T(8,128)}, f32[120,4096]{1,0:T(8,128)}, u32[]{:S(2)}, u32[]{:S(2)}) collective-permute-start(f32[120,4096]{1,0:T(8,128)} %collective-permute-done.4.refs_2_), channel_id=1, source_target_pairs={{0,1},{1,0},{2,3},{3,2},{4,5},{5,4},{6,7},{7,6},{8,9},{9,8},{10,11... | collective-permute-start | bytes 5898248 | tf_op jit(solution)/shard_map/ppermute | solution.py:541
  960.1 79.7 %collective-permute-start.9 = (f32[120,4096]{1,0:T(8,128)}, f32[120,4096]{1,0:T(8,128)}, u32[]{:S(2)}, u32[]{:S(2)}) collective-permute-start(f32[120,4096]{1,0:T(8,128)} %collective-permute-done.5.refs_3_), channel_id=1, source_target_pairs={{0,1},{1,0},{2,3},{3,2},{4,5},{5,4},{6,7},{7,6},{8,9},{9,8},{10,11... | collective-permute-start | bytes 5898248 | tf_op jit(solution)/shard_map/ppermute | solution.py:541
  960.1 97.4 %collective-permute-start.10 = (f32[960,256]{1,0:T(8,128)S(1)}, f32[960,256]{1,0:T(8,128)}, u32[]{:S(2)}, u32[]{:S(2)}) collective-permute-start(f32[960,256]{1,0:T(8,128)S(1)} %copy-done.7), channel_id=1, source_target_pairs={{0,8},{8,0},{1,9},{9,1},{2,10},{10,2},{3,11},{11,3},{4,12},{12,4},... | collective-permute-start | bytes 2949128 | tf_op jit(solution)/shard_map/ppermute | solution.py:519
  1039.2 18.3 %copy-start.9 = (f32[1024]{0:T(1024)}, f32[1024]{0:T(1024)S(1)}, u32[]{:S(2)}) copy-start(f32[1024]{0:T(1024)S(1)} %psum.7.refs_2_) | copy-start | bytes 12292
where the time goes:
time: 1060 us
  waiting for transfers between devices  561 us (53%)
  Pallas kernels  429 us (40%)
  blocking collectives  32.1 us (3%)
  other arithmetic  24.5 us (2%)
  starting transfers between devices  10.9 us (1%)
    ppermute x8, waiting for transfers between devices, local_step(): recv = lax.ppermute(table_c, 'dp', swap)  453 us
    pallas_call x8, Pallas kernels, grad_call(): pl.pallas_call(functools.partial(grad_kernel, first), grid=(tokens // TOK...  225 us
    pallas_call x1, Pallas kernels, stats_call(): pl.pallas_call(stats_kernel, in_specs=[vmem, vmem, hbm, hbm, hbm], out_sp...  65.5 us
    pallas_call x2, Pallas kernels, back_call(): pl.pallas_call(back_kernel, grid_spec=pltpu.PrefetchScalarGridSpec(num_sc...  65.2 us
    ppermute x2, waiting for transfers between devices, local_step(): away = lax.ppermute(away, 'tp', perms[s])  63.9 us
    pallas_call x8, Pallas kernels, add_call(): pl.pallas_call(add_kernel, grid=(size // step,), in_specs=in_specs, out_s...  45.8 us
    ppermute x7, waiting for transfers between devices, local_step(): pieces += [lax.ppermute(piece, 'tp', perms[s]) for piece in pieces]  43.3 us
    psum x1, blocking collectives, local_step(): small = lax.psum(small, ('dp', 'tp'))  32.1 us
  transfers between devices with their start and end apart: 18, of which 8 were waited for; matrix products, arithmetic and copies ran while one was open for 1% of the time, Pallas kernels for 9%

commit v1 on v0

--- a/solution.py
+++ b/solution.py
@@ -421,12 +421,13 @@
 
 
 def finish_kernel(off_ref, hid_ref, gain_ref, *refs):
-    piece_refs, (out_ref, norm_ref, a_ref, gain_buf) = refs[:-4], refs[-4:]
+    piece_refs, (out_ref, sum_ref, norm_ref, a_ref, gain_buf) = refs[:-5], refs[-5:]
     dim, toks = hid_ref.shape
 
     @pl.when(pl.program_id(0) == 0)
     def _():
         gain_buf[...] = jnp.broadcast_to(1.0 + gain_ref[...], (128, dim)).T
+        sum_ref[...] = jnp.zeros_like(sum_ref)
 
     hid = hid_ref[...].astype(jnp.float32)
     inv_rms = lax.rsqrt(jnp.mean(hid * hid, axis=0, keepdims=True) + NORM_EPS)
@@ -435,8 +436,12 @@
     for k, piece_ref in enumerate(piece_refs):
         rows = pl.ds(pl.multiple_of(off_ref[k], 8), piece_ref.shape[0])
         gain = gain_buf[rows, :]
+        acc = sum_ref[rows, :]
         for b in range(toks // 128):
-            a_ref[rows, b * 128:(b + 1) * 128] = piece_ref[:, b * 128:(b + 1) * 128] * gain
+            lanes = slice(b * 128, (b + 1) * 128)
+            a_ref[rows, lanes] = piece_ref[:, lanes] * gain
+            acc += piece_ref[:, lanes] * norm_ref[rows, lanes]
+        sum_ref[rows, :] = acc
         dot += jnp.sum(a_ref[rows, :] * norm_ref[rows, :], axis=0, keepdims=True)
     out_ref[...] = (inv_rms * (a_ref[...] - norm_ref[...] * (dot / dim))).astype(jnp.bfloat16)
 
@@ -451,10 +456,10 @@
             grid=(tokens // TOK,),
             in_specs=[pl.BlockSpec((dim, TOK), lambda i, o: (0, i)), pl.BlockSpec((1, dim), lambda i, o: (0, 0))]
             + [pl.BlockSpec((rows, TOK), lambda i, o: (0, i))] * len(pieces),
-            out_specs=pl.BlockSpec((dim, TOK), lambda i, o: (0, i)),
+            out_specs=[pl.BlockSpec((dim, TOK), lambda i, o: (0, i)), pl.BlockSpec((dim, 128), lambda i, o: (0, 0))],
             scratch_shapes=[pltpu.VMEM((dim, TOK), jnp.float32), pltpu.VMEM((dim, TOK), jnp.float32), pltpu.VMEM((dim, 128), jnp.float32)],
         ),
-        out_shape=jax.ShapeDtypeStruct((dim, tokens), jnp.bfloat16),
+        out_shape=[jax.ShapeDtypeStruct((dim, tokens), jnp.bfloat16), jax.ShapeDtypeStruct((dim, 128), jnp.float32)],
         compiler_params=pltpu.CompilerParams(vmem_limit_bytes=VMEM_LIMIT),
         cost_estimate=pl.CostEstimate(flops=10 * tokens * dim, bytes_accessed=8 * tokens * dim, transcendentals=0),
         name="finish",
@@ -544,16 +549,11 @@
         spots += [(1 - c, v, u), (1 - c, v, 1 - u), (1 - c, 1 - v, u), (1 - c, 1 - v, 1 - u)]
         offsets = jnp.stack([place(spot, dim) for spot in spots])
 
-        hid_g = lax.optimization_barrier(hid_t)
-        hid_f = hid_g.astype(jnp.float32)
-        inv_rms = lax.rsqrt(jnp.mean(hid_f * hid_f, axis=0, keepdims=True) + NORM_EPS)
-        hid_own = lax.dynamic_slice_in_dim(hid_g, offsets[0], dim // 8, 0).astype(jnp.float32)
-        gain_part = jnp.sum(own * (hid_own * inv_rms), axis=1)
-        loss_part = SOFT_CAP * jnp.sum(kl) + jnp.sum(log_part) / tp
-        small = lax.dynamic_update_slice_in_dim(jnp.zeros((1024,), jnp.float32), gain_part, offsets[0], 0)
-        small = small + jnp.where(jnp.arange(1024) == dim, loss_part, 0.0)
-        small = lax.psum(small, ("dp", "tp"))
-        grad_h = finish_call(offsets, hid_t, w_final.reshape(1, dim), pieces)
+        loss_part = lax.psum(SOFT_CAP * jnp.sum(kl), "tp") + jnp.sum(log_part)
+        grad_h, gain_part = finish_call(offsets, hid_t, w_final.reshape(1, dim), pieces)
+        small = jnp.concatenate([jnp.sum(gain_part, axis=1), jnp.full((1024 - dim,), loss_part)])
+        other = lax.ppermute(small, "dp", swap)
+        small = small + other
 
         out = None
         for n, (begin, own, recv) in enumerate(parts):

time: 1060 us -> 945 us (0.89)
  waiting for transfers between devices: 561 us -> 465 us
  blocking collectives: 32.1 us -> 13.5 us
    ppermute x8, waiting for transfers between devices: 453 us -> 370 us  [local_step(): recv = lax.ppermute(table_c, 'dp', swap)]
    psum x1, blocking collectives: 32.1 us -> 13.5 us  [local_step(): loss_part = lax.psum(SOFT_CAP * jnp.sum(kl), 'tp') + jnp.sum(log_part)]
    ppermute x7, waiting for transfers between devices: 43.3 us -> 31.4 us  [local_step(): pieces += [lax.ppermute(piece, 'tp', perms[s]) for piece in pieces]]
  transfers between devices with their start and end apart: 18 -> 19, of which waited for: 8 -> 9; matrix products, arithmetic and copies ran while one was open for 1% -> 1% of each run, Pallas kernels for 9% -> 10%
where the time goes in v1:
time: 945 us; the launch traced here: 942 us
  waiting for transfers between devices  465 us (49%)
  Pallas kernels  428 us (45%)
  other arithmetic  18.6 us (2%)
  blocking collectives  13.5 us (1%)
  starting transfers between devices  12.5 us (1%)
    ppermute x8, waiting for transfers between devices, local_step(): recv = lax.ppermute(table_c, 'dp', swap)  370 us
    pallas_call x8, Pallas kernels, grad_call(): pl.pallas_call(functools.partial(grad_kernel, first), grid=(tokens // TOK...  224 us
    pallas_call x1, Pallas kernels, stats_call(): pl.pallas_call(stats_kernel, in_specs=[vmem, vmem, hbm, hbm, hbm], out_sp...  65.5 us
    pallas_call x2, Pallas kernels, back_call(): pl.pallas_call(back_kernel, grid_spec=pltpu.PrefetchScalarGridSpec(num_sc...  65.1 us
    ppermute x2, waiting for transfers between devices, local_step(): away = lax.ppermute(away, 'tp', perms[s])  63.8 us
    pallas_call x8, Pallas kernels, add_call(): pl.pallas_call(add_kernel, grid=(size // step,), in_specs=in_specs, out_s...  45.8 us
    ppermute x7, waiting for transfers between devices, local_step(): pieces += [lax.ppermute(piece, 'tp', perms[s]) for piece in pieces]  31.4 us
  transfers between devices with their start and end apart: 19, of which 9 were waited for; matrix products, arithmetic and copies ran while one was open for 1% of the time, Pallas kernels for 10%

profile of v1, /device:TPU:0, one launch (start us, length us, event | category | flops | bytes accessed | tf_op | source)
XLA Modules:
  0.0 942.3 jit_solution(10172364833352861930)
XLA Ops:
  0.6 65.5 %stats.1 = (bf16[4096,960]{1,0:T(8,128)(2,1)}, bf16[960,4096]{1,0:T(8,128)(2,1)}, f32[64,128]{1,0:T(8,128)}) custom-call(f32[32,128]{1,0:T(8,128)} %bitcast.34, f32[1,960]{1,0:T(1,128)} %bitcast.36, bf16[960,4096]{1,0:T(8,128)(2,1)} %bitcast.31, bf16[960,6144]{1,0:T(8,128)(2,1)} %bitcast.19, bf16[4096,6144]{1,0:T(8,128)(2,1)} %tea_ref.15), custom_call_target="tpu_custom_call" | custom-call | flops 48318382080 | bytes 50331648 | tf_op jit(solution)/shard_map/stats/pallas_call | solution.py:183
  66.1 9.8 %exchange.1 = (f32[64,128]{1,0:T(8,128)}, f32[8,128]{1,0:T(8,128)}) custom-call(f32[64,128]{1,0:T(8,128)} %get-tuple-element.35.stats_ref, f32[32,128]{1,0:T(8,128)} %bitcast.35), custom_call_target="tpu_custom_call" | custom-call | tf_op jit(solution)/shard_map/exchange/pallas_call | solution.py:255
  76.0 14.9 %shard_map.84 = (f32[960,256]{1,0:T(8,128)}, bf16[4096,256]{1,0:T(8,128)(2,1)}, f32[8,128]{1,0:T(8,128)}) custom-call(f32[64,128]{1,0:T(8,128)} %get-tuple-element.36.ab_ref, bf16[4096,960]{1,0:T(8,128)(2,1)} %get-tuple-element.37.x_ref, bf16[960,4096]{1,0:T(8,128)(2,1)} %get-tuple-element.38.xt_ref, bf16[960,6144]{1,0:T(8,128)(2,1)} %bitcast.20, ...), custom_call_target="tpu_custom_call" | custom-call | flops 4026531840 | bytes 4194304 | tf_op jit(solution)/shard_map/pallas_call | solution.py:363
  90.9 14.8 %shard_map.85 = (f32[960,256]{1,0:T(8,128)}, bf16[4096,256]{1,0:T(8,128)(2,1)}, f32[8,128]{1,0:T(8,128)}) custom-call(f32[64,128]{1,0:T(8,128)} %get-tuple-element.36.ab_ref, bf16[4096,960]{1,0:T(8,128)(2,1)} %get-tuple-element.37.x_ref, bf16[960,4096]{1,0:T(8,128)(2,1)} %get-tuple-element.38.xt_ref, bf16[960,6144]{1,0:T(8,128)(2,1)} %bitcast.21, ...), custom_call_target="tpu_custom_call" | custom-call | flops 4026531840 | bytes 4194304 | tf_op jit(solution)/shard_map/pallas_call | solution.py:363
  105.7 18.0 %shard_map.86 = (f32[960,512]{1,0:T(8,128)}, bf16[4096,512]{1,0:T(8,128)(2,1)}, f32[8,128]{1,0:T(8,128)}) custom-call(f32[64,128]{1,0:T(8,128)} %get-tuple-element.36.ab_ref, bf16[4096,960]{1,0:T(8,128)(2,1)} %get-tuple-element.37.x_ref, bf16[960,4096]{1,0:T(8,128)(2,1)} %get-tuple-element.38.xt_ref, bf16[960,6144]{1,0:T(8,128)(2,1)} %bitcast.22, ...), custom_call_target="tpu_custom_call" | custom-call | flops 8053063680 | bytes 8388608 | tf_op jit(solution)/shard_map/pallas_call | solution.py:363
  123.7 30.2 %shard_map.87 = (f32[960,1024]{1,0:T(8,128)}, bf16[4096,1024]{1,0:T(8,128)(2,1)}, f32[8,128]{1,0:T(8,128)}) custom-call(f32[64,128]{1,0:T(8,128)} %get-tuple-element.36.ab_ref, bf16[4096,960]{1,0:T(8,128)(2,1)} %get-tuple-element.37.x_ref, bf16[960,4096]{1,0:T(8,128)(2,1)} %get-tuple-element.38.xt_ref, bf16[960,6144]{1,0:T(8,128)(2,1)} %bitcast.23, ...), custom_call_target="tpu_custom_call" | custom-call | flops 16106127360 | bytes 16777216 | tf_op jit(solution)/shard_map/pallas_call | solution.py:363
  153.8 66.7 %shard_map.88 = (f32[960,2048]{1,0:T(8,128)}, bf16[4096,2048]{1,0:T(8,128)(2,1)}, f32[8,128]{1,0:T(8,128)}) custom-call(f32[64,128]{1,0:T(8,128)} %get-tuple-element.36.ab_ref, bf16[4096,960]{1,0:T(8,128)(2,1)} %get-tuple-element.37.x_ref, bf16[960,4096]{1,0:T(8,128)(2,1)} %get-tuple-element.38.xt_ref, bf16[960,6144]{1,0:T(8,128)(2,1)} %bitcast.24, ...), custom_call_target="tpu_custom_call" | custom-call | flops 32212254720 | bytes 33554432 | tf_op jit(solution)/shard_map/pallas_call | solution.py:363
  220.5 50.2 %shard_map.89 = (f32[960,1536]{1,0:T(8,128)}, bf16[4096,1536]{1,0:T(8,128)(2,1)}, f32[8,128]{1,0:T(8,128)}) custom-call(f32[64,128]{1,0:T(8,128)} %get-tuple-element.36.ab_ref, bf16[4096,960]{1,0:T(8,128)(2,1)} %get-tuple-element.37.x_ref, bf16[960,4096]{1,0:T(8,128)(2,1)} %get-tuple-element.38.xt_ref, bf16[960,6144]{1,0:T(8,128)(2,1)} %bitcast.25, ...), custom_call_target="tpu_custom_call" | custom-call | flops 24159191040 | bytes 25165824 | tf_op jit(solution)/shard_map/pallas_call | solution.py:363
  270.7 14.8 %shard_map.90 = (f32[960,256]{1,0:T(8,128)}, bf16[4096,256]{1,0:T(8,128)(2,1)}, f32[8,128]{1,0:T(8,128)}) custom-call(f32[64,128]{1,0:T(8,128)} %get-tuple-element.36.ab_ref, bf16[4096,960]{1,0:T(8,128)(2,1)} %get-tuple-element.37.x_ref, bf16[960,4096]{1,0:T(8,128)(2,1)} %get-tuple-element.38.xt_ref, bf16[960,6144]{1,0:T(8,128)(2,1)} %bitcast.26, ...), custom_call_target="tpu_custom_call" | custom-call | flops 4026531840 | bytes 4194304 | tf_op jit(solution)/shard_map/pallas_call | solution.py:363
  285.5 14.8 %shard_map.91 = (f32[960,256]{1,0:T(8,128)}, bf16[4096,256]{1,0:T(8,128)(2,1)}, f32[8,128]{1,0:T(8,128)}) custom-call(f32[64,128]{1,0:T(8,128)} %get-tuple-element.36.ab_ref, bf16[4096,960]{1,0:T(8,128)(2,1)} %get-tuple-element.37.x_ref, bf16[960,4096]{1,0:T(8,128)(2,1)} %get-tuple-element.38.xt_ref, bf16[960,6144]{1,0:T(8,128)(2,1)} %bitcast.27, ...), custom_call_target="tpu_custom_call" | custom-call | flops 4026531840 | bytes 4194304 | tf_op jit(solution)/shard_map/pallas_call | solution.py:363
  300.3 32.6 %back.3 = f32[480,4096]{1,0:T(8,128)} custom-call(s32[1]{0:T(128)} %bitcast.13.half_ref, bf16[960,6144]{1,0:T(8,128)(2,1)} %bitcast.28, bf16[4096,256]{1,0:T(8,128)(2,1)} %get-tuple-element.39.refs_0_, bf16[4096,256]{1,0:T(8,128)(2,1)} %get-tuple-element.41.refs_1_, bf16[4096,512]{1,0:T(8,128)(2,1)} %get-tuple-element.43.refs_2_, ...), custom_call_target="tpu_custom_call" | custom-call | flops 24159191040 | bytes 50331648 | tf_op jit(solution)/shard_map/back/pallas_call | solution.py:407
  333.0 32.6 %back.2 = f32[480,4096]{1,0:T(8,128)} custom-call(s32[1]{0:T(128)} %bitcast.10.half_ref, bf16[960,6144]{1,0:T(8,128)(2,1)} %bitcast.29, bf16[4096,256]{1,0:T(8,128)(2,1)} %get-tuple-element.39.refs_0_, bf16[4096,256]{1,0:T(8,128)(2,1)} %get-tuple-element.41.refs_1_, bf16[4096,512]{1,0:T(8,128)(2,1)} %get-tuple-element.43.refs_2_, ...), custom_call_target="tpu_custom_call" | custom-call | flops 24159191040 | bytes 50331648 | tf_op jit(solution)/shard_map/back/pallas_call | solution.py:407
  365.6 10.7 %dynamic-slice_add_fusion.1 = (f32[240,4096]{1,0:T(8,128)}, f32[240,4096]{1,0:T(8,128)}) fusion(f32[480,4096]{1,0:T(8,128)} %collective-permute-done, s32[]{:T(128)S(6)} %select_n.25, f32[480,4096]{1,0:T(8,128)} %back.2, s32[]{:T(128)S(6)} %select_n.27), kind=kLoop, calls=%fused_computation.1 | loop fusion | flops 1966080 | bytes 23592968 | tf_op jit(solution)/shard_map/add | solution.py:541
  376.4 1.5 collective-permute-start.1
  377.8 44.5 %collective-permute-done.1 = f32[240,4096]{1,0:T(8,128)} collective-permute-done((f32[240,4096]{1,0:T(8,128)}, f32[240,4096]{1,0:T(8,128)}, u32[]{:S(2)}, u32[]{:S(2)}) %collective-permute-start.1) | collective-permute-done | bytes 3932192 | tf_op jit(solution)/shard_map/ppermute | solution.py:539
  422.4 2.3 dynamic-slice_add_fusion.2
  424.7 1.5 collective-permute-start.2
  426.2 2.0 collective-permute-start.16
  428.3 2.0 collective-permute-start.18
  430.3 19.2 %collective-permute-done.2 = f32[120,4096]{1,0:T(8,128)} collective-permute-done((f32[120,4096]{1,0:T(8,128)S(1)}, f32[120,4096]{1,0:T(8,128)}, u32[]{:S(2)}, u32[]{:S(2)}) %collective-permute-start.2) | collective-permute-done | bytes 1966112 | tf_op jit(solution)/shard_map/ppermute | solution.py:539
  449.5 3.1 add_add_fusion.refs_0_
  452.5 1.5 collective-permute-start.3
  454.1 207.8 %collective-permute-done.17.recv_ref = f32[960,256]{1,0:T(8,128)} collective-permute-done((f32[960,256]{1,0:T(8,128)}, f32[960,256]{1,0:T(8,128)}, u32[]{:S(2)}, u32[]{:S(2)}) %collective-permute-start.17) | collective-permute-done | bytes 983072 | tf_op jit(solution)/shard_map/ppermute | solution.py:524
  661.8 1.5 collective-permute-start.4
  663.3 17.9 %collective-permute-done.18.recv_ref = f32[960,256]{1,0:T(8,128)} collective-permute-done((f32[960,256]{1,0:T(8,128)}, f32[960,256]{1,0:T(8,128)}, u32[]{:S(2)}, u32[]{:S(2)}) %collective-permute-start.18) | collective-permute-done | bytes 983072 | tf_op jit(solution)/shard_map/ppermute | solution.py:524
  681.4 0.6 collective-permute-start.5
  682.0 4.5 collective-permute-done.4.refs_2_
  686.5 21.0 %collective-permute-done.5.refs_3_ = f32[120,4096]{1,0:T(8,128)S(1)} collective-permute-done((f32[120,4096]{1,0:T(8,128)S(1)}, f32[120,4096]{1,0:T(8,128)S(1)}, u32[]{:S(2)}, u32[]{:S(2)}) %collective-permute-start.5) | collective-permute-done | bytes 1966112 | tf_op jit(solution)/shard_map/ppermute | solution.py:546
  707.5 0.5 collective-permute-start.9
  708.1 3.4 collective-permute-done.8.refs_6_
  711.8 2.5 collective-permute-done.9.refs_7_
  714.6 1.0 copy-done.7
  715.6 0.6 reduce_sum.28
  716.9 13.5 %psum.7 = f32[]{:T(128)} all-reduce(f32[]{:T(128)S(6)} %mul_shard_map.3), channel_id=1, replica_groups=mesh['dp'=2,'tp'=8] {'tp'}, use_global_device_ids=true, to_apply=%region_2.3 | all-reduce | flops 1 | bytes 8 | tf_op jit(solution)/shard_map/psum | solution.py:552
  730.4 0.6 reduce_sum.29
  732.2 0.6 stack.35.off_ref
  732.8 17.5 %finish.1 = (bf16[960,4096]{1,0:T(8,128)(2,1)}, f32[960,128]{1,0:T(8,128)}) custom-call(s32[8]{0:T(128)} %stack.35.off_ref, bf16[960,4096]{1,0:T(8,128)(2,1)} %bitcast.32, f32[1,960]{1,0:T(1,128)} %bitcast.37, f32[120,4096]{1,0:T(8,128)} %copy-done, f32[120,4096]{1,0:T(8,128)} %copy-done.1, f32[120,4096]{1,0:T(8,128)} %copy-done.2, f32[120,4096]{1,0:T(8,128)} %copy-done.4, ...), custom_call_target="tpu_custom_call" | custom-call | flops 39321600 | bytes 31457280 | tf_op jit(solution)/shard_map/finish/pallas_call | solution.py:452
  750.3 1.2 reduce_sum.27
  751.6 144.1 %collective-permute-done.15.recv_ref = f32[960,1024]{1,0:T(8,128)} collective-permute-done((f32[960,1024]{1,0:T(8,128)}, f32[960,1024]{1,0:T(8,128)}, u32[]{:S(2)}, u32[]{:S(2)}) %collective-permute-start.15) | collective-permute-done | bytes 3932192 | tf_op jit(solution)/shard_map/ppermute | solution.py:524
  896.0 2.3 shard_map.92.refs_0_
  898.3 2.3 shard_map.93.refs_0_
  900.6 4.1 shard_map.94.refs_0_
  904.7 7.4 shard_map.95.refs_0_
  912.1 14.2 %shard_map.96.refs_0_ = f32[960,6144]{1,0:T(8,128)} custom-call(f32[960,2048]{1,0:T(8,128)} %get-tuple-element.61.own_ref, f32[960,2048]{1,0:T(8,128)} %collective-permute-done.14.recv_ref, f32[960,6144]{1,0:T(8,128)} %shard_map.95.refs_0_), custom_call_target="tpu_custom_call", output_to_operand_aliasing={{}: (2, {})} | custom-call | flops 1966080 | bytes 23592960 | tf_op jit(solution)/shard_map/pallas_call | solution.py:486
  926.3 10.8 %shard_map.97.refs_0_ = f32[960,6144]{1,0:T(8,128)} custom-call(f32[960,1536]{1,0:T(8,128)} %get-tuple-element.60.own_ref, f32[960,1536]{1,0:T(8,128)} %collective-permute-done.13.recv_ref, f32[960,6144]{1,0:T(8,128)} %shard_map.96.refs_0_), custom_call_target="tpu_custom_call", output_to_operand_aliasing={{}: (2, {})} | custom-call | flops 1474560 | bytes 17694720 | tf_op jit(solution)/shard_map/pallas_call | solution.py:486
  937.1 2.3 shard_map.98.refs_0_
  939.4 0.6 slice.6
  940.0 2.3 shard_map.99
  (44 shorter events, 1.5 us)
Async XLA Ops:
  332.9 32.7 %collective-permute-start = (f32[480,4096]{1,0:T(8,128)}, f32[480,4096]{1,0:T(8,128)}, u32[]{:S(2)}, u32[]{:S(2)}) collective-permute-start(f32[480,4096]{1,0:T(8,128)} %back.3), channel_id=1, source_target_pairs={{0,1},{1,0},{2,3},{3,2},{4,5},{5,4},{6,7},{7,6},{8,9},{9,8},{10,11... | collective-permute-start | bytes 23592968 | tf_op jit(solution)/shard_map/ppermute | solution.py:533
  376.4 46.0 %collective-permute-start.1 = (f32[240,4096]{1,0:T(8,128)}, f32[240,4096]{1,0:T(8,128)}, u32[]{:S(2)}, u32[]{:S(2)}) collective-permute-start(f32[240,4096]{1,0:T(8,128)} %get-tuple-element.67), channel_id=1, source_target_pairs={{0,2},{1,5},{2,0},{3,7},{4,6},{5,1},{6,4},{7,3},{8,10},{9,13},{10,... | collective-permute-start | bytes 11796488 | tf_op jit(solution)/shard_map/ppermute | solution.py:539
  424.7 24.8 %collective-permute-start.2 = (f32[120,4096]{1,0:T(8,128)S(1)}, f32[120,4096]{1,0:T(8,128)}, u32[]{:S(2)}, u32[]{:S(2)}) collective-permute-start(f32[120,4096]{1,0:T(8,128)S(1)} %dynamic-slice_add_fusion.2), channel_id=1, source_target_pairs={{0,4},{1,3},{2,6},{3,1},{4,0},{5,7},{6,2},{7,5},{8,12},{9,11},{10,... | collective-permute-start | bytes 5898248 | tf_op jit(solution)/shard_map/ppermute | solution.py:539
  426.2 485.9 %collective-permute-start.14 = (f32[960,2048]{1,0:T(8,128)}, f32[960,2048]{1,0:T(8,128)}, u32[]{:S(2)}, u32[]{:S(2)}) collective-permute-start(f32[960,2048]{1,0:T(8,128)} %get-tuple-element.61.own_ref), channel_id=1, source_target_pairs={{0,8},{8,0},{1,9},{9,1},{2,10},{10,2},{3,11},{11,3},{4,12},{12,4},... | collective-permute-start | bytes 23592968 | tf_op jit(solution)/shard_map/ppermute | solution.py:524
  426.2 254.9 %collective-permute-start.16 = (f32[960,512]{1,0:T(8,128)}, f32[960,512]{1,0:T(8,128)}, u32[]{:S(2)}, u32[]{:S(2)}) collective-permute-start(f32[960,512]{1,0:T(8,128)} %get-tuple-element.63.own_ref), channel_id=1, source_target_pairs={{0,8},{8,0},{1,9},{9,1},{2,10},{10,2},{3,11},{11,3},{4,12},{12,4},... | collective-permute-start | bytes 5898248 | tf_op jit(solution)/shard_map/ppermute | solution.py:524
  428.2 233.6 %collective-permute-start.17 = (f32[960,256]{1,0:T(8,128)}, f32[960,256]{1,0:T(8,128)}, u32[]{:S(2)}, u32[]{:S(2)}) collective-permute-start(f32[960,256]{1,0:T(8,128)} %get-tuple-element.64.own_ref), channel_id=1, source_target_pairs={{0,8},{8,0},{1,9},{9,1},{2,10},{10,2},{3,11},{11,3},{4,12},{12,4},... | collective-permute-start | bytes 2949128 | tf_op jit(solution)/shard_map/ppermute | solution.py:524
  428.3 252.9 %collective-permute-start.18 = (f32[960,256]{1,0:T(8,128)}, f32[960,256]{1,0:T(8,128)}, u32[]{:S(2)}, u32[]{:S(2)}) collective-permute-start(f32[960,256]{1,0:T(8,128)} %get-tuple-element.65.own_ref), channel_id=1, source_target_pairs={{0,8},{8,0},{1,9},{9,1},{2,10},{10,2},{3,11},{11,3},{4,12},{12,4},... | collective-permute-start | bytes 2949128 | tf_op jit(solution)/shard_map/ppermute | solution.py:524
  430.3 285.4 %copy-start.10 = (f32[8,128]{1,0:T(8,128)S(1)}, f32[8,128]{1,0:T(8,128)}, u32[]{:S(2)}) copy-start(f32[8,128]{1,0:T(8,128)} %get-tuple-element.55) | copy-start | bytes 12292
  430.3 300.1 %copy-start.9 = (f32[8,128]{1,0:T(8,128)S(1)}, f32[8,128]{1,0:T(8,128)}, u32[]{:S(2)}) copy-start(f32[8,128]{1,0:T(8,128)} %get-tuple-element.56) | copy-start | bytes 12292
  452.5 280.3 %copy-start = (f32[120,4096]{1,0:T(8,128)}, f32[120,4096]{1,0:T(8,128)S(1)}, u32[]{:S(2)}) copy-start(f32[120,4096]{1,0:T(8,128)S(1)} %add_add_fusion.refs_0_) | copy-start | bytes 5898244
  452.5 228.9 %collective-permute-start.3 = (f32[120,4096]{1,0:T(8,128)S(1)}, f32[120,4096]{1,0:T(8,128)S(1)}, u32[]{:S(2)}, u32[]{:S(2)}) collective-permute-start(f32[120,4096]{1,0:T(8,128)S(1)} %add_add_fusion.refs_0_), channel_id=1, source_target_pairs={{0,4},{1,3},{2,6},{3,1},{4,0},{5,7},{6,2},{7,5},{8,12},{9,11},{10,... | collective-permute-start | bytes 5898248 | tf_op jit(solution)/shard_map/ppermute | solution.py:546
  661.8 24.6 %collective-permute-start.4 = (f32[120,4096]{1,0:T(8,128)S(1)}, f32[120,4096]{1,0:T(8,128)S(1)}, u32[]{:S(2)}, u32[]{:S(2)}) collective-permute-start(f32[120,4096]{1,0:T(8,128)S(1)} %add_add_fusion.refs_0_), channel_id=1, source_target_pairs={{0,2},{1,5},{2,0},{3,7},{4,6},{5,1},{6,4},{7,3},{8,10},{9,13},{10,... | collective-permute-start | bytes 5898248 | tf_op jit(solution)/shard_map/ppermute | solution.py:546
  681.1 5.3 collective-permute-start.6
  681.1 245.2 %collective-permute-start.13 = (f32[960,1536]{1,0:T(8,128)}, f32[960,1536]{1,0:T(8,128)}, u32[]{:S(2)}, u32[]{:S(2)}) collective-permute-start(f32[960,1536]{1,0:T(8,128)} %get-tuple-element.60.own_ref), channel_id=1, source_target_pairs={{0,8},{8,0},{1,9},{9,1},{2,10},{10,2},{3,11},{11,3},{4,12},{12,4},... | collective-permute-start | bytes 17694728 | tf_op jit(solution)/shard_map/ppermute | solution.py:524
  681.4 5.0 copy-start.1
  681.4 26.1 %collective-permute-start.5 = (f32[120,4096]{1,0:T(8,128)S(1)}, f32[120,4096]{1,0:T(8,128)S(1)}, u32[]{:S(2)}, u32[]{:S(2)}) collective-permute-start(f32[120,4096]{1,0:T(8,128)S(1)} %collective-permute-done.3.refs_1_), channel_id=1, source_target_pairs={{0,2},{1,5},{2,0},{3,7},{4,6},{5,1},{6,4},{7,3},{8,10},{9,13},{10,... | collective-permute-start | bytes 5898248 | tf_op jit(solution)/shard_map/ppermute | solution.py:546
  686.4 21.1 %copy-start.2 = (f32[120,4096]{1,0:T(8,128)}, f32[120,4096]{1,0:T(8,128)S(1)}, u32[]{:S(2)}) copy-start(f32[120,4096]{1,0:T(8,128)S(1)} %collective-permute-done.4.refs_2_) | copy-start | bytes 5898244
  686.4 21.1 %collective-permute-start.7 = (f32[120,4096]{1,0:T(8,128)S(1)}, f32[120,4096]{1,0:T(8,128)S(1)}, u32[]{:S(2)}, u32[]{:S(2)}) collective-permute-start(f32[120,4096]{1,0:T(8,128)S(1)} %collective-permute-done.3.refs_1_), channel_id=1, source_target_pairs={{0,1},{1,0},{2,3},{3,2},{4,5},{5,4},{6,7},{7,6},{8,9},{9,8},{10,11... | collective-permute-start | bytes 5898248 | tf_op jit(solution)/shard_map/ppermute | solution.py:546
  686.5 25.0 %copy-start.3 = (f32[120,4096]{1,0:T(8,128)}, f32[120,4096]{1,0:T(8,128)S(1)}, u32[]{:S(2)}) copy-start(f32[120,4096]{1,0:T(8,128)S(1)} %collective-permute-done.6.refs_4_) | copy-start | bytes 5898244
  686.5 209.2 %collective-permute-start.15 = (f32[960,1024]{1,0:T(8,128)}, f32[960,1024]{1,0:T(8,128)}, u32[]{:S(2)}, u32[]{:S(2)}) collective-permute-start(f32[960,1024]{1,0:T(8,128)} %get-tuple-element.62.own_ref), channel_id=1, source_target_pairs={{0,8},{8,0},{1,9},{9,1},{2,10},{10,2},{3,11},{11,3},{4,12},{12,4},... | collective-permute-start | bytes 11796488 | tf_op jit(solution)/shard_map/ppermute | solution.py:524
  707.5 4.0 copy-start.4
  707.5 4.0 collective-permute-start.8
  707.5 6.8 copy-start.5
  707.5 6.8 collective-permute-start.9
  711.5 2.8 copy-start.6
  711.5 225.6 %collective-permute-start.12 = (f32[960,256]{1,0:T(8,128)}, f32[960,256]{1,0:T(8,128)}, u32[]{:S(2)}, u32[]{:S(2)}) collective-permute-start(f32[960,256]{1,0:T(8,128)} %get-tuple-element.59.own_ref), channel_id=1, source_target_pairs={{0,8},{8,0},{1,9},{9,1},{2,10},{10,2},{3,11},{11,3},{4,12},{12,4},... | collective-permute-start | bytes 2949128 | tf_op jit(solution)/shard_map/ppermute | solution.py:524
  714.3 1.3 copy-start.7
  714.3 225.7 %collective-permute-start.11 = (f32[960,256]{1,0:T(8,128)}, f32[960,256]{1,0:T(8,128)}, u32[]{:S(2)}, u32[]{:S(2)}) collective-permute-start(f32[960,256]{1,0:T(8,128)} %get-tuple-element.58.own_ref), channel_id=1, source_target_pairs={{0,8},{8,0},{1,9},{9,1},{2,10},{10,2},{3,11},{11,3},{4,12},{12,4},... | collective-permute-start | bytes 2949128 | tf_op jit(solution)/shard_map/ppermute | solution.py:524
  895.7 43.7 %collective-permute-start.10 = (f32[1024]{0:T(1024)S(1)}, f32[1024]{0:T(1024)S(1)}, u32[]{:S(2)}, u32[]{:S(2)}) collective-permute-start(f32[1024]{0:T(1024)S(1)} %concatenate.3), channel_id=1, source_target_pairs={{0,8},{8,0},{1,9},{9,1},{2,10},{10,2},{3,11},{11,3},{4,12},{12,4},... | collective-permute-start | bytes 12296 | tf_op jit(solution)/shard_map/ppermute | solution.py:555
  939.4 0.6 copy-start.8

commit v2 on v1

--- a/solution.py
+++ b/solution.py
@@ -216,15 +216,33 @@
     )(mask_lines, gain_row, hid_t, tab_t, tea_rows)
 
 
-def exchange_kernel(tp, stats_ref, mask_ref, ab_ref, log_ref, slots, mask_slot, send_sem, recv_sem, msend_sem, mrecv_sem):
+def first_kernel(tp, stats_ref, mask_ref, x_hbm, xt_hbm, tab_hbm, tea_hbm, ab_ref, log_ref, table_ref, g_ref, kl_ref,
+                 slots, mask_slot, x_buf, xt_buf, tab_buf, tea_buf, z0_ref, z1_ref, stu_ref, tea_ref, gap_ref, coef0_ref, coef1_ref,
+                 send_sem, recv_sem, msend_sem, mrecv_sem, x_sem, xt_sem, tab_sem, tea_sem):
     dp_me = lax.axis_index("dp")
     me = lax.axis_index("tp")
+    tokens, width = g_ref.shape
+    blocks = tokens // TOK
+
+    def x_copy(m):
+        rows = pl.ds(m * TOK, TOK)
+        return pltpu.make_async_copy(x_hbm.at[rows, :], x_buf.at[rows, :], x_sem.at[m])
+
+    tab_copy = pltpu.make_async_copy(tab_hbm.at[:, pl.ds(0, width)], tab_buf, tab_sem)
+    tea_copy = pltpu.make_async_copy(tea_hbm.at[:, pl.ds(0, width)], tea_buf, tea_sem)
+    xt_copy = pltpu.make_async_copy(xt_hbm, xt_buf, xt_sem)
+    tab_copy.start()
+    x_copy(0).start()
+    tea_copy.start()
+    for m in range(1, blocks):
+        x_copy(m).start()
+    xt_copy.start()
+
     barrier = pltpu.get_barrier_semaphore()
     for d in range(1, tp):
         pl.semaphore_signal(barrier, inc=1, device_id=(dp_me, lax.rem(me + d, tp)), device_id_type=MESH)
     pl.semaphore_signal(barrier, inc=1, device_id=(1 - dp_me, me), device_id_type=MESH)
     pl.semaphore_wait(barrier, tp)
-
     copies = []
     for d in range(1, tp):
         copies.append(pltpu.make_async_remote_copy(
@@ -236,6 +254,49 @@
     for copy in copies:
         copy.start()
     slots[me] = stats_ref[...]
+
+    z_refs = (z0_ref, z1_ref)
+
+    def logits(m, par):
+        rows = pl.ds(pl.multiple_of(m * TOK, TOK), TOK)
+        z_refs[par][...] = lax.dot_general(x_buf[rows, :], tab_buf[...], NN, preferred_element_type=jnp.float32)
+
+    def terms(m, par):
+        for r in range(0, TOK, 64):
+            rows = pl.ds(pl.multiple_of(m * TOK + r, 64), 64)
+            gap = jnp.zeros((64, 128), jnp.float32)
+            for q in range(width // 128):
+                lanes = slice(q * 128, (q + 1) * 128)
+                ts = jnp.tanh(z_refs[par][r:r + 64, lanes] * INV_CAP)
+                tt = jnp.tanh(tea_buf[rows, lanes].astype(jnp.float32) * INV_CAP)
+                slope = 1.0 - ts * ts
+                eb = jnp.exp2(tt * EXP_SCALE)
+                stu_ref[rows, lanes] = jnp.exp2(ts * EXP_SCALE) * slope
+                tea_ref[rows, lanes] = eb * slope
+                gap += eb * (tt - ts)
+            gap_ref[rows, :] = gap
+
+    tab_copy.wait()
+    x_copy(0).wait()
+    tea_copy.wait()
+    logits(0, 0)
+
+    def ahead(p, _):
+        for par in range(2):
+            m = 2 * p + par
+            pltpu.make_async_copy(x_hbm.at[pl.ds(0, TOK), :], x_buf.at[pl.ds(0, TOK), :], x_sem.at[m + 1]).wait()
+            logits(m + 1, 1 - par)
+            terms(m, par)
+        return 0
+
+    if blocks > 2:
+        lax.fori_loop(0, blocks // 2 - 1, ahead, 0)
+    x_copy(blocks - 1).wait()
+    logits(blocks - 1, 1)
+    terms(blocks - 2, 0)
+    terms(blocks - 1, 1)
+
+    xt_copy.wait()
     for copy in copies:
         copy.wait()
     total = slots[0]
@@ -249,25 +310,95 @@
     logs = weight * (jnp.log(total[:half]) - jnp.log(total[half:]))
     log_ref[...] = jnp.sum(logs.reshape(-1, 8, 128), axis=0)
 
-
-def exchange_call(stats, mask_lines, tp):
+    kl_ref[...] = jnp.zeros_like(kl_ref)
+    table_ref[...] = jnp.zeros_like(table_ref)
+    coef_refs = (coef0_ref, coef1_ref)
+
+    def spread(m, par):
+        for k in range(2):
+            for b in range(LINES):
+                line = ab_ref[pl.ds(k * half + m * LINES + b, 1), :]
+                coef_refs[par][k, b * 128:(b + 1) * 128, :] = jnp.broadcast_to(line, (128, 128)).T
+
+    def weigh(m, par):
+        kl_acc = kl_ref[...]
+        for r in range(0, TOK, 64):
+            rows = pl.ds(pl.multiple_of(m * TOK + r, 64), 64)
+            a = coef_refs[par][0, r:r + 64, :]
+            b = coef_refs[par][1, r:r + 64, :]
+            gap = gap_ref[rows, :] * b
+            for w in range(0, 64, 8):
+                kl_acc += gap[w:w + 8]
+            for q in range(width // 128):
+                lanes = slice(q * 128, (q + 1) * 128)
+                g_ref[rows, lanes] = (stu_ref[rows, lanes] * a - tea_ref[rows, lanes] * b).astype(jnp.bfloat16)
+        kl_ref[...] = kl_acc
+
+    def product(m):
+        rows = pl.ds(pl.multiple_of(m * TOK, TOK), TOK)
+        table_ref[...] += lax.dot_general(xt_buf[:, rows], g_ref[rows, :], NN, preferred_element_type=jnp.float32)
+
+    spread(0, 0)
+    spread(1, 1)
+    weigh(0, 0)
+
+    def behind(p, _):
+        for par in range(2):
+            m = 2 * p + par
+            spread(m, par)
+            weigh(m - 1, 1 - par)
+            product(m - 2)
+        return 0
+
+    lax.fori_loop(1, blocks // 2, behind, 0)
+    weigh(blocks - 1, 1)
+    product(blocks - 2)
+    product(blocks - 1)
+
+
+def first_call(stats, mask_lines, x_rows, x_t, tab_t, tea_rows, width, tp):
+    tokens, dim = x_rows.shape
     whole = pl.BlockSpec(memory_space=pltpu.VMEM)
+    hbm = pl.BlockSpec(memory_space=pl.ANY)
+    blocks = tokens // TOK
     return pl.pallas_call(
-        functools.partial(exchange_kernel, tp),
-        in_specs=[whole, whole],
-        out_specs=[whole, whole],
-        out_shape=[jax.ShapeDtypeStruct(stats.shape, jnp.float32), jax.ShapeDtypeStruct((8, 128), jnp.float32)],
+        functools.partial(first_kernel, tp),
+        in_specs=[whole, whole, hbm, hbm, hbm, hbm],
+        out_specs=[whole] * 5,
+        out_shape=[
+            jax.ShapeDtypeStruct(stats.shape, jnp.float32),
+            jax.ShapeDtypeStruct((8, 128), jnp.float32),
+            jax.ShapeDtypeStruct((dim, width), jnp.float32),
+            jax.ShapeDtypeStruct((tokens, width), jnp.bfloat16),
+            jax.ShapeDtypeStruct((8, 128), jnp.float32),
+        ],
         scratch_shapes=[
             pltpu.VMEM((tp,) + stats.shape, jnp.float32),
             pltpu.VMEM(mask_lines.shape, jnp.float32),
+            pltpu.VMEM((tokens, dim), jnp.bfloat16),
+            pltpu.VMEM((dim, tokens), jnp.bfloat16),
+            pltpu.VMEM((dim, width), jnp.bfloat16),
+            pltpu.VMEM((tokens, width), jnp.bfloat16),
+            pltpu.VMEM((TOK, width), jnp.float32),
+            pltpu.VMEM((TOK, width), jnp.float32),
+            pltpu.VMEM((tokens, width), jnp.float32),
+            pltpu.VMEM((tokens, width), jnp.float32),
+            pltpu.VMEM((tokens, 128), jnp.float32),
+            pltpu.VMEM((2, TOK, 128), jnp.float32),
+            pltpu.VMEM((2, TOK, 128), jnp.float32),
             pltpu.SemaphoreType.DMA((tp,)),
             pltpu.SemaphoreType.DMA((tp,)),
             pltpu.SemaphoreType.DMA,
             pltpu.SemaphoreType.DMA,
+            pltpu.SemaphoreType.DMA((blocks,)),
+            pltpu.SemaphoreType.DMA,
+            pltpu.SemaphoreType.DMA,
+            pltpu.SemaphoreType.DMA,
         ],
-        compiler_params=pltpu.CompilerParams(collective_id=0, has_side_effects=True),
-        name="exchange",
-    )(stats, mask_lines)
+        compiler_params=pltpu.CompilerParams(collective_id=0, has_side_effects=True, vmem_limit_bytes=VMEM_LIMIT),
+        cost_estimate=pl.CostEstimate(flops=4 * tokens * width * dim, bytes_accessed=4 * tokens * dim, transcendentals=0),
+        name="first",
+    )(stats, mask_lines, x_rows, x_t, tab_t, tea_rows)
 
 
 def grad_kernel(first, ab_ref, x_ref, xt_ref, tab_ref, tea_ref, *refs):
@@ -512,14 +643,15 @@
         hid_t, tab_t = hid_rows.T, tab_rows.T
         mask_lines = mask_rows.reshape(tokens // 128, 128)
         x_rows, x_t, stats = stats_call(mask_lines, w_final.reshape(1, dim), hid_t, tab_t, tea_rows)
-        ab, log_part = exchange_call(stats, mask_lines, tp)
 
         swap = [(0, 1), (1, 0)]
-        kl = None
         start = 0
         parts, grads = [], []
         for c, size in enumerate(CHUNKS):
-            table_c, g, kl = grad_call(ab, x_rows, x_t, tab_t, tea_rows, start, size, kl)
+            if c == 0:
+                ab, log_part, table_c, g, kl = first_call(stats, mask_lines, x_rows, x_t, tab_t, tea_rows, size, tp)
+            else:
+                table_c, g, kl = grad_call(ab, x_rows, x_t, tab_t, tea_rows, start, size, kl)
             grads.append(g)
             recv = lax.ppermute(table_c, "dp", swap)
             parts.append((start, table_c, recv))

time: 945 us -> 938 us (level)
    pallas_call x8 -> x7, Pallas kernels: 224 us -> 209 us  [grad_call(): pl.pallas_call(functools.partial(grad_kernel, first), grid=(tokens // TOK...]
where the time goes in v2:
time: 938 us; the launch traced here: 936 us
  waiting for transfers between devices  464 us (49%)
  Pallas kernels  420 us (45%)
  other arithmetic  18.6 us (2%)
  starting transfers between devices  14.7 us (2%)
  blocking collectives  13.6 us (1%)
    ppermute x8, waiting for transfers between devices, local_step(): recv = lax.ppermute(table_c, 'dp', swap)  369 us
    pallas_call x7, Pallas kernels, grad_call(): pl.pallas_call(functools.partial(grad_kernel, first), grid=(tokens // TOK...  209 us
    pallas_call x1, Pallas kernels, stats_call(): pl.pallas_call(stats_kernel, in_specs=[vmem, vmem, hbm, hbm, hbm], out_sp...  65.5 us
    pallas_call x2, Pallas kernels, back_call(): pl.pallas_call(back_kernel, grid_spec=pltpu.PrefetchScalarGridSpec(num_sc...  65.2 us
    ppermute x2, waiting for transfers between devices, local_step(): away = lax.ppermute(away, 'tp', perms[s])  62.6 us
    pallas_call x8, Pallas kernels, add_call(): pl.pallas_call(add_kernel, grid=(size // step,), in_specs=in_specs, out_s...  45.8 us
    ppermute x7, waiting for transfers between devices, local_step(): pieces += [lax.ppermute(piece, 'tp', perms[s]) for piece in pieces]  31.9 us
  transfers between devices with their start and end apart: 19, of which 9 were waited for; matrix products, arithmetic and copies ran while one was open for 1% of the time, Pallas kernels for 10%

profile of v2, /device:TPU:0, one launch (start us, length us, event | category | flops | bytes accessed | tf_op | source)
XLA Modules:
  0.0 936.3 jit_solution(17486112725427120591)
XLA Ops:
  0.6 65.5 %stats.1 = (bf16[4096,960]{1,0:T(8,128)(2,1)}, bf16[960,4096]{1,0:T(8,128)(2,1)}, f32[64,128]{1,0:T(8,128)}) custom-call(f32[32,128]{1,0:T(8,128)} %bitcast.33, f32[1,960]{1,0:T(1,128)} %bitcast.36, bf16[960,4096]{1,0:T(8,128)(2,1)} %bitcast.31, bf16[960,6144]{1,0:T(8,128)(2,1)} %bitcast.19, bf16[4096,6144]{1,0:T(8,128)(2,1)} %tea_ref.13), custom_call_target="tpu_custom_call" | custom-call | flops 48318382080 | bytes 50331648 | tf_op jit(solution)/shard_map/stats/pallas_call | solution.py:183
  66.1 17.1 %first.1 = (f32[64,128]{1,0:T(8,128)}, f32[8,128]{1,0:T(8,128)}, f32[960,256]{1,0:T(8,128)}, bf16[4096,256]{1,0:T(8,128)(2,1)}, f32[8,128]{1,0:T(8,128)}) custom-call(f32[64,128]{1,0:T(8,128)} %get-tuple-element.35.stats_ref, f32[32,128]{1,0:T(8,128)} %bitcast.34, bf16[4096,960]{1,0:T(8,128)(2,1)} %get-tuple-element.36.x_hbm.x_ref, ...), custom_call_target="tpu_custom_call" | custom-call | flops 4026531840 | bytes 15728640 | tf_op jit(solution)/shard_map/first/pallas_call | solution.py:364
  83.2 14.8 %shard_map.84 = (f32[960,256]{1,0:T(8,128)}, bf16[4096,256]{1,0:T(8,128)(2,1)}, f32[8,128]{1,0:T(8,128)}) custom-call(f32[64,128]{1,0:T(8,128)} %get-tuple-element.39.ab_ref, bf16[4096,960]{1,0:T(8,128)(2,1)} %get-tuple-element.36.x_hbm.x_ref, bf16[960,4096]{1,0:T(8,128)(2,1)} %get-tuple-element.37.xt_hbm.xt_ref, bf16[960,6144]{1,0:T(8,128)(2,1)} %bitcast.21, ...), custom_call_target="tpu_custom_call" | custom-call | flops 4026531840 | bytes 4194304 | tf_op jit(solution)/shard_map/pallas_call | solution.py:494
  98.0 18.0 %shard_map.85 = (f32[960,512]{1,0:T(8,128)}, bf16[4096,512]{1,0:T(8,128)(2,1)}, f32[8,128]{1,0:T(8,128)}) custom-call(f32[64,128]{1,0:T(8,128)} %get-tuple-element.39.ab_ref, bf16[4096,960]{1,0:T(8,128)(2,1)} %get-tuple-element.36.x_hbm.x_ref, bf16[960,4096]{1,0:T(8,128)(2,1)} %get-tuple-element.37.xt_hbm.xt_ref, bf16[960,6144]{1,0:T(8,128)(2,1)} %bitcast.22, ...), custom_call_target="tpu_custom_call" | custom-call | flops 8053063680 | bytes 8388608 | tf_op jit(solution)/shard_map/pallas_call | solution.py:494
  116.0 30.2 %shard_map.86 = (f32[960,1024]{1,0:T(8,128)}, bf16[4096,1024]{1,0:T(8,128)(2,1)}, f32[8,128]{1,0:T(8,128)}) custom-call(f32[64,128]{1,0:T(8,128)} %get-tuple-element.39.ab_ref, bf16[4096,960]{1,0:T(8,128)(2,1)} %get-tuple-element.36.x_hbm.x_ref, bf16[960,4096]{1,0:T(8,128)(2,1)} %get-tuple-element.37.xt_hbm.xt_ref, bf16[960,6144]{1,0:T(8,128)(2,1)} %bitcast.23, ...), custom_call_target="tpu_custom_call" | custom-call | flops 16106127360 | bytes 16777216 | tf_op jit(solution)/shard_map/pallas_call | solution.py:494
  146.2 66.9 %shard_map.87 = (f32[960,2048]{1,0:T(8,128)}, bf16[4096,2048]{1,0:T(8,128)(2,1)}, f32[8,128]{1,0:T(8,128)}) custom-call(f32[64,128]{1,0:T(8,128)} %get-tuple-element.39.ab_ref, bf16[4096,960]{1,0:T(8,128)(2,1)} %get-tuple-element.36.x_hbm.x_ref, bf16[960,4096]{1,0:T(8,128)(2,1)} %get-tuple-element.37.xt_hbm.xt_ref, bf16[960,6144]{1,0:T(8,128)(2,1)} %bitcast.24, ...), custom_call_target="tpu_custom_call" | custom-call | flops 32212254720 | bytes 33554432 | tf_op jit(solution)/shard_map/pallas_call | solution.py:494
  213.1 49.9 %shard_map.88 = (f32[960,1536]{1,0:T(8,128)}, bf16[4096,1536]{1,0:T(8,128)(2,1)}, f32[8,128]{1,0:T(8,128)}) custom-call(f32[64,128]{1,0:T(8,128)} %get-tuple-element.39.ab_ref, bf16[4096,960]{1,0:T(8,128)(2,1)} %get-tuple-element.36.x_hbm.x_ref, bf16[960,4096]{1,0:T(8,128)(2,1)} %get-tuple-element.37.xt_hbm.xt_ref, bf16[960,6144]{1,0:T(8,128)(2,1)} %bitcast.25, ...), custom_call_target="tpu_custom_call" | custom-call | flops 24159191040 | bytes 25165824 | tf_op jit(solution)/shard_map/pallas_call | solution.py:494
  263.0 14.8 %shard_map.89 = (f32[960,256]{1,0:T(8,128)}, bf16[4096,256]{1,0:T(8,128)(2,1)}, f32[8,128]{1,0:T(8,128)}) custom-call(f32[64,128]{1,0:T(8,128)} %get-tuple-element.39.ab_ref, bf16[4096,960]{1,0:T(8,128)(2,1)} %get-tuple-element.36.x_hbm.x_ref, bf16[960,4096]{1,0:T(8,128)(2,1)} %get-tuple-element.37.xt_hbm.xt_ref, bf16[960,6144]{1,0:T(8,128)(2,1)} %bitcast.26, ...), custom_call_target="tpu_custom_call" | custom-call | flops 4026531840 | bytes 4194304 | tf_op jit(solution)/shard_map/pallas_call | solution.py:494
  277.9 14.8 %shard_map.90 = (f32[960,256]{1,0:T(8,128)}, bf16[4096,256]{1,0:T(8,128)(2,1)}, f32[8,128]{1,0:T(8,128)}) custom-call(f32[64,128]{1,0:T(8,128)} %get-tuple-element.39.ab_ref, bf16[4096,960]{1,0:T(8,128)(2,1)} %get-tuple-element.36.x_hbm.x_ref, bf16[960,4096]{1,0:T(8,128)(2,1)} %get-tuple-element.37.xt_hbm.xt_ref, bf16[960,6144]{1,0:T(8,128)(2,1)} %bitcast.27, ...), custom_call_target="tpu_custom_call" | custom-call | flops 4026531840 | bytes 4194304 | tf_op jit(solution)/shard_map/pallas_call | solution.py:494
  292.7 32.6 %back.3 = f32[480,4096]{1,0:T(8,128)} custom-call(s32[1]{0:T(128)} %bitcast.13.half_ref, bf16[960,6144]{1,0:T(8,128)(2,1)} %bitcast.28, bf16[4096,256]{1,0:T(8,128)(2,1)} %get-tuple-element.38.refs_0_, bf16[4096,256]{1,0:T(8,128)(2,1)} %get-tuple-element.41.refs_1_, bf16[4096,512]{1,0:T(8,128)(2,1)} %get-tuple-element.43.refs_2_, ...), custom_call_target="tpu_custom_call" | custom-call | flops 24159191040 | bytes 50331648 | tf_op jit(solution)/shard_map/back/pallas_call | solution.py:538
  325.3 0.5 collective-permute-start
  325.7 32.6 %back.2 = f32[480,4096]{1,0:T(8,128)} custom-call(s32[1]{0:T(128)} %bitcast.10.half_ref, bf16[960,6144]{1,0:T(8,128)(2,1)} %bitcast.29, bf16[4096,256]{1,0:T(8,128)(2,1)} %get-tuple-element.38.refs_0_, bf16[4096,256]{1,0:T(8,128)(2,1)} %get-tuple-element.41.refs_1_, bf16[4096,512]{1,0:T(8,128)(2,1)} %get-tuple-element.43.refs_2_, ...), custom_call_target="tpu_custom_call" | custom-call | flops 24159191040 | bytes 50331648 | tf_op jit(solution)/shard_map/back/pallas_call | solution.py:538
  358.3 10.7 %dynamic-slice_add_fusion.1 = (f32[240,4096]{1,0:T(8,128)}, f32[240,4096]{1,0:T(8,128)}) fusion(f32[480,4096]{1,0:T(8,128)} %collective-permute-done, s32[]{:T(128)S(6)} %select_n.25, f32[480,4096]{1,0:T(8,128)} %back.2, s32[]{:T(128)S(6)} %select_n.27), kind=kLoop, calls=%fused_computation.1 | loop fusion | flops 1966080 | bytes 23592968 | tf_op jit(solution)/shard_map/add | solution.py:673
  369.1 2.8 collective-permute-start.1
  371.9 44.0 %collective-permute-done.1 = f32[240,4096]{1,0:T(8,128)} collective-permute-done((f32[240,4096]{1,0:T(8,128)}, f32[240,4096]{1,0:T(8,128)}, u32[]{:S(2)}, u32[]{:S(2)}) %collective-permute-start.1) | collective-permute-done | bytes 3932192 | tf_op jit(solution)/shard_map/ppermute | solution.py:671
  415.8 2.3 dynamic-slice_add_fusion.2
  418.2 2.1 collective-permute-start.2
  420.3 2.0 collective-permute-start.16
  422.3 2.0 collective-permute-start.18
  424.3 18.7 %collective-permute-done.2 = f32[120,4096]{1,0:T(8,128)} collective-permute-done((f32[120,4096]{1,0:T(8,128)S(1)}, f32[120,4096]{1,0:T(8,128)}, u32[]{:S(2)}, u32[]{:S(2)}) %collective-permute-start.2) | collective-permute-done | bytes 1966112 | tf_op jit(solution)/shard_map/ppermute | solution.py:671
  443.0 3.1 add_add_fusion.refs_0_
  446.1 2.1 collective-permute-start.3
  448.1 207.8 %collective-permute-done.17.recv_ref = f32[960,256]{1,0:T(8,128)} collective-permute-done((f32[960,256]{1,0:T(8,128)}, f32[960,256]{1,0:T(8,128)}, u32[]{:S(2)}, u32[]{:S(2)}) %collective-permute-start.17) | collective-permute-done | bytes 983072 | tf_op jit(solution)/shard_map/ppermute | solution.py:656
  655.9 1.5 collective-permute-start.4
  657.4 17.6 %collective-permute-done.18.recv_ref = f32[960,256]{1,0:T(8,128)} collective-permute-done((f32[960,256]{1,0:T(8,128)}, f32[960,256]{1,0:T(8,128)}, u32[]{:S(2)}, u32[]{:S(2)}) %collective-permute-start.18) | collective-permute-done | bytes 983072 | tf_op jit(solution)/shard_map/ppermute | solution.py:656
  675.3 0.3 collective-permute-start.5
  675.6 4.9 collective-permute-done.4.refs_2_
  680.6 21.0 %collective-permute-done.5.refs_3_ = f32[120,4096]{1,0:T(8,128)S(1)} collective-permute-done((f32[120,4096]{1,0:T(8,128)S(1)}, f32[120,4096]{1,0:T(8,128)S(1)}, u32[]{:S(2)}, u32[]{:S(2)}) %collective-permute-start.5) | collective-permute-done | bytes 1966112 | tf_op jit(solution)/shard_map/ppermute | solution.py:678
  701.6 0.5 collective-permute-start.9
  702.1 3.4 collective-permute-done.8.refs_6_
  705.7 2.7 collective-permute-done.9.refs_7_
  708.5 1.2 copy-done.7
  709.7 0.6 reduce_sum.28
  711.0 13.6 %psum.7 = f32[]{:T(128)} all-reduce(f32[]{:T(128)S(6)} %mul_shard_map.3), channel_id=1, replica_groups=mesh['dp'=2,'tp'=8] {'tp'}, use_global_device_ids=true, to_apply=%region_2.3 | all-reduce | flops 1 | bytes 8 | tf_op jit(solution)/shard_map/psum | solution.py:684
  724.5 0.7 reduce_sum.29
  726.5 0.7 stack.35.off_ref
  727.2 17.5 %finish.1 = (bf16[960,4096]{1,0:T(8,128)(2,1)}, f32[960,128]{1,0:T(8,128)}) custom-call(s32[8]{0:T(128)} %stack.35.off_ref, bf16[960,4096]{1,0:T(8,128)(2,1)} %bitcast.32, f32[1,960]{1,0:T(1,128)} %bitcast.37, f32[120,4096]{1,0:T(8,128)} %copy-done, f32[120,4096]{1,0:T(8,128)} %copy-done.1, f32[120,4096]{1,0:T(8,128)} %copy-done.2, f32[120,4096]{1,0:T(8,128)} %copy-done.4, ...), custom_call_target="tpu_custom_call" | custom-call | flops 39321600 | bytes 31457280 | tf_op jit(solution)/shard_map/finish/pallas_call | solution.py:583
  744.7 1.2 reduce_sum.27
  745.9 143.6 %collective-permute-done.15.recv_ref = f32[960,1024]{1,0:T(8,128)} collective-permute-done((f32[960,1024]{1,0:T(8,128)}, f32[960,1024]{1,0:T(8,128)}, u32[]{:S(2)}, u32[]{:S(2)}) %collective-permute-start.15) | collective-permute-done | bytes 3932192 | tf_op jit(solution)/shard_map/ppermute | solution.py:656
  889.8 2.3 shard_map.91.refs_0_
  892.1 2.3 shard_map.92.refs_0_
  894.5 4.1 shard_map.93.refs_0_
  898.6 7.4 shard_map.94.refs_0_
  906.0 14.2 %shard_map.95.refs_0_ = f32[960,6144]{1,0:T(8,128)} custom-call(f32[960,2048]{1,0:T(8,128)} %get-tuple-element.61.own_ref, f32[960,2048]{1,0:T(8,128)} %collective-permute-done.14.recv_ref, f32[960,6144]{1,0:T(8,128)} %shard_map.94.refs_0_), custom_call_target="tpu_custom_call", output_to_operand_aliasing={{}: (2, {})} | custom-call | flops 1966080 | bytes 23592960 | tf_op jit(solution)/shard_map/pallas_call | solution.py:617
  920.2 10.8 %shard_map.96.refs_0_ = f32[960,6144]{1,0:T(8,128)} custom-call(f32[960,1536]{1,0:T(8,128)} %get-tuple-element.60.own_ref, f32[960,1536]{1,0:T(8,128)} %collective-permute-done.13.recv_ref, f32[960,6144]{1,0:T(8,128)} %shard_map.95.refs_0_), custom_call_target="tpu_custom_call", output_to_operand_aliasing={{}: (2, {})} | custom-call | flops 1474560 | bytes 17694720 | tf_op jit(solution)/shard_map/pallas_call | solution.py:617
  931.0 2.3 shard_map.97.refs_0_
  933.3 0.6 slice.6
  933.9 2.3 shard_map.98
  (43 shorter events, 1.0 us)
Async XLA Ops:
  325.3 33.1 %collective-permute-start = (f32[480,4096]{1,0:T(8,128)}, f32[480,4096]{1,0:T(8,128)}, u32[]{:S(2)}, u32[]{:S(2)}) collective-permute-start(f32[480,4096]{1,0:T(8,128)} %back.3), channel_id=1, source_target_pairs={{0,1},{1,0},{2,3},{3,2},{4,5},{5,4},{6,7},{7,6},{8,9},{9,8},{10,11... | collective-permute-start | bytes 23592968 | tf_op jit(solution)/shard_map/ppermute | solution.py:665
  369.1 46.8 %collective-permute-start.1 = (f32[240,4096]{1,0:T(8,128)}, f32[240,4096]{1,0:T(8,128)}, u32[]{:S(2)}, u32[]{:S(2)}) collective-permute-start(f32[240,4096]{1,0:T(8,128)} %get-tuple-element.67), channel_id=1, source_target_pairs={{0,2},{1,5},{2,0},{3,7},{4,6},{5,1},{6,4},{7,3},{8,10},{9,13},{10,... | collective-permute-start | bytes 11796488 | tf_op jit(solution)/shard_map/ppermute | solution.py:671
  418.2 24.8 %collective-permute-start.2 = (f32[120,4096]{1,0:T(8,128)S(1)}, f32[120,4096]{1,0:T(8,128)}, u32[]{:S(2)}, u32[]{:S(2)}) collective-permute-start(f32[120,4096]{1,0:T(8,128)S(1)} %dynamic-slice_add_fusion.2), channel_id=1, source_target_pairs={{0,4},{1,3},{2,6},{3,1},{4,0},{5,7},{6,2},{7,5},{8,12},{9,11},{10,... | collective-permute-start | bytes 5898248 | tf_op jit(solution)/shard_map/ppermute | solution.py:671
  420.3 485.7 %collective-permute-start.14 = (f32[960,2048]{1,0:T(8,128)}, f32[960,2048]{1,0:T(8,128)}, u32[]{:S(2)}, u32[]{:S(2)}) collective-permute-start(f32[960,2048]{1,0:T(8,128)} %get-tuple-element.61.own_ref), channel_id=1, source_target_pairs={{0,8},{8,0},{1,9},{9,1},{2,10},{10,2},{3,11},{11,3},{4,12},{12,4},... | collective-permute-start | bytes 23592968 | tf_op jit(solution)/shard_map/ppermute | solution.py:656
  420.3 254.7 %collective-permute-start.16 = (f32[960,512]{1,0:T(8,128)}, f32[960,512]{1,0:T(8,128)}, u32[]{:S(2)}, u32[]{:S(2)}) collective-permute-start(f32[960,512]{1,0:T(8,128)} %get-tuple-element.63.own_ref), channel_id=1, source_target_pairs={{0,8},{8,0},{1,9},{9,1},{2,10},{10,2},{3,11},{11,3},{4,12},{12,4},... | collective-permute-start | bytes 5898248 | tf_op jit(solution)/shard_map/ppermute | solution.py:656
  422.3 233.6 %collective-permute-start.17 = (f32[960,256]{1,0:T(8,128)}, f32[960,256]{1,0:T(8,128)}, u32[]{:S(2)}, u32[]{:S(2)}) collective-permute-start(f32[960,256]{1,0:T(8,128)} %get-tuple-element.64.own_ref), channel_id=1, source_target_pairs={{0,8},{8,0},{1,9},{9,1},{2,10},{10,2},{3,11},{11,3},{4,12},{12,4},... | collective-permute-start | bytes 2949128 | tf_op jit(solution)/shard_map/ppermute | solution.py:656
  422.3 252.7 %collective-permute-start.18 = (f32[960,256]{1,0:T(8,128)}, f32[960,256]{1,0:T(8,128)}, u32[]{:S(2)}, u32[]{:S(2)}) collective-permute-start(f32[960,256]{1,0:T(8,128)} %get-tuple-element.65.own_ref), channel_id=1, source_target_pairs={{0,8},{8,0},{1,9},{9,1},{2,10},{10,2},{3,11},{11,3},{4,12},{12,4},... | collective-permute-start | bytes 2949128 | tf_op jit(solution)/shard_map/ppermute | solution.py:656
  424.3 285.4 %copy-start.10 = (f32[8,128]{1,0:T(8,128)S(1)}, f32[8,128]{1,0:T(8,128)}, u32[]{:S(2)}) copy-start(f32[8,128]{1,0:T(8,128)} %get-tuple-element.55) | copy-start | bytes 12292
  424.3 300.2 %copy-start.9 = (f32[8,128]{1,0:T(8,128)S(1)}, f32[8,128]{1,0:T(8,128)}, u32[]{:S(2)}) copy-start(f32[8,128]{1,0:T(8,128)} %get-tuple-element.56) | copy-start | bytes 12292
  446.0 281.1 %copy-start = (f32[120,4096]{1,0:T(8,128)}, f32[120,4096]{1,0:T(8,128)S(1)}, u32[]{:S(2)}) copy-start(f32[120,4096]{1,0:T(8,128)S(1)} %add_add_fusion.refs_0_) | copy-start | bytes 5898244
  446.1 229.2 %collective-permute-start.3 = (f32[120,4096]{1,0:T(8,128)S(1)}, f32[120,4096]{1,0:T(8,128)S(1)}, u32[]{:S(2)}, u32[]{:S(2)}) collective-permute-start(f32[120,4096]{1,0:T(8,128)S(1)} %add_add_fusion.refs_0_), channel_id=1, source_target_pairs={{0,4},{1,3},{2,6},{3,1},{4,0},{5,7},{6,2},{7,5},{8,12},{9,11},{10,... | collective-permute-start | bytes 5898248 | tf_op jit(solution)/shard_map/ppermute | solution.py:678
  655.9 24.6 %collective-permute-start.4 = (f32[120,4096]{1,0:T(8,128)S(1)}, f32[120,4096]{1,0:T(8,128)S(1)}, u32[]{:S(2)}, u32[]{:S(2)}) collective-permute-start(f32[120,4096]{1,0:T(8,128)S(1)} %add_add_fusion.refs_0_), channel_id=1, source_target_pairs={{0,2},{1,5},{2,0},{3,7},{4,6},{5,1},{6,4},{7,3},{8,10},{9,13},{10,... | collective-permute-start | bytes 5898248 | tf_op jit(solution)/shard_map/ppermute | solution.py:678
  675.0 5.5 collective-permute-start.6
  675.0 245.2 %collective-permute-start.13 = (f32[960,1536]{1,0:T(8,128)}, f32[960,1536]{1,0:T(8,128)}, u32[]{:S(2)}, u32[]{:S(2)}) collective-permute-start(f32[960,1536]{1,0:T(8,128)} %get-tuple-element.60.own_ref), channel_id=1, source_target_pairs={{0,8},{8,0},{1,9},{9,1},{2,10},{10,2},{3,11},{11,3},{4,12},{12,4},... | collective-permute-start | bytes 17694728 | tf_op jit(solution)/shard_map/ppermute | solution.py:656
  675.3 5.2 copy-start.1
  675.3 26.3 %collective-permute-start.5 = (f32[120,4096]{1,0:T(8,128)S(1)}, f32[120,4096]{1,0:T(8,128)S(1)}, u32[]{:S(2)}, u32[]{:S(2)}) collective-permute-start(f32[120,4096]{1,0:T(8,128)S(1)} %collective-permute-done.3.refs_1_), channel_id=1, source_target_pairs={{0,2},{1,5},{2,0},{3,7},{4,6},{5,1},{6,4},{7,3},{8,10},{9,13},{10,... | collective-permute-start | bytes 5898248 | tf_op jit(solution)/shard_map/ppermute | solution.py:678
  680.5 21.1 %copy-start.2 = (f32[120,4096]{1,0:T(8,128)}, f32[120,4096]{1,0:T(8,128)S(1)}, u32[]{:S(2)}) copy-start(f32[120,4096]{1,0:T(8,128)S(1)} %collective-permute-done.4.refs_2_) | copy-start | bytes 5898244
  680.5 21.1 %collective-permute-start.7 = (f32[120,4096]{1,0:T(8,128)S(1)}, f32[120,4096]{1,0:T(8,128)S(1)}, u32[]{:S(2)}, u32[]{:S(2)}) collective-permute-start(f32[120,4096]{1,0:T(8,128)S(1)} %collective-permute-done.3.refs_1_), channel_id=1, source_target_pairs={{0,1},{1,0},{2,3},{3,2},{4,5},{5,4},{6,7},{7,6},{8,9},{9,8},{10,11... | collective-permute-start | bytes 5898248 | tf_op jit(solution)/shard_map/ppermute | solution.py:678
  680.5 25.0 %copy-start.3 = (f32[120,4096]{1,0:T(8,128)}, f32[120,4096]{1,0:T(8,128)S(1)}, u32[]{:S(2)}) copy-start(f32[120,4096]{1,0:T(8,128)S(1)} %collective-permute-done.6.refs_4_) | copy-start | bytes 5898244
  680.5 209.0 %collective-permute-start.15 = (f32[960,1024]{1,0:T(8,128)}, f32[960,1024]{1,0:T(8,128)}, u32[]{:S(2)}, u32[]{:S(2)}) collective-permute-start(f32[960,1024]{1,0:T(8,128)} %get-tuple-element.62.own_ref), channel_id=1, source_target_pairs={{0,8},{8,0},{1,9},{9,1},{2,10},{10,2},{3,11},{11,3},{4,12},{12,4},... | collective-permute-start | bytes 11796488 | tf_op jit(solution)/shard_map/ppermute | solution.py:656
  701.6 4.0 copy-start.4
  701.6 4.0 collective-permute-start.8
  701.6 6.8 copy-start.5
  701.6 6.8 collective-permute-start.9
  705.6 2.8 copy-start.6
  705.6 225.4 %collective-permute-start.12 = (f32[960,256]{1,0:T(8,128)}, f32[960,256]{1,0:T(8,128)}, u32[]{:S(2)}, u32[]{:S(2)}) collective-permute-start(f32[960,256]{1,0:T(8,128)} %get-tuple-element.59.own_ref), channel_id=1, source_target_pairs={{0,8},{8,0},{1,9},{9,1},{2,10},{10,2},{3,11},{11,3},{4,12},{12,4},... | collective-permute-start | bytes 2949128 | tf_op jit(solution)/shard_map/ppermute | solution.py:656
  708.4 1.3 copy-start.7
  708.4 225.6 %collective-permute-start.11 = (f32[960,256]{1,0:T(8,128)}, f32[960,256]{1,0:T(8,128)}, u32[]{:S(2)}, u32[]{:S(2)}) collective-permute-start(f32[960,256]{1,0:T(8,128)} %get-tuple-element.58.own_ref), channel_id=1, source_target_pairs={{0,8},{8,0},{1,9},{9,1},{2,10},{10,2},{3,11},{11,3},{4,12},{12,4},... | collective-permute-start | bytes 2949128 | tf_op jit(solution)/shard_map/ppermute | solution.py:656
  889.6 43.8 %collective-permute-start.10 = (f32[1024]{0:T(1024)S(1)}, f32[1024]{0:T(1024)S(1)}, u32[]{:S(2)}, u32[]{:S(2)}) collective-permute-start(f32[1024]{0:T(1024)S(1)} %concatenate.3), channel_id=1, source_target_pairs={{0,8},{8,0},{1,9},{9,1},{2,10},{10,2},{3,11},{11,3},{4,12},{12,4},... | collective-permute-start | bytes 12296 | tf_op jit(solution)/shard_map/ppermute | solution.py:687
  933.3 0.6 copy-start.8

commit v3 on v2

--- a/solution.py
+++ b/solution.py
@@ -17,18 +17,17 @@
 RUN = 16
 STOK = 256
 COL = 512
-BACK = 512
 GCOL = 256
-CHUNKS = (256, 256, 512, 1024, 2048, 1536, 256, 256)
+CHUNKS = (256, 256, 512, 1024, 2048, 1536, 384, 128)
 VMEM_LIMIT = 62 * 1024 * 1024
 MESH = pl.DeviceIdType.MESH
 NT = (((1,), (1,)), ((), ()))
 NN = (((1,), (0,)), ((), ()))
 
 
-def stats_kernel(mask_ref, gain_ref, hid_hbm, tab_hbm, tea_hbm, x_hbm, xt_hbm, out_ref,
-                 hid_buf, x_buf, xt_buf, tab_buf, tea_buf, rows_ref, z0_ref, z1_ref, acc_ref, sum_ref, gain_buf, flag_buf,
-                 flags, order, hid_sem, tab_sem, tea_sem, flag_sem, out_sem):
+def stats_kernel(mask_hbm, gain_hbm, hid_hbm, tab_hbm, tea_hbm, x_hbm, xt_hbm, out_ref,
+                 mask_buf, row_buf, hid_buf, x_buf, xt_buf, tab_buf, tea_buf, rows_ref, z0_ref, z1_ref, acc_ref, sum_ref, gain_buf, flag_buf,
+                 flags, order, hid_sem, tab_sem, tea_sem, flag_sem, row_sem, out_sem):
     z_refs = (z0_ref, z1_ref)
     dim, tokens = hid_hbm.shape
     count = tab_hbm.shape[1] // COL
@@ -44,35 +43,26 @@
         cols = pl.ds(i * COL, COL)
         return pltpu.make_async_copy(tab_hbm.at[:, cols], tab_buf.at[:, cols], tab_sem)
 
+    mask_copy = pltpu.make_async_copy(mask_hbm, mask_buf, flag_sem)
+    row_copy = pltpu.make_async_copy(gain_hbm, row_buf, row_sem)
+    mask_copy.start()
+    row_copy.start()
     for i in range(slabs):
         hid_copy(i).start()
     for i in range(count):
         tab_copy(i).start()
 
-    flag = mask_ref[...]
+    mask_copy.wait()
+    flag = mask_buf[...]
     for shift in (1, 2, 4, 8):
         flag = jnp.maximum(flag, pltpu.roll(flag, 128 - shift, 1))
     flag_buf[...] = (flag > 0).astype(jnp.int32)
     flag_copy = pltpu.make_async_copy(flag_buf, flags, flag_sem)
     flag_copy.start()
-    gain_buf[...] = jnp.broadcast_to(1.0 + gain_ref[...], (128, dim)).T
+    row_copy.wait()
+    gain_buf[...] = jnp.broadcast_to(1.0 + row_buf[...], (128, dim)).T
     sum_ref[...] = jnp.ones_like(sum_ref)
     flag_copy.wait()
-
-    def mark(r, found):
-        order[found] = r
-        return found + flags[lax.div(r, 128 // RUN), lax.rem(r, 128 // RUN) * RUN]
-
-    found = lax.fori_loop(0, runs, mark, 0)
-    last = order[jnp.maximum(found - 1, 0)]
-    last = jnp.where(found > 0, last, 0)
-
-    def fill(k, _):
-        order[found + k] = last
-        return 0
-
-    lax.fori_loop(0, 2 * per, fill, 0)
-    blocks = lax.div(found + per - 1, per)
 
     def tea_start(b):
         slot = lax.rem(b, 2)
@@ -89,12 +79,12 @@
         slot = lax.rem(b, 2)
         pltpu.make_async_copy(tea_hbm.at[pl.ds(0, STOK), :], tea_buf.at[slot], tea_sem.at[slot]).wait()
 
-    @pl.when(blocks > 0)
-    def _():
-        tea_start(0)
-
-    def slab(i, _):
+    def slab(i, found, marks):
         pltpu.make_async_copy(hid_hbm.at[:, pl.ds(0, TOK)], hid_buf.at[:, pl.ds(0, TOK)], hid_sem.at[i]).wait()
+        for r in range(marks):
+            run = i * marks + r
+            order[found] = run
+            found = found + flags[lax.div(i * marks, 128 // RUN) + r // (128 // RUN), r % (128 // RUN) * RUN]
         for b in range(LINES):
             lanes = pl.ds(pl.multiple_of(i * TOK + b * 128, 128), 128)
             hid = hid_buf[:, lanes].astype(jnp.float32)
@@ -102,9 +92,21 @@
             xb = (hid * inv_rms * gain_buf[...]).astype(jnp.bfloat16)
             xt_buf[:, lanes] = xb
             x_buf[lanes, :] = xb.T
-        return 0
-
-    lax.fori_loop(0, slabs, slab, 0)
+        return found
+
+    early = slabs // 2
+    found = lax.fori_loop(0, early, lambda i, found: slab(i, found, runs // early), 0)
+    last = order[jnp.maximum(found - 1, 0)]
+    last = jnp.where(found > 0, last, 0)
+    for k in range(2 * per):
+        order[found + k] = last
+    blocks = lax.div(found + per - 1, per)
+
+    @pl.when(blocks > 0)
+    def _():
+        tea_start(0)
+
+    lax.fori_loop(early, slabs, lambda i, _: slab(i, 0, 0), 0)
     x_out = pltpu.make_async_copy(x_buf, x_hbm, out_sem.at[0])
     xt_out = pltpu.make_async_copy(xt_buf, xt_hbm, out_sem.at[1])
     x_out.start()
@@ -146,11 +148,11 @@
             tea_start(b + 1)
 
         tea_wait(b)
-        gather(b + 1)
         for n in range(count):
             if n + 1 < count:
                 logits(b, n + 1, (n + 1) % 2)
             else:
+                gather(b + 1)
                 logits(b + 1, 0, 0)
             collect(b, n, n % 2)
         for k in range(per):
@@ -182,7 +184,7 @@
     per = STOK // RUN
     return pl.pallas_call(
         stats_kernel,
-        in_specs=[vmem, vmem, hbm, hbm, hbm],
+        in_specs=[hbm] * 5,
         out_specs=[hbm, hbm, vmem],
         out_shape=[
             jax.ShapeDtypeStruct((tokens, dim), jnp.bfloat16),
@@ -190,6 +192,8 @@
             jax.ShapeDtypeStruct((tokens // 64, 128), jnp.float32),
         ],
         scratch_shapes=[
+            pltpu.VMEM(mask_lines.shape, jnp.float32),
+            pltpu.VMEM((1, dim), jnp.float32),
             pltpu.VMEM((dim, tokens), jnp.bfloat16),
             pltpu.VMEM((tokens, dim), jnp.bfloat16),
             pltpu.VMEM((dim, tokens), jnp.bfloat16),
@@ -208,6 +212,7 @@
             pltpu.SemaphoreType.DMA,
             pltpu.SemaphoreType.DMA((2,)),
             pltpu.SemaphoreType.DMA,
+            pltpu.SemaphoreType.DMA,
             pltpu.SemaphoreType.DMA((2,)),
         ],
         compiler_params=pltpu.CompilerParams(vmem_limit_bytes=VMEM_LIMIT),
@@ -216,14 +221,18 @@
     )(mask_lines, gain_row, hid_t, tab_t, tea_rows)
 
 
-def first_kernel(tp, stats_ref, mask_ref, x_hbm, xt_hbm, tab_hbm, tea_hbm, ab_ref, log_ref, table_ref, g_ref, kl_ref,
-                 slots, mask_slot, x_buf, xt_buf, tab_buf, tea_buf, z0_ref, z1_ref, stu_ref, tea_ref, gap_ref, coef0_ref, coef1_ref,
-                 send_sem, recv_sem, msend_sem, mrecv_sem, x_sem, xt_sem, tab_sem, tea_sem):
+def first_kernel(tp, stats_hbm, mask_hbm, x_hbm, xt_hbm, tab_hbm, tea_hbm, ab_ref, log_ref, table_ref, g_hbm, kl_ref,
+                 stats_ref, mask_ref, g_ref, slots, mask_slot, x_buf, xt_buf, tab_buf, tea_buf, z0_ref, z1_ref, stu_ref, tea_ref, gap_ref, coef0_ref, coef1_ref,
+                 send_sem, recv_sem, msend_sem, mrecv_sem, stats_sem, mask_sem, x_sem, xt_sem, tab_sem, tea_sem, g_sem):
     dp_me = lax.axis_index("dp")
     me = lax.axis_index("tp")
     tokens, width = g_ref.shape
     blocks = tokens // TOK
 
+    def g_copy(m):
+        rows = pl.ds(pl.multiple_of(m * TOK, TOK), TOK)
+        return pltpu.make_async_copy(g_ref.at[rows, :], g_hbm.at[rows, :], g_sem)
+
     def x_copy(m):
         rows = pl.ds(m * TOK, TOK)
         return pltpu.make_async_copy(x_hbm.at[rows, :], x_buf.at[rows, :], x_sem.at[m])
@@ -231,29 +240,20 @@
     tab_copy = pltpu.make_async_copy(tab_hbm.at[:, pl.ds(0, width)], tab_buf, tab_sem)
     tea_copy = pltpu.make_async_copy(tea_hbm.at[:, pl.ds(0, width)], tea_buf, tea_sem)
     xt_copy = pltpu.make_async_copy(xt_hbm, xt_buf, xt_sem)
+    stats_copy = pltpu.make_async_copy(stats_hbm, stats_ref, stats_sem)
+    mask_copy = pltpu.make_async_copy(mask_hbm, mask_ref, mask_sem)
+    barrier = pltpu.get_barrier_semaphore()
+    for d in range(1, tp):
+        pl.semaphore_signal(barrier, inc=1, device_id=(dp_me, lax.rem(me + d, tp)), device_id_type=MESH)
+    pl.semaphore_signal(barrier, inc=1, device_id=(1 - dp_me, me), device_id_type=MESH)
+    stats_copy.start()
+    mask_copy.start()
     tab_copy.start()
     x_copy(0).start()
     tea_copy.start()
     for m in range(1, blocks):
         x_copy(m).start()
     xt_copy.start()
-
-    barrier = pltpu.get_barrier_semaphore()
-    for d in range(1, tp):
-        pl.semaphore_signal(barrier, inc=1, device_id=(dp_me, lax.rem(me + d, tp)), device_id_type=MESH)
-    pl.semaphore_signal(barrier, inc=1, device_id=(1 - dp_me, me), device_id_type=MESH)
-    pl.semaphore_wait(barrier, tp)
-    copies = []
-    for d in range(1, tp):
-        copies.append(pltpu.make_async_remote_copy(
-            src_ref=stats_ref, dst_ref=slots.at[me], send_sem=send_sem.at[d], recv_sem=recv_sem.at[d],
-            device_id=(dp_me, lax.rem(me + d, tp)), device_id_type=MESH))
-    copies.append(pltpu.make_async_remote_copy(
-        src_ref=mask_ref, dst_ref=mask_slot, send_sem=msend_sem, recv_sem=mrecv_sem,
-        device_id=(1 - dp_me, me), device_id_type=MESH))
-    for copy in copies:
-        copy.start()
-    slots[me] = stats_ref[...]
 
     z_refs = (z0_ref, z1_ref)
 
@@ -276,6 +276,20 @@
                 gap += eb * (tt - ts)
             gap_ref[rows, :] = gap
 
+    stats_copy.wait()
+    mask_copy.wait()
+    pl.semaphore_wait(barrier, tp)
+    copies = []
+    for d in range(1, tp):
+        copies.append(pltpu.make_async_remote_copy(
+            src_ref=stats_ref, dst_ref=slots.at[me], send_sem=send_sem.at[d], recv_sem=recv_sem.at[d],
+            device_id=(dp_me, lax.rem(me + d, tp)), device_id_type=MESH))
+    copies.append(pltpu.make_async_remote_copy(
+        src_ref=mask_ref, dst_ref=mask_slot, send_sem=msend_sem, recv_sem=mrecv_sem,
+        device_id=(1 - dp_me, me), device_id_type=MESH))
+    for copy in copies:
+        copy.start()
+    slots[me] = stats_ref[...]
     tab_copy.wait()
     x_copy(0).wait()
     tea_copy.wait()
@@ -348,12 +362,17 @@
             spread(m, par)
             weigh(m - 1, 1 - par)
             product(m - 2)
+        g_copy(2 * p - 2).start()
+        g_copy(2 * p - 1).start()
         return 0
 
     lax.fori_loop(1, blocks // 2, behind, 0)
     weigh(blocks - 1, 1)
     product(blocks - 2)
     product(blocks - 1)
+    g_copy(blocks - 2).start()
+    g_copy(blocks - 1).start()
+    pltpu.make_async_copy(g_ref, g_hbm, g_sem).wait()
 
 
 def first_call(stats, mask_lines, x_rows, x_t, tab_t, tea_rows, width, tp):
@@ -363,8 +382,8 @@
     blocks = tokens // TOK
     return pl.pallas_call(
         functools.partial(first_kernel, tp),
-        in_specs=[whole, whole, hbm, hbm, hbm, hbm],
-        out_specs=[whole] * 5,
+        in_specs=[hbm] * 6,
+        out_specs=[whole, whole, whole, hbm, whole],
         out_shape=[
             jax.ShapeDtypeStruct(stats.shape, jnp.float32),
             jax.ShapeDtypeStruct((8, 128), jnp.float32),
@@ -373,6 +392,9 @@
             jax.ShapeDtypeStruct((8, 128), jnp.float32),
         ],
         scratch_shapes=[
+            pltpu.VMEM(stats.shape, jnp.float32),
+            pltpu.VMEM(mask_lines.shape, jnp.float32),
+            pltpu.VMEM((tokens, width), jnp.bfloat16),
             pltpu.VMEM((tp,) + stats.shape, jnp.float32),
             pltpu.VMEM(mask_lines.shape, jnp.float32),
             pltpu.VMEM((tokens, dim), jnp.bfloat16),
@@ -390,7 +412,10 @@
             pltpu.SemaphoreType.DMA((tp,)),
             pltpu.SemaphoreType.DMA,
             pltpu.SemaphoreType.DMA,
+            pltpu.SemaphoreType.DMA,
+            pltpu.SemaphoreType.DMA,
             pltpu.SemaphoreType.DMA((blocks,)),
+            pltpu.SemaphoreType.DMA,
             pltpu.SemaphoreType.DMA,
             pltpu.SemaphoreType.DMA,
             pltpu.SemaphoreType.DMA,
@@ -401,11 +426,7 @@
     )(stats, mask_lines, x_rows, x_t, tab_t, tea_rows)
 
 
-def grad_kernel(first, ab_ref, x_ref, xt_ref, tab_ref, tea_ref, *refs):
-    if first:
-        table_ref, g_ref, kl_ref, z0_ref, z1_ref, coef_ref = refs
-    else:
-        kl_in_ref, table_ref, g_ref, kl_ref, z0_ref, z1_ref, coef_ref = refs
+def grad_kernel(ab_ref, x_ref, xt_ref, tab_ref, tea_ref, kl_in_ref, table_ref, g_ref, kl_ref, z0_ref, z1_ref, coef_ref):
     z_refs = (z0_ref, z1_ref)
     col = z0_ref.shape[1]
     count = tab_ref.shape[1] // col
@@ -414,7 +435,7 @@
     @pl.when(block == 0)
     def _():
         table_ref[...] = jnp.zeros_like(table_ref)
-        kl_ref[...] = jnp.zeros_like(kl_ref) if first else kl_in_ref[...]
+        kl_ref[...] = kl_in_ref[...]
 
     for k in range(2):
         for b in range(LINES):
@@ -428,9 +449,7 @@
         z_refs[par][...] = lax.dot_general(x_ref[...], tab_ref[:, columns(n)], NN, preferred_element_type=jnp.float32)
 
     def weigh(n, par):
-        kl_acc = kl_ref[...]
-        for r in range(0, TOK, 64):
-            rows = slice(r, r + 64)
+        def strip(rows, kl_acc):
             a = coef_ref[0, rows, :]
             b = coef_ref[1, rows, :]
             for q in range(col // 128):
@@ -445,7 +464,15 @@
                 for w in range(0, 64, 8):
                     kl_acc += kl[w:w + 8]
                 g_ref[rows, lanes] = ((pa - pb) * (1.0 - ts * ts)).astype(jnp.bfloat16)
-        kl_ref[...] = kl_acc
+            return kl_acc
+
+        if count <= 2:
+            kl_ref[...] = lax.fori_loop(0, TOK // 64, lambda r, acc: strip(pl.ds(pl.multiple_of(r * 64, 64), 64), acc), kl_ref[...])
+        else:
+            kl_acc = kl_ref[...]
+            for r in range(0, TOK, 64):
+                kl_acc = strip(slice(r, r + 64), kl_acc)
+            kl_ref[...] = kl_acc
 
     def product(n):
         table_ref[:, columns(n)] += lax.dot_general(xt_ref[...], g_ref[:, columns(n)], NN, preferred_element_type=jnp.float32)
@@ -477,42 +504,36 @@
 
 def grad_call(ab, x_rows, x_t, tab_t, tea_rows, start, size, kl):
     tokens, dim = x_rows.shape
-    first = kl is None
-    col = min(GCOL, size)
-    assert size == col or size % (2 * col) == 0
-    in_specs = [
-        pl.BlockSpec(ab.shape, lambda i: (0, 0)),
-        pl.BlockSpec((TOK, dim), lambda i: (i, 0)),
-        pl.BlockSpec((dim, TOK), lambda i: (0, i)),
-        pl.BlockSpec((pl.Element(dim), pl.Element(size)), lambda i: (0, start), pipeline_mode=pl.Buffered(1)),
-        pl.BlockSpec((pl.Element(TOK), pl.Element(size)), lambda i: (i * TOK, start)),
-    ]
-    operands = [ab, x_rows, x_t, tab_t, tea_rows]
-    if not first:
-        in_specs.append(pl.BlockSpec((8, 128), lambda i: (0, 0)))
-        operands.append(kl)
+    col = GCOL if size % (2 * GCOL) == 0 else size
     return pl.pallas_call(
-        functools.partial(grad_kernel, first),
+        grad_kernel,
         grid=(tokens // TOK,),
-        in_specs=in_specs,
+        in_specs=[
+            pl.BlockSpec(ab.shape, lambda i: (0, 0)),
+            pl.BlockSpec((TOK, dim), lambda i: (i, 0)),
+            pl.BlockSpec((dim, TOK), lambda i: (0, i)),
+            pl.BlockSpec((pl.Element(dim), pl.Element(size)), lambda i: (0, start), pipeline_mode=pl.Buffered(1)),
+            pl.BlockSpec((pl.Element(TOK), pl.Element(size)), lambda i: (i * TOK, start)),
+            pl.BlockSpec((8, 128), lambda i: (0, 0)),
+        ],
         out_specs=[
             pl.BlockSpec((dim, size), lambda i: (0, 0)),
             pl.BlockSpec((TOK, size), lambda i: (i, 0)),
             pl.BlockSpec((8, 128), lambda i: (0, 0)),
+        ],
+        scratch_shapes=[
+            pltpu.VMEM((TOK, col), jnp.float32),
+            pltpu.VMEM((TOK, col), jnp.float32),
+            pltpu.VMEM((2, TOK, 128), jnp.float32),
         ],
         out_shape=[
             jax.ShapeDtypeStruct((dim, size), jnp.float32),
             jax.ShapeDtypeStruct((tokens, size), jnp.bfloat16),
             jax.ShapeDtypeStruct((8, 128), jnp.float32),
         ],
-        scratch_shapes=[
-            pltpu.VMEM((TOK, col), jnp.float32),
-            pltpu.VMEM((TOK, col), jnp.float32),
-            pltpu.VMEM((2, TOK, 128), jnp.float32),
-        ],
         compiler_params=pltpu.CompilerParams(vmem_limit_bytes=VMEM_LIMIT),
         cost_estimate=pl.CostEstimate(flops=4 * tokens * size * dim, bytes_accessed=4 * tokens * size, transcendentals=0),
-    )(*operands)
+    )(ab, x_rows, x_t, tab_t, tea_rows, kl)
 
 
 def back_kernel(half_ref, tab_ref, *refs):
@@ -520,7 +541,8 @@
     start = 0
     for g_ref in g_refs:
         size = g_ref.shape[1]
-        step = min(BACK, size)
+        step = min(size, 1024 if size % 1024 == 0 else 768)
+        assert size % step == 0
         for n in range(size // step):
             cols = slice(start + n * step, start + (n + 1) * step)
             dx = lax.dot_general(tab_ref[:, cols], g_ref[:, n * step:(n + 1) * step], NT, preferred_element_type=jnp.float32)

time: 938 us -> 969 us (1.033)
  Pallas kernels: 420 us -> 447 us
    pallas_call x9, Pallas kernels: 292 us -> 316 us  [the longest x7 228 us: grad_call(): pl.pallas_call(grad_kernel, grid=(tokens // TOK,), in_specs=[pl.BlockSpec...]
where the time goes in v3:
time: 969 us; the launch traced here: 963 us
  waiting for transfers between devices  464 us (48%)
  Pallas kernels  447 us (46%)
  other arithmetic  18.6 us (2%)
  starting transfers between devices  15 us (2%)
  blocking collectives  13.5 us (1%)
    ppermute x8, waiting for transfers between devices, local_step(): recv = lax.ppermute(table_c, 'dp', swap)  368 us
    pallas_call x7, Pallas kernels, grad_call(): pl.pallas_call(grad_kernel, grid=(tokens // TOK,), in_specs=[pl.BlockSpec...  228 us
    pallas_call x1, Pallas kernels, stats_call(): pl.pallas_call(stats_kernel, in_specs=[hbm] * 5, out_specs=[hbm, hbm, vme...  71.1 us
    pallas_call x2, Pallas kernels, back_call(): pl.pallas_call(back_kernel, grid_spec=pltpu.PrefetchScalarGridSpec(num_sc...  67.4 us
    ppermute x2, waiting for transfers between devices, local_step(): away = lax.ppermute(away, 'tp', perms[s])  64.7 us
    pallas_call x8, Pallas kernels, add_call(): pl.pallas_call(add_kernel, grid=(size // step,), in_specs=in_specs, out_s...  46.6 us
    ppermute x7, waiting for transfers between devices, local_step(): pieces += [lax.ppermute(piece, 'tp', perms[s]) for piece in pieces]  31.5 us
  transfers between devices with their start and end apart: 19, of which 9 were waited for; matrix products, arithmetic and copies ran while one was open for 1% of the time, Pallas kernels for 10%

profile of v3, /device:TPU:0, one launch (start us, length us, event | category | flops | bytes accessed | tf_op | source)
XLA Modules:
  0.0 963.3 jit_solution(11884421032467290335)
XLA Ops:
  0.6 71.1 %stats.1 = (bf16[4096,960]{1,0:T(8,128)(2,1)}, bf16[960,4096]{1,0:T(8,128)(2,1)}, f32[64,128]{1,0:T(8,128)}) custom-call(f32[32,128]{1,0:T(8,128)} %bitcast.33, f32[1,960]{1,0:T(1,128)} %bitcast.36, bf16[960,4096]{1,0:T(8,128)(2,1)} %bitcast.30, bf16[960,6144]{1,0:T(8,128)(2,1)} %bitcast.19, bf16[4096,6144]{1,0:T(8,128)(2,1)} %tea_ref.13), custom_call_target="tpu_custom_call" | custom-call | flops 48318382080 | bytes 50331648 | tf_op jit(solution)/shard_map/stats/pallas_call | solution.py:185
  71.7 16.4 %first.1 = (f32[64,128]{1,0:T(8,128)}, f32[8,128]{1,0:T(8,128)}, f32[960,256]{1,0:T(8,128)}, bf16[4096,256]{1,0:T(8,128)(2,1)}, f32[8,128]{1,0:T(8,128)}) custom-call(f32[64,128]{1,0:T(8,128)} %get-tuple-element.35.stats_hbm, f32[32,128]{1,0:T(8,128)} %bitcast.34, bf16[4096,960]{1,0:T(8,128)(2,1)} %get-tuple-element.36.x_hbm.x_ref, ...), custom_call_target="tpu_custom_call" | custom-call | flops 4026531840 | bytes 15728640 | tf_op jit(solution)/shard_map/first/pallas_call | solution.py:383
  88.2 17.9 %shard_map.84 = (f32[960,256]{1,0:T(8,128)}, bf16[4096,256]{1,0:T(8,128)(2,1)}, f32[8,128]{1,0:T(8,128)}) custom-call(f32[64,128]{1,0:T(8,128)} %get-tuple-element.39.ab_ref, bf16[4096,960]{1,0:T(8,128)(2,1)} %get-tuple-element.36.x_hbm.x_ref, bf16[960,4096]{1,0:T(8,128)(2,1)} %get-tuple-element.37.xt_hbm.xt_ref, bf16[960,6144]{1,0:T(8,128)(2,1)} %bitcast.21, ...), custom_call_target="tpu_custom_call" | custom-call | flops 4026531840 | bytes 4194304 | tf_op jit(solution)/shard_map/pallas_call | solution.py:508
  106.1 27.4 %shard_map.85 = (f32[960,512]{1,0:T(8,128)}, bf16[4096,512]{1,0:T(8,128)(2,1)}, f32[8,128]{1,0:T(8,128)}) custom-call(f32[64,128]{1,0:T(8,128)} %get-tuple-element.39.ab_ref, bf16[4096,960]{1,0:T(8,128)(2,1)} %get-tuple-element.36.x_hbm.x_ref, bf16[960,4096]{1,0:T(8,128)(2,1)} %get-tuple-element.37.xt_hbm.xt_ref, bf16[960,6144]{1,0:T(8,128)(2,1)} %bitcast.22, ...), custom_call_target="tpu_custom_call" | custom-call | flops 8053063680 | bytes 8388608 | tf_op jit(solution)/shard_map/pallas_call | solution.py:508
  133.4 30.2 %shard_map.86 = (f32[960,1024]{1,0:T(8,128)}, bf16[4096,1024]{1,0:T(8,128)(2,1)}, f32[8,128]{1,0:T(8,128)}) custom-call(f32[64,128]{1,0:T(8,128)} %get-tuple-element.39.ab_ref, bf16[4096,960]{1,0:T(8,128)(2,1)} %get-tuple-element.36.x_hbm.x_ref, bf16[960,4096]{1,0:T(8,128)(2,1)} %get-tuple-element.37.xt_hbm.xt_ref, bf16[960,6144]{1,0:T(8,128)(2,1)} %bitcast.23, ...), custom_call_target="tpu_custom_call" | custom-call | flops 16106127360 | bytes 16777216 | tf_op jit(solution)/shard_map/pallas_call | solution.py:508
  163.6 67.1 %shard_map.87 = (f32[960,2048]{1,0:T(8,128)}, bf16[4096,2048]{1,0:T(8,128)(2,1)}, f32[8,128]{1,0:T(8,128)}) custom-call(f32[64,128]{1,0:T(8,128)} %get-tuple-element.39.ab_ref, bf16[4096,960]{1,0:T(8,128)(2,1)} %get-tuple-element.36.x_hbm.x_ref, bf16[960,4096]{1,0:T(8,128)(2,1)} %get-tuple-element.37.xt_hbm.xt_ref, bf16[960,6144]{1,0:T(8,128)(2,1)} %bitcast.24, ...), custom_call_target="tpu_custom_call" | custom-call | flops 32212254720 | bytes 33554432 | tf_op jit(solution)/shard_map/pallas_call | solution.py:508
  230.7 50.0 %shard_map.88 = (f32[960,1536]{1,0:T(8,128)}, bf16[4096,1536]{1,0:T(8,128)(2,1)}, f32[8,128]{1,0:T(8,128)}) custom-call(f32[64,128]{1,0:T(8,128)} %get-tuple-element.39.ab_ref, bf16[4096,960]{1,0:T(8,128)(2,1)} %get-tuple-element.36.x_hbm.x_ref, bf16[960,4096]{1,0:T(8,128)(2,1)} %get-tuple-element.37.xt_hbm.xt_ref, bf16[960,6144]{1,0:T(8,128)(2,1)} %bitcast.25, ...), custom_call_target="tpu_custom_call" | custom-call | flops 24159191040 | bytes 25165824 | tf_op jit(solution)/shard_map/pallas_call | solution.py:508
  280.7 19.8 %shard_map.89 = (f32[960,384]{1,0:T(8,128)}, bf16[4096,384]{1,0:T(8,128)(2,1)}, f32[8,128]{1,0:T(8,128)}) custom-call(f32[64,128]{1,0:T(8,128)} %get-tuple-element.39.ab_ref, bf16[4096,960]{1,0:T(8,128)(2,1)} %get-tuple-element.36.x_hbm.x_ref, bf16[960,4096]{1,0:T(8,128)(2,1)} %get-tuple-element.37.xt_hbm.xt_ref, bf16[960,6144]{1,0:T(8,128)(2,1)} %bitcast.26, ...), custom_call_target="tpu_custom_call" | custom-call | flops 6039797760 | bytes 6291456 | tf_op jit(solution)/shard_map/pallas_call | solution.py:508
  300.5 15.9 %shard_map.90 = (f32[960,128]{1,0:T(8,128)}, bf16[4096,128]{1,0:T(8,128)(2,1)}, f32[8,128]{1,0:T(8,128)}) custom-call(f32[64,128]{1,0:T(8,128)} %get-tuple-element.39.ab_ref, bf16[4096,960]{1,0:T(8,128)(2,1)} %get-tuple-element.36.x_hbm.x_ref, bf16[960,4096]{1,0:T(8,128)(2,1)} %get-tuple-element.37.xt_hbm.xt_ref, bf16[960,6144]{1,0:T(8,128)(2,1)} %bitcast.27, ...), custom_call_target="tpu_custom_call" | custom-call | flops 2013265920 | bytes 2097152 | tf_op jit(solution)/shard_map/pallas_call | solution.py:508
  316.4 33.6 %back.3 = f32[480,4096]{1,0:T(8,128)} custom-call(s32[1]{0:T(128)} %bitcast.13.half_ref, bf16[960,6144]{1,0:T(8,128)(2,1)} %bitcast.28, bf16[4096,256]{1,0:T(8,128)(2,1)} %get-tuple-element.38.refs_0_, bf16[4096,256]{1,0:T(8,128)(2,1)} %get-tuple-element.41.refs_1_, bf16[4096,512]{1,0:T(8,128)(2,1)} %get-tuple-element.43.refs_2_, ...), custom_call_target="tpu_custom_call" | custom-call | flops 24159191040 | bytes 50331648 | tf_op jit(solution)/shard_map/back/pallas_call | solution.py:560
  350.0 0.5 collective-permute-start
  350.6 33.8 %back.2 = f32[480,4096]{1,0:T(8,128)} custom-call(s32[1]{0:T(128)} %bitcast.10.half_ref, bf16[960,6144]{1,0:T(8,128)(2,1)} %bitcast.29, bf16[4096,256]{1,0:T(8,128)(2,1)} %get-tuple-element.38.refs_0_, bf16[4096,256]{1,0:T(8,128)(2,1)} %get-tuple-element.41.refs_1_, bf16[4096,512]{1,0:T(8,128)(2,1)} %get-tuple-element.43.refs_2_, ...), custom_call_target="tpu_custom_call" | custom-call | flops 24159191040 | bytes 50331648 | tf_op jit(solution)/shard_map/back/pallas_call | solution.py:560
  384.3 10.7 %dynamic-slice_add_fusion.1 = (f32[240,4096]{1,0:T(8,128)}, f32[240,4096]{1,0:T(8,128)}) fusion(f32[480,4096]{1,0:T(8,128)} %collective-permute-done, s32[]{:T(128)S(6)} %select_n.25, f32[480,4096]{1,0:T(8,128)} %back.2, s32[]{:T(128)S(6)} %select_n.27), kind=kLoop, calls=%fused_computation.1 | loop fusion | flops 1966080 | bytes 23592968 | tf_op jit(solution)/shard_map/add | solution.py:695
  395.1 2.5 collective-permute-start.1
  397.6 44.0 %collective-permute-done.1 = f32[240,4096]{1,0:T(8,128)} collective-permute-done((f32[240,4096]{1,0:T(8,128)}, f32[240,4096]{1,0:T(8,128)}, u32[]{:S(2)}, u32[]{:S(2)}) %collective-permute-start.1) | collective-permute-done | bytes 3932192 | tf_op jit(solution)/shard_map/ppermute | solution.py:693
  441.6 2.3 dynamic-slice_add_fusion.2
  443.9 2.1 collective-permute-start.2
  446.0 2.0 collective-permute-start.16
  448.1 20.7 %collective-permute-done.2 = f32[120,4096]{1,0:T(8,128)} collective-permute-done((f32[120,4096]{1,0:T(8,128)S(1)}, f32[120,4096]{1,0:T(8,128)}, u32[]{:S(2)}, u32[]{:S(2)}) %collective-permute-start.2) | collective-permute-done | bytes 1966112 | tf_op jit(solution)/shard_map/ppermute | solution.py:693
  468.7 3.1 add_add_fusion.refs_0_
  471.8 2.1 collective-permute-start.3
  473.9 2.0 collective-permute-start.18
  475.9 205.7 %collective-permute-done.17.recv_ref = f32[960,256]{1,0:T(8,128)} collective-permute-done((f32[960,256]{1,0:T(8,128)S(1)}, f32[960,256]{1,0:T(8,128)}, u32[]{:S(2)}, u32[]{:S(2)}) %collective-permute-start.17) | collective-permute-done | bytes 983072 | tf_op jit(solution)/shard_map/ppermute | solution.py:678
  681.6 1.5 collective-permute-start.4
  683.1 17.9 %collective-permute-done.18.recv_ref = f32[960,256]{1,0:T(8,128)} collective-permute-done((f32[960,256]{1,0:T(8,128)S(1)}, f32[960,256]{1,0:T(8,128)}, u32[]{:S(2)}, u32[]{:S(2)}) %collective-permute-start.18) | collective-permute-done | bytes 983072 | tf_op jit(solution)/shard_map/ppermute | solution.py:678
  701.6 4.6 collective-permute-done.4.refs_2_
  706.3 21.0 %collective-permute-done.5.refs_3_ = f32[120,4096]{1,0:T(8,128)S(1)} collective-permute-done((f32[120,4096]{1,0:T(8,128)S(1)}, f32[120,4096]{1,0:T(8,128)S(1)}, u32[]{:S(2)}, u32[]{:S(2)}) %collective-permute-start.5) | collective-permute-done | bytes 1966112 | tf_op jit(solution)/shard_map/ppermute | solution.py:700
  727.4 0.5 collective-permute-start.9
  727.9 3.4 collective-permute-done.8.refs_6_
  731.7 2.4 collective-permute-done.9.refs_7_
  734.1 0.4 collective-permute-start.11
  734.5 0.9 copy-done.7
  735.4 0.6 reduce_sum.28
  736.7 13.5 %psum.7 = f32[]{:T(128)} all-reduce(f32[]{:T(128)S(6)} %mul_shard_map.3), channel_id=1, replica_groups=mesh['dp'=2,'tp'=8] {'tp'}, use_global_device_ids=true, to_apply=%region_2.3 | all-reduce | flops 1 | bytes 8 | tf_op jit(solution)/shard_map/psum | solution.py:706
  750.2 0.7 reduce_sum.29
  752.2 0.6 stack.35.off_ref
  752.8 17.5 %finish.1 = (bf16[960,4096]{1,0:T(8,128)(2,1)}, f32[960,128]{1,0:T(8,128)}) custom-call(s32[8]{0:T(128)} %stack.35.off_ref, bf16[960,4096]{1,0:T(8,128)(2,1)} %bitcast.31, f32[1,960]{1,0:T(1,128)} %bitcast.37, f32[120,4096]{1,0:T(8,128)} %copy-done, f32[120,4096]{1,0:T(8,128)} %copy-done.1, f32[120,4096]{1,0:T(8,128)} %copy-done.2, f32[120,4096]{1,0:T(8,128)} %copy-done.4, ...), custom_call_target="tpu_custom_call" | custom-call | flops 39321600 | bytes 31457280 | tf_op jit(solution)/shard_map/finish/pallas_call | solution.py:605
  770.3 1.2 reduce_sum.27
  771.6 144.0 %collective-permute-done.15.recv_ref = f32[960,1024]{1,0:T(8,128)} collective-permute-done((f32[960,1024]{1,0:T(8,128)}, f32[960,1024]{1,0:T(8,128)}, u32[]{:S(2)}, u32[]{:S(2)}) %collective-permute-start.15) | collective-permute-done | bytes 3932192 | tf_op jit(solution)/shard_map/ppermute | solution.py:678
  915.8 2.3 shard_map.91.refs_0_
  918.1 2.3 shard_map.92.refs_0_
  920.5 4.1 shard_map.93.refs_0_
  924.6 7.4 shard_map.94.refs_0_
  932.0 14.2 %shard_map.95.refs_0_ = f32[960,6144]{1,0:T(8,128)} custom-call(f32[960,2048]{1,0:T(8,128)} %get-tuple-element.61.own_ref, f32[960,2048]{1,0:T(8,128)} %collective-permute-done.14.recv_ref, f32[960,6144]{1,0:T(8,128)} %shard_map.94.refs_0_), custom_call_target="tpu_custom_call", output_to_operand_aliasing={{}: (2, {})} | custom-call | flops 1966080 | bytes 23592960 | tf_op jit(solution)/shard_map/pallas_call | solution.py:639
  946.2 10.6 %shard_map.96.refs_0_ = f32[960,6144]{1,0:T(8,128)} custom-call(f32[960,1536]{1,0:T(8,128)} %get-tuple-element.60.own_ref, f32[960,1536]{1,0:T(8,128)} %collective-permute-done.13.recv_ref, f32[960,6144]{1,0:T(8,128)} %shard_map.95.refs_0_), custom_call_target="tpu_custom_call", output_to_operand_aliasing={{}: (2, {})} | custom-call | flops 1474560 | bytes 17694720 | tf_op jit(solution)/shard_map/pallas_call | solution.py:639
  956.8 3.7 shard_map.97.refs_0_
  960.5 0.6 slice.6
  961.1 2.0 shard_map.98
  (47 shorter events, 1.4 us)
Async XLA Ops:
  350.0 34.3 %collective-permute-start = (f32[480,4096]{1,0:T(8,128)}, f32[480,4096]{1,0:T(8,128)}, u32[]{:S(2)}, u32[]{:S(2)}) collective-permute-start(f32[480,4096]{1,0:T(8,128)} %back.3), channel_id=1, source_target_pairs={{0,1},{1,0},{2,3},{3,2},{4,5},{5,4},{6,7},{7,6},{8,9},{9,8},{10,11... | collective-permute-start | bytes 23592968 | tf_op jit(solution)/shard_map/ppermute | solution.py:687
  395.1 46.5 %collective-permute-start.1 = (f32[240,4096]{1,0:T(8,128)}, f32[240,4096]{1,0:T(8,128)}, u32[]{:S(2)}, u32[]{:S(2)}) collective-permute-start(f32[240,4096]{1,0:T(8,128)} %get-tuple-element.67), channel_id=1, source_target_pairs={{0,2},{1,5},{2,0},{3,7},{4,6},{5,1},{6,4},{7,3},{8,10},{9,13},{10,... | collective-permute-start | bytes 11796488 | tf_op jit(solution)/shard_map/ppermute | solution.py:693
  443.9 24.8 %collective-permute-start.2 = (f32[120,4096]{1,0:T(8,128)S(1)}, f32[120,4096]{1,0:T(8,128)}, u32[]{:S(2)}, u32[]{:S(2)}) collective-permute-start(f32[120,4096]{1,0:T(8,128)S(1)} %dynamic-slice_add_fusion.2), channel_id=1, source_target_pairs={{0,4},{1,3},{2,6},{3,1},{4,0},{5,7},{6,2},{7,5},{8,12},{9,11},{10,... | collective-permute-start | bytes 5898248 | tf_op jit(solution)/shard_map/ppermute | solution.py:693
  446.0 486.0 %collective-permute-start.14 = (f32[960,2048]{1,0:T(8,128)}, f32[960,2048]{1,0:T(8,128)}, u32[]{:S(2)}, u32[]{:S(2)}) collective-permute-start(f32[960,2048]{1,0:T(8,128)} %get-tuple-element.61.own_ref), channel_id=1, source_target_pairs={{0,8},{8,0},{1,9},{9,1},{2,10},{10,2},{3,11},{11,3},{4,12},{12,4},... | collective-permute-start | bytes 23592968 | tf_op jit(solution)/shard_map/ppermute | solution.py:678
  446.0 255.0 %collective-permute-start.16 = (f32[960,512]{1,0:T(8,128)}, f32[960,512]{1,0:T(8,128)}, u32[]{:S(2)}, u32[]{:S(2)}) collective-permute-start(f32[960,512]{1,0:T(8,128)} %get-tuple-element.63.own_ref), channel_id=1, source_target_pairs={{0,8},{8,0},{1,9},{9,1},{2,10},{10,2},{3,11},{11,3},{4,12},{12,4},... | collective-permute-start | bytes 5898248 | tf_op jit(solution)/shard_map/ppermute | solution.py:678
  448.1 25.8 %copy-start.9 = (f32[960,256]{1,0:T(8,128)S(1)}, f32[960,256]{1,0:T(8,128)}, u32[]{:S(2)}) copy-start(f32[960,256]{1,0:T(8,128)} %get-tuple-element.64.own_ref) | copy-start | bytes 2949124
  448.1 25.8 %copy-start.8 = (f32[960,256]{1,0:T(8,128)S(1)}, f32[960,256]{1,0:T(8,128)}, u32[]{:S(2)}) copy-start(f32[960,256]{1,0:T(8,128)} %get-tuple-element.65.own_ref) | copy-start | bytes 2949124
  448.1 287.4 %copy-start.12 = (f32[8,128]{1,0:T(8,128)S(1)}, f32[8,128]{1,0:T(8,128)}, u32[]{:S(2)}) copy-start(f32[8,128]{1,0:T(8,128)} %get-tuple-element.55) | copy-start | bytes 12292
  448.1 302.1 %copy-start.11 = (f32[8,128]{1,0:T(8,128)S(1)}, f32[8,128]{1,0:T(8,128)}, u32[]{:S(2)}) copy-start(f32[8,128]{1,0:T(8,128)} %get-tuple-element.56) | copy-start | bytes 12292
  471.8 281.0 %copy-start = (f32[120,4096]{1,0:T(8,128)}, f32[120,4096]{1,0:T(8,128)S(1)}, u32[]{:S(2)}) copy-start(f32[120,4096]{1,0:T(8,128)S(1)} %add_add_fusion.refs_0_) | copy-start | bytes 5898244
  471.8 229.5 %collective-permute-start.3 = (f32[120,4096]{1,0:T(8,128)S(1)}, f32[120,4096]{1,0:T(8,128)S(1)}, u32[]{:S(2)}, u32[]{:S(2)}) collective-permute-start(f32[120,4096]{1,0:T(8,128)S(1)} %add_add_fusion.refs_0_), channel_id=1, source_target_pairs={{0,4},{1,3},{2,6},{3,1},{4,0},{5,7},{6,2},{7,5},{8,12},{9,11},{10,... | collective-permute-start | bytes 5898248 | tf_op jit(solution)/shard_map/ppermute | solution.py:700
  473.9 207.8 %collective-permute-start.17 = (f32[960,256]{1,0:T(8,128)S(1)}, f32[960,256]{1,0:T(8,128)}, u32[]{:S(2)}, u32[]{:S(2)}) collective-permute-start(f32[960,256]{1,0:T(8,128)S(1)} %copy-done.9), channel_id=1, source_target_pairs={{0,8},{8,0},{1,9},{9,1},{2,10},{10,2},{3,11},{11,3},{4,12},{12,4},... | collective-permute-start | bytes 2949128 | tf_op jit(solution)/shard_map/ppermute | solution.py:678
  473.9 227.1 %collective-permute-start.18 = (f32[960,256]{1,0:T(8,128)S(1)}, f32[960,256]{1,0:T(8,128)}, u32[]{:S(2)}, u32[]{:S(2)}) collective-permute-start(f32[960,256]{1,0:T(8,128)S(1)} %copy-done.8), channel_id=1, source_target_pairs={{0,8},{8,0},{1,9},{9,1},{2,10},{10,2},{3,11},{11,3},{4,12},{12,4},... | collective-permute-start | bytes 2949128 | tf_op jit(solution)/shard_map/ppermute | solution.py:678
  681.6 24.6 %collective-permute-start.4 = (f32[120,4096]{1,0:T(8,128)S(1)}, f32[120,4096]{1,0:T(8,128)S(1)}, u32[]{:S(2)}, u32[]{:S(2)}) collective-permute-start(f32[120,4096]{1,0:T(8,128)S(1)} %add_add_fusion.refs_0_), channel_id=1, source_target_pairs={{0,2},{1,5},{2,0},{3,7},{4,6},{5,1},{6,4},{7,3},{8,10},{9,13},{10,... | collective-permute-start | bytes 5898248 | tf_op jit(solution)/shard_map/ppermute | solution.py:700
  701.0 5.3 collective-permute-start.6
  701.0 245.2 %collective-permute-start.13 = (f32[960,1536]{1,0:T(8,128)}, f32[960,1536]{1,0:T(8,128)}, u32[]{:S(2)}, u32[]{:S(2)}) collective-permute-start(f32[960,1536]{1,0:T(8,128)} %get-tuple-element.60.own_ref), channel_id=1, source_target_pairs={{0,8},{8,0},{1,9},{9,1},{2,10},{10,2},{3,11},{11,3},{4,12},{12,4},... | collective-permute-start | bytes 17694728 | tf_op jit(solution)/shard_map/ppermute | solution.py:678
  701.3 5.0 copy-start.1
  701.3 26.0 %collective-permute-start.5 = (f32[120,4096]{1,0:T(8,128)S(1)}, f32[120,4096]{1,0:T(8,128)S(1)}, u32[]{:S(2)}, u32[]{:S(2)}) collective-permute-start(f32[120,4096]{1,0:T(8,128)S(1)} %collective-permute-done.3.refs_1_), channel_id=1, source_target_pairs={{0,2},{1,5},{2,0},{3,7},{4,6},{5,1},{6,4},{7,3},{8,10},{9,13},{10,... | collective-permute-start | bytes 5898248 | tf_op jit(solution)/shard_map/ppermute | solution.py:700
  706.3 21.1 %copy-start.2 = (f32[120,4096]{1,0:T(8,128)}, f32[120,4096]{1,0:T(8,128)S(1)}, u32[]{:S(2)}) copy-start(f32[120,4096]{1,0:T(8,128)S(1)} %collective-permute-done.4.refs_2_) | copy-start | bytes 5898244
  706.3 21.1 %collective-permute-start.7 = (f32[120,4096]{1,0:T(8,128)S(1)}, f32[120,4096]{1,0:T(8,128)S(1)}, u32[]{:S(2)}, u32[]{:S(2)}) collective-permute-start(f32[120,4096]{1,0:T(8,128)S(1)} %collective-permute-done.3.refs_1_), channel_id=1, source_target_pairs={{0,1},{1,0},{2,3},{3,2},{4,5},{5,4},{6,7},{7,6},{8,9},{9,8},{10,11... | collective-permute-start | bytes 5898248 | tf_op jit(solution)/shard_map/ppermute | solution.py:700
  706.3 25.0 %copy-start.3 = (f32[120,4096]{1,0:T(8,128)}, f32[120,4096]{1,0:T(8,128)S(1)}, u32[]{:S(2)}) copy-start(f32[120,4096]{1,0:T(8,128)S(1)} %collective-permute-done.6.refs_4_) | copy-start | bytes 5898244
  706.3 209.3 %collective-permute-start.15 = (f32[960,1024]{1,0:T(8,128)}, f32[960,1024]{1,0:T(8,128)}, u32[]{:S(2)}, u32[]{:S(2)}) collective-permute-start(f32[960,1024]{1,0:T(8,128)} %get-tuple-element.62.own_ref), channel_id=1, source_target_pairs={{0,8},{8,0},{1,9},{9,1},{2,10},{10,2},{3,11},{11,3},{4,12},{12,4},... | collective-permute-start | bytes 11796488 | tf_op jit(solution)/shard_map/ppermute | solution.py:678
  727.3 4.0 copy-start.4
  727.3 4.0 collective-permute-start.8
  727.4 6.8 copy-start.5
  727.4 6.8 collective-permute-start.9
  731.3 2.8 copy-start.6
  731.3 225.5 %collective-permute-start.12 = (f32[960,384]{1,0:T(8,128)}, f32[960,384]{1,0:T(8,128)}, u32[]{:S(2)}, u32[]{:S(2)}) collective-permute-start(f32[960,384]{1,0:T(8,128)} %get-tuple-element.59.own_ref), channel_id=1, source_target_pairs={{0,8},{8,0},{1,9},{9,1},{2,10},{10,2},{3,11},{11,3},{4,12},{12,4},... | collective-permute-start | bytes 4423688 | tf_op jit(solution)/shard_map/ppermute | solution.py:678
  734.1 1.3 copy-start.7
  734.1 227.0 %collective-permute-start.11 = (f32[960,128]{1,0:T(8,128)}, f32[960,128]{1,0:T(8,128)}, u32[]{:S(2)}, u32[]{:S(2)}) collective-permute-start(f32[960,128]{1,0:T(8,128)} %get-tuple-element.58.own_ref), channel_id=1, source_target_pairs={{0,8},{8,0},{1,9},{9,1},{2,10},{10,2},{3,11},{11,3},{4,12},{12,4},... | collective-permute-start | bytes 1474568 | tf_op jit(solution)/shard_map/ppermute | solution.py:678
  915.6 44.9 %collective-permute-start.10 = (f32[1024]{0:T(1024)S(1)}, f32[1024]{0:T(1024)S(1)}, u32[]{:S(2)}, u32[]{:S(2)}) collective-permute-start(f32[1024]{0:T(1024)S(1)} %concatenate.3), channel_id=1, source_target_pairs={{0,8},{8,0},{1,9},{9,1},{2,10},{10,2},{3,11},{11,3},{4,12},{12,4},... | collective-permute-start | bytes 12296 | tf_op jit(solution)/shard_map/ppermute | solution.py:709
  960.5 0.6 copy-start.10

commit v4 on v3

--- a/solution.py
+++ b/solution.py
@@ -18,15 +18,15 @@
 STOK = 256
 COL = 512
 GCOL = 256
-CHUNKS = (256, 256, 512, 1024, 2048, 1536, 384, 128)
+CHUNKS = ((256,), (256,), (512,), (1024,), (2048,), (1536, 384, 128))
 VMEM_LIMIT = 62 * 1024 * 1024
 MESH = pl.DeviceIdType.MESH
 NT = (((1,), (1,)), ((), ()))
 NN = (((1,), (0,)), ((), ()))
 
 
-def stats_kernel(mask_hbm, gain_hbm, hid_hbm, tab_hbm, tea_hbm, x_hbm, xt_hbm, out_ref,
-                 mask_buf, row_buf, hid_buf, x_buf, xt_buf, tab_buf, tea_buf, rows_ref, z0_ref, z1_ref, acc_ref, sum_ref, gain_buf, flag_buf,
+def stats_kernel(mask_hbm, gain_hbm, hid_hbm, tab_hbm, tea_hbm, x_hbm, xt_hbm, out_ref, gain_buf,
+                 mask_buf, hid_buf, x_buf, xt_buf, tab_buf, tea_buf, rows_ref, z0_ref, z1_ref, acc_ref, sum_ref, flag_buf, row_buf,
                  flags, order, hid_sem, tab_sem, tea_sem, flag_sem, row_sem, out_sem):
     z_refs = (z0_ref, z1_ref)
     dim, tokens = hid_hbm.shape
@@ -185,15 +185,15 @@
     return pl.pallas_call(
         stats_kernel,
         in_specs=[hbm] * 5,
-        out_specs=[hbm, hbm, vmem],
+        out_specs=[hbm, hbm, vmem, vmem],
         out_shape=[
             jax.ShapeDtypeStruct((tokens, dim), jnp.bfloat16),
             jax.ShapeDtypeStruct((dim, tokens), jnp.bfloat16),
             jax.ShapeDtypeStruct((tokens // 64, 128), jnp.float32),
+            jax.ShapeDtypeStruct((dim, 128), jnp.float32),
         ],
         scratch_shapes=[
             pltpu.VMEM(mask_lines.shape, jnp.float32),
-            pltpu.VMEM((1, dim), jnp.float32),
             pltpu.VMEM((dim, tokens), jnp.bfloat16),
             pltpu.VMEM((tokens, dim), jnp.bfloat16),
             pltpu.VMEM((dim, tokens), jnp.bfloat16),
@@ -204,8 +204,8 @@
             pltpu.VMEM((STOK, COL), jnp.float32),
             pltpu.VMEM((2, STOK, 128), jnp.float32),
             pltpu.VMEM((2, tokens, 128), jnp.float32),
-            pltpu.VMEM((dim, 128), jnp.float32),
             pltpu.VMEM((tokens // 128, 128), jnp.int32),
+            pltpu.VMEM((1, dim), jnp.float32),
             pltpu.SMEM((tokens // 128, 128), jnp.int32),
             pltpu.SMEM((tokens // RUN + 2 * per,), jnp.int32),
             pltpu.SemaphoreType.DMA((tokens // TOK,)),
@@ -322,7 +322,7 @@
     ab_ref[:half, :] = weight / total[:half]
     ab_ref[half:, :] = weight / total[half:]
     logs = weight * (jnp.log(total[:half]) - jnp.log(total[half:]))
-    log_ref[...] = jnp.sum(logs.reshape(-1, 8, 128), axis=0)
+    log_ref[...] = logs
 
     kl_ref[...] = jnp.zeros_like(kl_ref)
     table_ref[...] = jnp.zeros_like(table_ref)
@@ -335,7 +335,7 @@
                 coef_refs[par][k, b * 128:(b + 1) * 128, :] = jnp.broadcast_to(line, (128, 128)).T
 
     def weigh(m, par):
-        kl_acc = kl_ref[...]
+        kl_acc = kl_ref[:8, :]
         for r in range(0, TOK, 64):
             rows = pl.ds(pl.multiple_of(m * TOK + r, 64), 64)
             a = coef_refs[par][0, r:r + 64, :]
@@ -346,7 +346,7 @@
             for q in range(width // 128):
                 lanes = slice(q * 128, (q + 1) * 128)
                 g_ref[rows, lanes] = (stu_ref[rows, lanes] * a - tea_ref[rows, lanes] * b).astype(jnp.bfloat16)
-        kl_ref[...] = kl_acc
+        kl_ref[:8, :] = kl_acc
 
     def product(m):
         rows = pl.ds(pl.multiple_of(m * TOK, TOK), TOK)
@@ -386,10 +386,10 @@
         out_specs=[whole, whole, whole, hbm, whole],
         out_shape=[
             jax.ShapeDtypeStruct(stats.shape, jnp.float32),
-            jax.ShapeDtypeStruct((8, 128), jnp.float32),
+            jax.ShapeDtypeStruct(mask_lines.shape, jnp.float32),
             jax.ShapeDtypeStruct((dim, width), jnp.float32),
             jax.ShapeDtypeStruct((tokens, width), jnp.bfloat16),
-            jax.ShapeDtypeStruct((8, 128), jnp.float32),
+            jax.ShapeDtypeStruct((32, 128), jnp.float32),
         ],
         scratch_shapes=[
             pltpu.VMEM(stats.shape, jnp.float32),
@@ -426,7 +426,10 @@
     )(stats, mask_lines, x_rows, x_t, tab_t, tea_rows)
 
 
-def grad_kernel(ab_ref, x_ref, xt_ref, tab_ref, tea_ref, kl_in_ref, table_ref, g_ref, kl_ref, z0_ref, z1_ref, coef_ref):
+def grad_kernel(pieces, ab_ref, x_ref, xt_ref, tab_ref, tea_ref, kl_in_ref, *refs):
+    out_refs = refs[:pieces]
+    g_ref, kl_ref, z0_ref, z1_ref, coef_ref = refs[pieces:pieces + 5]
+    table_ref = refs[-1] if pieces > 1 else out_refs[0]
     z_refs = (z0_ref, z1_ref)
     col = z0_ref.shape[1]
     count = tab_ref.shape[1] // col
@@ -449,7 +452,9 @@
         z_refs[par][...] = lax.dot_general(x_ref[...], tab_ref[:, columns(n)], NN, preferred_element_type=jnp.float32)
 
     def weigh(n, par):
-        def strip(rows, kl_acc):
+        kl_acc = kl_ref[:8, :]
+        for r in range(0, TOK, 64):
+            rows = slice(r, r + 64)
             a = coef_ref[0, rows, :]
             b = coef_ref[1, rows, :]
             for q in range(col // 128):
@@ -464,15 +469,7 @@
                 for w in range(0, 64, 8):
                     kl_acc += kl[w:w + 8]
                 g_ref[rows, lanes] = ((pa - pb) * (1.0 - ts * ts)).astype(jnp.bfloat16)
-            return kl_acc
-
-        if count <= 2:
-            kl_ref[...] = lax.fori_loop(0, TOK // 64, lambda r, acc: strip(pl.ds(pl.multiple_of(r * 64, 64), 64), acc), kl_ref[...])
-        else:
-            kl_acc = kl_ref[...]
-            for r in range(0, TOK, 64):
-                kl_acc = strip(slice(r, r + 64), kl_acc)
-            kl_ref[...] = kl_acc
+        kl_ref[:8, :] = kl_acc
 
     def product(n):
         table_ref[:, columns(n)] += lax.dot_general(xt_ref[...], g_ref[:, columns(n)], NN, preferred_element_type=jnp.float32)
@@ -500,13 +497,22 @@
     product(count - 2)
     weigh(count - 1, 1)
     product(count - 1)
-
-
-def grad_call(ab, x_rows, x_t, tab_t, tea_rows, start, size, kl):
+    if pieces > 1:
+        @pl.when(block == pl.num_programs(0) - 1)
+        def _():
+            begin = 0
+            for out_ref in out_refs:
+                out_ref[...] = table_ref[:, begin:begin + out_ref.shape[1]]
+                begin += out_ref.shape[1]
+
+
+def grad_call(ab, x_rows, x_t, tab_t, tea_rows, start, pieces, kl):
     tokens, dim = x_rows.shape
+    size = sum(pieces)
     col = GCOL if size % (2 * GCOL) == 0 else size
+    split = len(pieces) > 1
     return pl.pallas_call(
-        grad_kernel,
+        functools.partial(grad_kernel, len(pieces)),
         grid=(tokens // TOK,),
         in_specs=[
             pl.BlockSpec(ab.shape, lambda i: (0, 0)),
@@ -514,22 +520,20 @@
             pl.BlockSpec((dim, TOK), lambda i: (0, i)),
             pl.BlockSpec((pl.Element(dim), pl.Element(size)), lambda i: (0, start), pipeline_mode=pl.Buffered(1)),
             pl.BlockSpec((pl.Element(TOK), pl.Element(size)), lambda i: (i * TOK, start)),
-            pl.BlockSpec((8, 128), lambda i: (0, 0)),
+            pl.BlockSpec((32, 128), lambda i: (0, 0)),
         ],
-        out_specs=[
-            pl.BlockSpec((dim, size), lambda i: (0, 0)),
+        out_specs=[pl.BlockSpec((dim, width), lambda i: (0, 0)) for width in pieces] + [
             pl.BlockSpec((TOK, size), lambda i: (i, 0)),
-            pl.BlockSpec((8, 128), lambda i: (0, 0)),
+            pl.BlockSpec((32, 128), lambda i: (0, 0)),
         ],
         scratch_shapes=[
             pltpu.VMEM((TOK, col), jnp.float32),
             pltpu.VMEM((TOK, col), jnp.float32),
             pltpu.VMEM((2, TOK, 128), jnp.float32),
-        ],
-        out_shape=[
-            jax.ShapeDtypeStruct((dim, size), jnp.float32),
+        ] + [pltpu.VMEM((dim, size), jnp.float32)] * split,
+        out_shape=[jax.ShapeDtypeStruct((dim, width), jnp.float32) for width in pieces] + [
             jax.ShapeDtypeStruct((tokens, size), jnp.bfloat16),
-            jax.ShapeDtypeStruct((8, 128), jnp.float32),
+            jax.ShapeDtypeStruct((32, 128), jnp.float32),
         ],
         compiler_params=pltpu.CompilerParams(vmem_limit_bytes=VMEM_LIMIT),
         cost_estimate=pl.CostEstimate(flops=4 * tokens * size * dim, bytes_accessed=4 * tokens * size, transcendentals=0),
@@ -574,12 +578,11 @@
 
 
 def finish_kernel(off_ref, hid_ref, gain_ref, *refs):
-    piece_refs, (out_ref, sum_ref, norm_ref, a_ref, gain_buf) = refs[:-5], refs[-5:]
+    piece_refs, (out_ref, sum_ref, norm_ref, a_ref) = refs[:-4], refs[-4:]
     dim, toks = hid_ref.shape
 
     @pl.when(pl.program_id(0) == 0)
     def _():
-        gain_buf[...] = jnp.broadcast_to(1.0 + gain_ref[...], (128, dim)).T
         sum_ref[...] = jnp.zeros_like(sum_ref)
 
     hid = hid_ref[...].astype(jnp.float32)
@@ -588,7 +591,7 @@
     dot = jnp.zeros((1, toks), jnp.float32)
     for k, piece_ref in enumerate(piece_refs):
         rows = pl.ds(pl.multiple_of(off_ref[k], 8), piece_ref.shape[0])
-        gain = gain_buf[rows, :]
+        gain = gain_ref[rows, :]
         acc = sum_ref[rows, :]
         for b in range(toks // 128):
             lanes = slice(b * 128, (b + 1) * 128)
@@ -599,7 +602,7 @@
     out_ref[...] = (inv_rms * (a_ref[...] - norm_ref[...] * (dot / dim))).astype(jnp.bfloat16)
 
 
-def finish_call(offsets, hid_t, gain_row, pieces):
+def finish_call(offsets, hid_t, gain_cols, pieces):
     dim, tokens = hid_t.shape
     rows = pieces[0].shape[0]
     return pl.pallas_call(
@@ -607,16 +610,16 @@
         grid_spec=pltpu.PrefetchScalarGridSpec(
             num_scalar_prefetch=1,
             grid=(tokens // TOK,),
-            in_specs=[pl.BlockSpec((dim, TOK), lambda i, o: (0, i)), pl.BlockSpec((1, dim), lambda i, o: (0, 0))]
+            in_specs=[pl.BlockSpec((dim, TOK), lambda i, o: (0, i)), pl.BlockSpec((dim, 128), lambda i, o: (0, 0))]
             + [pl.BlockSpec((rows, TOK), lambda i, o: (0, i))] * len(pieces),
             out_specs=[pl.BlockSpec((dim, TOK), lambda i, o: (0, i)), pl.BlockSpec((dim, 128), lambda i, o: (0, 0))],
-            scratch_shapes=[pltpu.VMEM((dim, TOK), jnp.float32), pltpu.VMEM((dim, TOK), jnp.float32), pltpu.VMEM((dim, 128), jnp.float32)],
+            scratch_shapes=[pltpu.VMEM((dim, TOK), jnp.float32), pltpu.VMEM((dim, TOK), jnp.float32)],
         ),
         out_shape=[jax.ShapeDtypeStruct((dim, tokens), jnp.bfloat16), jax.ShapeDtypeStruct((dim, 128), jnp.float32)],
         compiler_params=pltpu.CompilerParams(vmem_limit_bytes=VMEM_LIMIT),
         cost_estimate=pl.CostEstimate(flops=10 * tokens * dim, bytes_accessed=8 * tokens * dim, transcendentals=0),
         name="finish",
-    )(offsets, hid_t, gain_row, *pieces)
+    )(offsets, hid_t, gain_cols, *pieces)
 
 
 def add_kernel(own_ref, recv_ref, *refs):
@@ -664,20 +667,21 @@
         tokens, dim = hid_rows.shape
         hid_t, tab_t = hid_rows.T, tab_rows.T
         mask_lines = mask_rows.reshape(tokens // 128, 128)
-        x_rows, x_t, stats = stats_call(mask_lines, w_final.reshape(1, dim), hid_t, tab_t, tea_rows)
+        x_rows, x_t, stats, gain_cols = stats_call(mask_lines, w_final.reshape(1, dim), hid_t, tab_t, tea_rows)
 
         swap = [(0, 1), (1, 0)]
         start = 0
         parts, grads = [], []
-        for c, size in enumerate(CHUNKS):
+        for c, pieces in enumerate(CHUNKS):
             if c == 0:
-                ab, log_part, table_c, g, kl = first_call(stats, mask_lines, x_rows, x_t, tab_t, tea_rows, size, tp)
+                ab, log_part, *tables, g, kl = first_call(stats, mask_lines, x_rows, x_t, tab_t, tea_rows, sum(pieces), tp)
             else:
-                table_c, g, kl = grad_call(ab, x_rows, x_t, tab_t, tea_rows, start, size, kl)
+                *tables, g, kl = grad_call(ab, x_rows, x_t, tab_t, tea_rows, start, pieces, kl)
             grads.append(g)
-            recv = lax.ppermute(table_c, "dp", swap)
-            parts.append((start, table_c, recv))
-            start += size
+            for table in tables:
+                recv = lax.ppermute(table, "dp", swap)
+                parts.append((start, table, recv))
+                start += table.shape[1]
 
         me = lax.axis_index("tp")
         core, xb, yb = me & 1, (me >> 1) & 1, (me >> 2) & 1
@@ -690,9 +694,11 @@
             half = keep.shape[0] // 2
             gone = (1 - bits[s]) * half
             away = lax.dynamic_slice_in_dim(keep, gone, half, 0) + lax.dynamic_slice_in_dim(recv, gone, half, 0)
+            away, keep, recv = lax.optimization_barrier((away, keep, recv))
             away = lax.ppermute(away, "tp", perms[s])
             kept = bits[s] * half
             keep = lax.dynamic_slice_in_dim(keep, kept, half, 0) + lax.dynamic_slice_in_dim(recv, kept, half, 0)
+            keep, kl = lax.optimization_barrier((keep, kl))
             recv = away
         own = keep + recv
         pieces = [own]
@@ -704,7 +710,7 @@
         offsets = jnp.stack([place(spot, dim) for spot in spots])
 
         loss_part = lax.psum(SOFT_CAP * jnp.sum(kl), "tp") + jnp.sum(log_part)
-        grad_h, gain_part = finish_call(offsets, hid_t, w_final.reshape(1, dim), pieces)
+        grad_h, gain_part = finish_call(offsets, hid_t, gain_cols, pieces)
         small = jnp.concatenate([jnp.sum(gain_part, axis=1), jnp.full((1024 - dim,), loss_part)])
         other = lax.ppermute(small, "dp", swap)
         small = small + other

time: 969 us -> 922 us (0.951)
  Pallas kernels: 447 us -> 410 us
    pallas_call x7 -> x5, Pallas kernels: 228 us -> 197 us  [grad_call(): pl.pallas_call(functools.partial(grad_kernel, len(pieces)), grid=(tokens...]
where the time goes in v4:
time: 922 us; the launch traced here: 920 us
  waiting for transfers between devices  459 us (50%)
  Pallas kernels  410 us (44%)
  other arithmetic  17.9 us (2%)
  starting transfers between devices  14.7 us (2%)
  blocking collectives  13.3 us (1%)
    ppermute x8, waiting for transfers between devices, local_step(): recv = lax.ppermute(table, 'dp', swap)  369 us
    pallas_call x5, Pallas kernels, grad_call(): pl.pallas_call(functools.partial(grad_kernel, len(pieces)), grid=(tokens...  197 us
    pallas_call x1, Pallas kernels, stats_call(): pl.pallas_call(stats_kernel, in_specs=[hbm] * 5, out_specs=[hbm, hbm, vme...  68.2 us
    pallas_call x2, Pallas kernels, back_call(): pl.pallas_call(back_kernel, grid_spec=pltpu.PrefetchScalarGridSpec(num_sc...  64.1 us
    ppermute x2, waiting for transfers between devices, local_step(): away = lax.ppermute(away, 'tp', perms[s])  58.5 us
    pallas_call x8, Pallas kernels, add_call(): pl.pallas_call(add_kernel, grid=(size // step,), in_specs=in_specs, out_s...  46.8 us
    ppermute x7, waiting for transfers between devices, local_step(): pieces += [lax.ppermute(piece, 'tp', perms[s]) for piece in pieces]  31.9 us
  transfers between devices with their start and end apart: 19, of which 9 were waited for; matrix products, arithmetic and copies ran while one was open for 1% of the time, Pallas kernels for 10%

profile of v4, /device:TPU:0, one launch (start us, length us, event | category | flops | bytes accessed | tf_op | source)
XLA Modules:
  0.0 920.4 jit_solution(9083097452914836911)
XLA Ops:
  0.6 68.2 %stats.1 = (bf16[4096,960]{1,0:T(8,128)(2,1)}, bf16[960,4096]{1,0:T(8,128)(2,1)}, f32[64,128]{1,0:T(8,128)}, f32[960,128]{1,0:T(8,128)}) custom-call(f32[32,128]{1,0:T(8,128)} %bitcast.31, f32[1,960]{1,0:T(1,128)} %bitcast.34, bf16[960,4096]{1,0:T(8,128)(2,1)} %bitcast.29, bf16[960,6144]{1,0:T(8,128)(2,1)} %bitcast.19, bf16[4096,6144]{1,0:T(8,128)(2,1)} %tea_ref.9), custom_call_target="tpu_custom_call" | custom-call | flops 48318382080 | bytes 50331648 | tf_op jit(solution)/shard_map/stats/pallas_call | solution.py:185
  68.8 16.4 %first.1 = (f32[64,128]{1,0:T(8,128)}, f32[32,128]{1,0:T(8,128)}, f32[960,256]{1,0:T(8,128)}, bf16[4096,256]{1,0:T(8,128)(2,1)}, f32[32,128]{1,0:T(8,128)}) custom-call(f32[64,128]{1,0:T(8,128)} %get-tuple-element.43.stats_hbm, f32[32,128]{1,0:T(8,128)} %bitcast.32, bf16[4096,960]{1,0:T(8,128)(2,1)} %get-tuple-element.44.x_hbm.x_ref, ...), custom_call_target="tpu_custom_call" | custom-call | flops 4026531840 | bytes 15728640 | tf_op jit(solution)/shard_map/first/pallas_call | solution.py:383
  85.3 15.3 %shard_map.84 = (f32[960,256]{1,0:T(8,128)}, bf16[4096,256]{1,0:T(8,128)(2,1)}, f32[32,128]{1,0:T(8,128)}) custom-call(f32[64,128]{1,0:T(8,128)} %get-tuple-element.47.ab_ref, bf16[4096,960]{1,0:T(8,128)(2,1)} %get-tuple-element.44.x_hbm.x_ref, bf16[960,4096]{1,0:T(8,128)(2,1)} %get-tuple-element.45.xt_hbm.xt_ref, bf16[960,6144]{1,0:T(8,128)(2,1)} %bitcast.21, ...), custom_call_target="tpu_custom_call" | custom-call | flops 4026531840 | bytes 4194304 | tf_op jit(solution)/shard_map/pallas_call | solution.py:514
  100.6 17.9 %shard_map.85 = (f32[960,512]{1,0:T(8,128)}, bf16[4096,512]{1,0:T(8,128)(2,1)}, f32[32,128]{1,0:T(8,128)}) custom-call(f32[64,128]{1,0:T(8,128)} %get-tuple-element.47.ab_ref, bf16[4096,960]{1,0:T(8,128)(2,1)} %get-tuple-element.44.x_hbm.x_ref, bf16[960,4096]{1,0:T(8,128)(2,1)} %get-tuple-element.45.xt_hbm.xt_ref, bf16[960,6144]{1,0:T(8,128)(2,1)} %bitcast.22, ...), custom_call_target="tpu_custom_call" | custom-call | flops 8053063680 | bytes 8388608 | tf_op jit(solution)/shard_map/pallas_call | solution.py:514
  118.5 30.3 %shard_map.86 = (f32[960,1024]{1,0:T(8,128)}, bf16[4096,1024]{1,0:T(8,128)(2,1)}, f32[32,128]{1,0:T(8,128)}) custom-call(f32[64,128]{1,0:T(8,128)} %get-tuple-element.47.ab_ref, bf16[4096,960]{1,0:T(8,128)(2,1)} %get-tuple-element.44.x_hbm.x_ref, bf16[960,4096]{1,0:T(8,128)(2,1)} %get-tuple-element.45.xt_hbm.xt_ref, bf16[960,6144]{1,0:T(8,128)(2,1)} %bitcast.23, ...), custom_call_target="tpu_custom_call" | custom-call | flops 16106127360 | bytes 16777216 | tf_op jit(solution)/shard_map/pallas_call | solution.py:514
  148.8 66.2 %shard_map.87 = (f32[960,2048]{1,0:T(8,128)}, bf16[4096,2048]{1,0:T(8,128)(2,1)}, f32[32,128]{1,0:T(8,128)}) custom-call(f32[64,128]{1,0:T(8,128)} %get-tuple-element.47.ab_ref, bf16[4096,960]{1,0:T(8,128)(2,1)} %get-tuple-element.44.x_hbm.x_ref, bf16[960,4096]{1,0:T(8,128)(2,1)} %get-tuple-element.45.xt_hbm.xt_ref, bf16[960,6144]{1,0:T(8,128)(2,1)} %bitcast.24, ...), custom_call_target="tpu_custom_call" | custom-call | flops 32212254720 | bytes 33554432 | tf_op jit(solution)/shard_map/pallas_call | solution.py:514
  215.0 67.3 %shard_map.88 = (f32[960,1536]{1,0:T(8,128)}, f32[960,384]{1,0:T(8,128)}, f32[960,128]{1,0:T(8,128)}, bf16[4096,2048]{1,0:T(8,128)(2,1)}, f32[32,128]{1,0:T(8,128)}) custom-call(f32[64,128]{1,0:T(8,128)} %get-tuple-element.47.ab_ref, bf16[4096,960]{1,0:T(8,128)(2,1)} %get-tuple-element.44.x_hbm.x_ref, bf16[960,4096]{1,0:T(8,128)(2,1)} %get-tuple-element.45.xt_hbm.xt_ref, ...), custom_call_target="tpu_custom_call" | custom-call | flops 32212254720 | bytes 33554432 | tf_op jit(solution)/shard_map/pallas_call | solution.py:514
  282.3 32.1 %back.3 = f32[480,4096]{1,0:T(8,128)} custom-call(s32[1]{0:T(128)} %bitcast.13.half_ref, bf16[960,6144]{1,0:T(8,128)(2,1)} %bitcast.26, bf16[4096,256]{1,0:T(8,128)(2,1)} %get-tuple-element.46.refs_0_, bf16[4096,256]{1,0:T(8,128)(2,1)} %get-tuple-element.49.refs_1_, bf16[4096,512]{1,0:T(8,128)(2,1)} %get-tuple-element.51.refs_2_, ...), custom_call_target="tpu_custom_call" | custom-call | flops 24159191040 | bytes 50331648 | tf_op jit(solution)/shard_map/back/pallas_call | solution.py:564
  314.3 0.5 collective-permute-start
  314.9 32.1 %back.2 = f32[480,4096]{1,0:T(8,128)} custom-call(s32[1]{0:T(128)} %bitcast.12.half_ref, bf16[960,6144]{1,0:T(8,128)(2,1)} %bitcast.27, bf16[4096,256]{1,0:T(8,128)(2,1)} %get-tuple-element.46.refs_0_, bf16[4096,256]{1,0:T(8,128)(2,1)} %get-tuple-element.49.refs_1_, bf16[4096,512]{1,0:T(8,128)(2,1)} %get-tuple-element.51.refs_2_, ...), custom_call_target="tpu_custom_call" | custom-call | flops 24159191040 | bytes 50331648 | tf_op jit(solution)/shard_map/back/pallas_call | solution.py:564
  346.9 5.8 dynamic-slice_add_fusion.1
  352.7 2.8 collective-permute-start.1
  355.5 3.7 dynamic-slice_add_fusion
  359.3 40.2 %collective-permute-done.1 = f32[240,4096]{1,0:T(8,128)} collective-permute-done((f32[240,4096]{1,0:T(8,128)}, f32[240,4096]{1,0:T(8,128)}, u32[]{:S(2)}, u32[]{:S(2)}) %collective-permute-start.1) | collective-permute-done | bytes 3932192 | tf_op jit(solution)/shard_map/ppermute | solution.py:698
  399.5 1.8 dynamic-slice_add_fusion.3
  401.3 2.1 collective-permute-start.2
  403.4 2.0 collective-permute-start.16
  405.4 2.3 dynamic-slice_add_fusion.2
  407.8 18.3 %collective-permute-done.2 = f32[120,4096]{1,0:T(8,128)} collective-permute-done((f32[120,4096]{1,0:T(8,128)S(1)}, f32[120,4096]{1,0:T(8,128)}, u32[]{:S(2)}, u32[]{:S(2)}) %collective-permute-start.2) | collective-permute-done | bytes 1966112 | tf_op jit(solution)/shard_map/ppermute | solution.py:698
  426.1 1.8 add.101.refs_0_
  427.9 2.1 collective-permute-start.3
  430.0 2.0 collective-permute-start.18
  432.0 207.0 %collective-permute-done.17.recv_ref = f32[960,256]{1,0:T(8,128)} collective-permute-done((f32[960,256]{1,0:T(8,128)S(1)}, f32[960,256]{1,0:T(8,128)}, u32[]{:S(2)}, u32[]{:S(2)}) %collective-permute-start.17) | collective-permute-done | bytes 983072 | tf_op jit(solution)/shard_map/ppermute | solution.py:682
  639.0 1.5 collective-permute-start.4
  640.5 17.7 %collective-permute-done.18.recv_ref = f32[960,256]{1,0:T(8,128)} collective-permute-done((f32[960,256]{1,0:T(8,128)S(1)}, f32[960,256]{1,0:T(8,128)}, u32[]{:S(2)}, u32[]{:S(2)}) %collective-permute-start.18) | collective-permute-done | bytes 983072 | tf_op jit(solution)/shard_map/ppermute | solution.py:682
  658.4 0.3 collective-permute-start.5
  658.8 4.9 collective-permute-done.4.refs_2_
  663.7 21.0 %collective-permute-done.5.refs_3_ = f32[120,4096]{1,0:T(8,128)S(1)} collective-permute-done((f32[120,4096]{1,0:T(8,128)S(1)}, f32[120,4096]{1,0:T(8,128)S(1)}, u32[]{:S(2)}, u32[]{:S(2)}) %collective-permute-start.5) | collective-permute-done | bytes 1966112 | tf_op jit(solution)/shard_map/ppermute | solution.py:706
  684.7 0.5 collective-permute-start.9
  685.3 3.4 collective-permute-done.8.refs_6_
  688.8 2.7 collective-permute-done.9.refs_7_
  691.5 1.3 copy-done.8
  692.9 0.6 reduce_sum.29
  693.5 0.6 reduce_sum.28
  694.6 0.6 stack.35.off_ref
  695.2 13.3 %psum.7 = f32[]{:T(128)} all-reduce(f32[]{:T(128)S(6)} %mul_shard_map.3), channel_id=1, replica_groups=mesh['dp'=2,'tp'=8] {'tp'}, use_global_device_ids=true, to_apply=%region_2.3 | all-reduce | flops 1 | bytes 8 | tf_op jit(solution)/shard_map/psum | solution.py:712
  709.8 17.7 %finish.1 = (bf16[960,4096]{1,0:T(8,128)(2,1)}, f32[960,128]{1,0:T(8,128)}) custom-call(s32[8]{0:T(128)} %stack.35.off_ref, bf16[960,4096]{1,0:T(8,128)(2,1)} %bitcast.30, f32[960,128]{1,0:T(8,128)} %get-tuple-element.42.gain_ref, f32[120,4096]{1,0:T(8,128)} %copy-done.1, f32[120,4096]{1,0:T(8,128)} %copy-done.2, f32[120,4096]{1,0:T(8,128)} %copy-done.3, ...), custom_call_target="tpu_custom_call" | custom-call | flops 39321600 | bytes 31457280 | tf_op jit(solution)/shard_map/finish/pallas_call | solution.py:608
  727.5 1.2 reduce_sum.27
  728.8 143.9 %collective-permute-done.15.recv_ref = f32[960,1024]{1,0:T(8,128)} collective-permute-done((f32[960,1024]{1,0:T(8,128)}, f32[960,1024]{1,0:T(8,128)}, u32[]{:S(2)}, u32[]{:S(2)}) %collective-permute-start.15) | collective-permute-done | bytes 3932192 | tf_op jit(solution)/shard_map/ppermute | solution.py:682
  873.0 2.3 shard_map.89.refs_0_
  875.3 2.3 shard_map.90.refs_0_
  877.6 4.1 shard_map.91.refs_0_
  881.7 7.4 shard_map.92.refs_0_
  889.1 14.2 %shard_map.93.refs_0_ = f32[960,6144]{1,0:T(8,128)} custom-call(f32[960,2048]{1,0:T(8,128)} %get-tuple-element.75.own_ref, f32[960,2048]{1,0:T(8,128)} %collective-permute-done.14.recv_ref, f32[960,6144]{1,0:T(8,128)} %shard_map.92.refs_0_), custom_call_target="tpu_custom_call", output_to_operand_aliasing={{}: (2, {})} | custom-call | flops 1966080 | bytes 23592960 | tf_op jit(solution)/shard_map/pallas_call | solution.py:642
  903.3 10.8 %shard_map.94.refs_0_ = f32[960,6144]{1,0:T(8,128)} custom-call(f32[960,1536]{1,0:T(8,128)} %get-tuple-element.74.own_ref, f32[960,1536]{1,0:T(8,128)} %collective-permute-done.13.recv_ref, f32[960,6144]{1,0:T(8,128)} %shard_map.93.refs_0_), custom_call_target="tpu_custom_call", output_to_operand_aliasing={{}: (2, {})} | custom-call | flops 1474560 | bytes 17694720 | tf_op jit(solution)/shard_map/pallas_call | solution.py:642
  914.1 3.7 shard_map.95.refs_0_
  917.8 0.6 slice.6
  918.4 2.0 shard_map.96
  (49 shorter events, 1.0 us)
Async XLA Ops:
  314.3 32.6 %collective-permute-start = (f32[480,4096]{1,0:T(8,128)}, f32[480,4096]{1,0:T(8,128)}, u32[]{:S(2)}, u32[]{:S(2)}) collective-permute-start(f32[480,4096]{1,0:T(8,128)} %back.3), channel_id=1, source_target_pairs={{0,1},{1,0},{2,3},{3,2},{4,5},{5,4},{6,7},{7,6},{8,9},{9,8},{10,11... | collective-permute-start | bytes 23592968 | tf_op jit(solution)/shard_map/ppermute | solution.py:691
  352.7 46.8 %collective-permute-start.1 = (f32[240,4096]{1,0:T(8,128)}, f32[240,4096]{1,0:T(8,128)}, u32[]{:S(2)}, u32[]{:S(2)}) collective-permute-start(f32[240,4096]{1,0:T(8,128)} %dynamic-slice_add_fusion.1), channel_id=1, source_target_pairs={{0,2},{1,5},{2,0},{3,7},{4,6},{5,1},{6,4},{7,3},{8,10},{9,13},{10,... | collective-permute-start | bytes 11796488 | tf_op jit(solution)/shard_map/ppermute | solution.py:698
  359.3 40.2 %copy-start = (f32[240,4096]{1,0:T(8,128)}, f32[240,4096]{1,0:T(8,128)S(1)}, u32[]{:S(2)}) copy-start(f32[240,4096]{1,0:T(8,128)S(1)} %dynamic-slice_add_fusion) | copy-start | bytes 11796484
  401.3 24.8 %collective-permute-start.2 = (f32[120,4096]{1,0:T(8,128)S(1)}, f32[120,4096]{1,0:T(8,128)}, u32[]{:S(2)}, u32[]{:S(2)}) collective-permute-start(f32[120,4096]{1,0:T(8,128)S(1)} %dynamic-slice_add_fusion.3), channel_id=1, source_target_pairs={{0,4},{1,3},{2,6},{3,1},{4,0},{5,7},{6,2},{7,5},{8,12},{9,11},{10,... | collective-permute-start | bytes 5898248 | tf_op jit(solution)/shard_map/ppermute | solution.py:698
  403.4 485.7 %collective-permute-start.14 = (f32[960,2048]{1,0:T(8,128)}, f32[960,2048]{1,0:T(8,128)}, u32[]{:S(2)}, u32[]{:S(2)}) collective-permute-start(f32[960,2048]{1,0:T(8,128)} %get-tuple-element.75.own_ref), channel_id=1, source_target_pairs={{0,8},{8,0},{1,9},{9,1},{2,10},{10,2},{3,11},{11,3},{4,12},{12,4},... | collective-permute-start | bytes 23592968 | tf_op jit(solution)/shard_map/ppermute | solution.py:682
  403.4 254.8 %collective-permute-start.16 = (f32[960,512]{1,0:T(8,128)}, f32[960,512]{1,0:T(8,128)}, u32[]{:S(2)}, u32[]{:S(2)}) collective-permute-start(f32[960,512]{1,0:T(8,128)} %get-tuple-element.77.own_ref), channel_id=1, source_target_pairs={{0,8},{8,0},{1,9},{9,1},{2,10},{10,2},{3,11},{11,3},{4,12},{12,4},... | collective-permute-start | bytes 5898248 | tf_op jit(solution)/shard_map/ppermute | solution.py:682
  407.8 22.2 %copy-start.10 = (f32[960,256]{1,0:T(8,128)S(1)}, f32[960,256]{1,0:T(8,128)}, u32[]{:S(2)}) copy-start(f32[960,256]{1,0:T(8,128)} %get-tuple-element.78.own_ref) | copy-start | bytes 2949124
  407.8 22.2 %copy-start.9 = (f32[960,256]{1,0:T(8,128)S(1)}, f32[960,256]{1,0:T(8,128)}, u32[]{:S(2)}) copy-start(f32[960,256]{1,0:T(8,128)} %get-tuple-element.79.own_ref) | copy-start | bytes 2949124
  407.8 285.1 %copy-start.12 = (f32[32,128]{1,0:T(8,128)S(1)}, f32[32,128]{1,0:T(8,128)}, u32[]{:S(2)}) copy-start(f32[32,128]{1,0:T(8,128)} %get-tuple-element.70) | copy-start | bytes 49156
  407.8 285.7 %copy-start.13 = (f32[32,128]{1,0:T(8,128)S(1)}, f32[32,128]{1,0:T(8,128)}, u32[]{:S(2)}) copy-start(f32[32,128]{1,0:T(8,128)} %get-tuple-element.69) | copy-start | bytes 49156
  427.9 281.9 %copy-start.1 = (f32[120,4096]{1,0:T(8,128)}, f32[120,4096]{1,0:T(8,128)S(1)}, u32[]{:S(2)}) copy-start(f32[120,4096]{1,0:T(8,128)S(1)} %add.101.refs_0_) | copy-start | bytes 5898244
  427.9 230.5 %collective-permute-start.3 = (f32[120,4096]{1,0:T(8,128)S(1)}, f32[120,4096]{1,0:T(8,128)S(1)}, u32[]{:S(2)}, u32[]{:S(2)}) collective-permute-start(f32[120,4096]{1,0:T(8,128)S(1)} %add.101.refs_0_), channel_id=1, source_target_pairs={{0,4},{1,3},{2,6},{3,1},{4,0},{5,7},{6,2},{7,5},{8,12},{9,11},{10,... | collective-permute-start | bytes 5898248 | tf_op jit(solution)/shard_map/ppermute | solution.py:706
  430.0 209.0 %collective-permute-start.17 = (f32[960,256]{1,0:T(8,128)S(1)}, f32[960,256]{1,0:T(8,128)}, u32[]{:S(2)}, u32[]{:S(2)}) collective-permute-start(f32[960,256]{1,0:T(8,128)S(1)} %copy-done.10), channel_id=1, source_target_pairs={{0,8},{8,0},{1,9},{9,1},{2,10},{10,2},{3,11},{11,3},{4,12},{12,4},... | collective-permute-start | bytes 2949128 | tf_op jit(solution)/shard_map/ppermute | solution.py:682
  430.0 228.2 %collective-permute-start.18 = (f32[960,256]{1,0:T(8,128)S(1)}, f32[960,256]{1,0:T(8,128)}, u32[]{:S(2)}, u32[]{:S(2)}) collective-permute-start(f32[960,256]{1,0:T(8,128)S(1)} %copy-done.9), channel_id=1, source_target_pairs={{0,8},{8,0},{1,9},{9,1},{2,10},{10,2},{3,11},{11,3},{4,12},{12,4},... | collective-permute-start | bytes 2949128 | tf_op jit(solution)/shard_map/ppermute | solution.py:682
  639.0 24.6 %collective-permute-start.4 = (f32[120,4096]{1,0:T(8,128)S(1)}, f32[120,4096]{1,0:T(8,128)S(1)}, u32[]{:S(2)}, u32[]{:S(2)}) collective-permute-start(f32[120,4096]{1,0:T(8,128)S(1)} %add.101.refs_0_), channel_id=1, source_target_pairs={{0,2},{1,5},{2,0},{3,7},{4,6},{5,1},{6,4},{7,3},{8,10},{9,13},{10,... | collective-permute-start | bytes 5898248 | tf_op jit(solution)/shard_map/ppermute | solution.py:706
  658.1 5.5 collective-permute-start.6
  658.1 245.2 %collective-permute-start.13 = (f32[960,1536]{1,0:T(8,128)}, f32[960,1536]{1,0:T(8,128)}, u32[]{:S(2)}, u32[]{:S(2)}) collective-permute-start(f32[960,1536]{1,0:T(8,128)} %get-tuple-element.74.own_ref), channel_id=1, source_target_pairs={{0,8},{8,0},{1,9},{9,1},{2,10},{10,2},{3,11},{11,3},{4,12},{12,4},... | collective-permute-start | bytes 17694728 | tf_op jit(solution)/shard_map/ppermute | solution.py:682
  658.4 5.2 copy-start.2
  658.4 26.3 %collective-permute-start.5 = (f32[120,4096]{1,0:T(8,128)S(1)}, f32[120,4096]{1,0:T(8,128)S(1)}, u32[]{:S(2)}, u32[]{:S(2)}) collective-permute-start(f32[120,4096]{1,0:T(8,128)S(1)} %collective-permute-done.3.refs_1_), channel_id=1, source_target_pairs={{0,2},{1,5},{2,0},{3,7},{4,6},{5,1},{6,4},{7,3},{8,10},{9,13},{10,... | collective-permute-start | bytes 5898248 | tf_op jit(solution)/shard_map/ppermute | solution.py:706
  663.6 21.1 %copy-start.3 = (f32[120,4096]{1,0:T(8,128)}, f32[120,4096]{1,0:T(8,128)S(1)}, u32[]{:S(2)}) copy-start(f32[120,4096]{1,0:T(8,128)S(1)} %collective-permute-done.4.refs_2_) | copy-start | bytes 5898244
  663.6 21.1 %collective-permute-start.7 = (f32[120,4096]{1,0:T(8,128)S(1)}, f32[120,4096]{1,0:T(8,128)S(1)}, u32[]{:S(2)}, u32[]{:S(2)}) collective-permute-start(f32[120,4096]{1,0:T(8,128)S(1)} %collective-permute-done.3.refs_1_), channel_id=1, source_target_pairs={{0,1},{1,0},{2,3},{3,2},{4,5},{5,4},{6,7},{7,6},{8,9},{9,8},{10,11... | collective-permute-start | bytes 5898248 | tf_op jit(solution)/shard_map/ppermute | solution.py:706
  663.7 25.0 %copy-start.4 = (f32[120,4096]{1,0:T(8,128)}, f32[120,4096]{1,0:T(8,128)S(1)}, u32[]{:S(2)}) copy-start(f32[120,4096]{1,0:T(8,128)S(1)} %collective-permute-done.6.refs_4_) | copy-start | bytes 5898244
  663.7 209.0 %collective-permute-start.15 = (f32[960,1024]{1,0:T(8,128)}, f32[960,1024]{1,0:T(8,128)}, u32[]{:S(2)}, u32[]{:S(2)}) collective-permute-start(f32[960,1024]{1,0:T(8,128)} %get-tuple-element.76.own_ref), channel_id=1, source_target_pairs={{0,8},{8,0},{1,9},{9,1},{2,10},{10,2},{3,11},{11,3},{4,12},{12,4},... | collective-permute-start | bytes 11796488 | tf_op jit(solution)/shard_map/ppermute | solution.py:682
  684.7 4.0 copy-start.5
  684.7 4.0 collective-permute-start.8
  684.7 6.8 copy-start.6
  684.7 6.8 collective-permute-start.9
  688.7 2.8 copy-start.7
  688.7 225.4 %collective-permute-start.12 = (f32[960,384]{1,0:T(8,128)}, f32[960,384]{1,0:T(8,128)}, u32[]{:S(2)}, u32[]{:S(2)}) collective-permute-start(f32[960,384]{1,0:T(8,128)} %get-tuple-element.73.own_ref), channel_id=1, source_target_pairs={{0,8},{8,0},{1,9},{9,1},{2,10},{10,2},{3,11},{11,3},{4,12},{12,4},... | collective-permute-start | bytes 4423688 | tf_op jit(solution)/shard_map/ppermute | solution.py:682
  691.5 1.3 copy-start.8
  692.8 225.7 %collective-permute-start.11 = (f32[960,128]{1,0:T(8,128)}, f32[960,128]{1,0:T(8,128)}, u32[]{:S(2)}, u32[]{:S(2)}) collective-permute-start(f32[960,128]{1,0:T(8,128)} %get-tuple-element.72.own_ref), channel_id=1, source_target_pairs={{0,8},{8,0},{1,9},{9,1},{2,10},{10,2},{3,11},{11,3},{4,12},{12,4},... | collective-permute-start | bytes 1474568 | tf_op jit(solution)/shard_map/ppermute | solution.py:682
  872.7 45.1 %collective-permute-start.10 = (f32[1024]{0:T(1024)S(1)}, f32[1024]{0:T(1024)S(1)}, u32[]{:S(2)}, u32[]{:S(2)}) collective-permute-start(f32[1024]{0:T(1024)S(1)} %concatenate.3), channel_id=1, source_target_pairs={{0,8},{8,0},{1,9},{9,1},{2,10},{10,2},{3,11},{11,3},{4,12},{12,4},... | collective-permute-start | bytes 12296 | tf_op jit(solution)/shard_map/ppermute | solution.py:715
  917.8 0.6 copy-start.11
